TPU v7x, 32 devices: a whole 2x2x4 slice. The times are simulated.
32 devices in a mesh: seq: 8 (over z, core), tp: 4 (over y, x).
Axes of the slice: x: 2, y: 2, z: 4, core: 2. Of those that a mesh axis runs over, the one named last changes fastest.
Arguments:
- hidden: bfloat16 [4096, 2048], P(('seq', 'tp')), may hold values from -5 to 5
- w_qkv: bfloat16 [2048, 3, 2048], P(None, None, 'tp'), may hold values from -0.125 to 0.125
- w_gate: bfloat16 [2048, 2048], P(None, 'tp'), may hold values from -0.125 to 0.125
- w_decay_beta: bfloat16 [2048, 2, 16], P(None, None, 'tp'), may hold values from -0.7 to 0.7
- conv_weight: bfloat16 [4, 3, 2048], P(None, None, 'tp'), may hold values from -2 to 2
- decay_rate: float32 [16], P('tp'), may hold values from 2e-05 to 0.05
- dt_bias: float32 [16], P('tp'), may hold values from -1 to 1
- norm_gain: float32 [128], replicated, may hold values from 0.1 to 1.9
Outputs:
- core: bfloat16 [4096, 2048], P('seq', 'tp')
All inputs are finite; a program needn't handle non-finite values.
Results may differ from a plain program's by a relative error of at most 0.01.
Values may be sent and summed in bfloat16 or wider, within the bound.
No kernel may reach another device: no remote copies, remote signals or barrier semaphores. Data moves between devices by JAX's collectives and lax.ppermute only.
A program may use at most 64 MiB of HBM per device.

v0:
```python
import functools
import math

import jax
import jax.numpy as jnp
from jax import lax
from jax.experimental import pallas as pl
from jax.experimental.pallas import tpu as pltpu
from jax.sharding import PartitionSpec as P

CHUNK = 128
LANES = 128
RIM = 8
EPS = 1e-6

f32 = jnp.float32
bf16 = jnp.bfloat16


def dot(left, right, contract=(1, 0), precision=None):
    dims = (((contract[0],), (contract[1],)), ((), ()))
    return lax.dot_general(left, right, dims, precision=precision, preferred_element_type=f32)


def whole(memory=pltpu.VMEM):
    return pl.BlockSpec(memory_space=memory)


def gather_blocks(block, axis):
    count = lax.axis_size(axis)
    bits = count.bit_length() - 1
    rows = block.shape[0]
    half = rows // 2

    def swap(value, bit):
        step = 1 << bit
        return lax.ppermute(value, axis, [(i, i ^ step) for i in range(count)])

    parts = [{0: block[:half]}, {0: block[half:]}]
    found = {0: block}
    for bit in range(bits):
        found[1 << bit] = swap(block, bit)
        parts[0][1 << bit] = found[1 << bit][:half]
        parts[1][1 << bit] = found[1 << bit][half:]
    for order, part in ((range(bits), parts[0]), (range(bits - 1, -1, -1), parts[1])):
        for bit in order:
            for mask in list(part):
                if mask | (1 << bit) not in part and not mask & (1 << bit):
                    part[mask | (1 << bit)] = swap(part[mask], bit)
    return [
        found[m] if m in found else jnp.concatenate([parts[0][m], parts[1][m]])
        for m in range(count)
    ]


def silu(x):
    return x / (1.0 + jnp.exp(-x))


def delta_kernel(
    heads, blocks, me_ref, p_ref, rim_ref, taps_ref, sc_ref, vec_ref,
    x_ref, qp_ref, o_ref, xp, act, sc, cols, masks,
):
    seq_rows, width = p_ref.shape
    columns = width // 3
    rows = seq_rows // blocks
    chunks = seq_rows // CHUNK
    taps = taps_ref.shape[0]
    me = me_ref[0]

    xp[:RIM] = rim_ref[...].astype(f32)
    for m in range(blocks):
        at = lax.bitwise_xor(me, m) * rows
        xp[pl.ds(pl.multiple_of(RIM + at, 8), rows)] = p_ref[m * rows:(m + 1) * rows].astype(f32)
        sc[pl.ds(pl.multiple_of(at, 8), rows)] = sc_ref[m * rows:(m + 1) * rows]

    ri = lax.broadcasted_iota(jnp.int32, (CHUNK, CHUNK), 0)
    ci = lax.broadcasted_iota(jnp.int32, (CHUNK, CHUNK), 1)
    strict = ri > ci
    upto = ri >= ci
    lower = upto.astype(f32)
    levels = CHUNK.bit_length() - 1
    for level in range(levels):
        hit = ((ri >> (level + 1)) == (ci >> (level + 1))) & ((ri >> level) > (ci >> level))
        masks[level] = hit.astype(f32).astype(bf16)

    root = 1.0 / math.sqrt(columns // heads)
    for chunk in range(chunks):
        base = chunk * CHUNK
        raw = sc[base:base + CHUNK]
        shifted = raw + vec_ref[1:2]
        soft = jnp.maximum(shifted, 0.0) + jnp.log1p(jnp.exp(-jnp.abs(shifted)))
        decay = dot(lower, vec_ref[0:1] * soft, precision=lax.Precision.HIGHEST)
        beta = 1.0 / (1.0 + jnp.exp(-raw))
        comb = jnp.where(ci < heads, decay, 0.0)
        for head in range(heads):
            norms = []
            for branch in range(3):
                lane = branch * columns + head * LANES
                total = None
                for i in range(taps):
                    start = RIM - taps + 1 + base + i
                    term = xp[start:start + CHUNK, lane:lane + LANES] * taps_ref[i:i + 1, lane:lane + LANES]
                    total = term if total is None else total + term
                value = silu(total).astype(bf16)
                act[branch, head, base:base + CHUNK] = value
                if branch < 2:
                    wide = value.astype(f32)
                    norms.append(lax.rsqrt(jnp.sum(wide * wide, axis=-1, keepdims=True) + EPS))
            scaled = beta[:, heads + head:heads + head + 1] * norms[1]
            comb = jnp.where(ci == heads + head, scaled, comb)
            comb = jnp.where(ci == 2 * heads + head, norms[0] * root, comb)
            comb = jnp.where(ci == 3 * heads + head, norms[1], comb)
        cols[chunk] = comb

    pairs = [(head, chunk) for head in range(heads) for chunk in range(chunks)]
    for head in range(heads):
        todo = list(range(chunks))
        turned = {}
        state = {}
        for chunk in todo:
            at = slice(chunk * CHUNK, (chunk + 1) * CHUNK)
            col = cols[chunk]
            row = col.T
            k = act[1, head, at]
            q = act[0, head, at]
            gap = col[:, head:head + 1] - row[head:head + 1]
            weight = jnp.exp(jnp.where(upto, gap, 0.0)) * row[heads + head:heads + head + 1]
            gram = dot(k, k, (1, 1))
            score = dot(q, k, (1, 1))
            key_norm = col[:, 3 * heads + head:3 * heads + head + 1]
            mix = (weight * gram * key_norm).astype(bf16)
            attend = jnp.where(upto, weight * score * col[:, 2 * heads + head:2 * heads + head + 1], 0.0)
            x = jnp.where(ri == ci, 1.0, 0.0) - (mix * masks[0]).astype(f32)
            state[chunk] = [mix, x, attend.astype(bf16), col, row]
        for level in range(1, levels):
            low = {c: state[c][1].astype(bf16) for c in todo}
            mid = {c: dot(state[c][0] * masks[level], low[c]).astype(bf16) for c in todo}
            for c in todo:
                state[c][1] = state[c][1] - dot(low[c], mid[c])
        p_run, r_run = None, None
        for chunk in todo:
            mix, x, attend, col, row = state[chunk]
            at = slice(chunk * CHUNK, (chunk + 1) * CHUNK)
            k, q, v = act[1, head, at], act[0, head, at], act[2, head, at]
            decay = col[:, head:head + 1]
            last = col[CHUNK - 1:CHUNK, head:head + 1]
            key_norm_row = row[3 * heads + head:3 * heads + head + 1]
            grown = jnp.exp(row[head:head + 1]) * key_norm_row
            new = dot(x.astype(bf16), v)
            back = dot((x * grown).astype(bf16), k)
            tail = col[:, heads + head:heads + head + 1] * jnp.exp(last - decay)
            both = jnp.concatenate([back, new], axis=1)
            change = dot(k, (both * tail).astype(bf16), (0, 0))
            inner = dot(attend, both.astype(bf16))
            eff = (jnp.exp(decay) * col[:, 2 * heads + head:2 * heads + head + 1]) * q.astype(f32) - inner[:, :LANES]
            if chunk == 0:
                qp_ref[head, at] = eff.astype(bf16)
                o_ref[head, at] = inner[:, LANES:]
                p_run = jnp.where(ri == ci, jnp.exp(last), 0.0) - change[:, :LANES]
                r_run = change[:, LANES:]
            else:
                run = jnp.concatenate([p_run, r_run], axis=1)
                low_run = run.astype(bf16)
                ahead = dot(eff.astype(bf16), low_run)
                qp_ref[head, at] = ahead[:, :LANES].astype(bf16)
                o_ref[head, at] = inner[:, LANES:] + ahead[:, LANES:]
                run = jnp.exp(last) * run - dot(change[:, :LANES].astype(bf16), low_run)
                p_run = run[:, :LANES]
                r_run = run[:, LANES:] + change[:, LANES:]
        x_ref[head] = jnp.concatenate([p_run, r_run], axis=1).astype(bf16)


def join_kernel(mine_ref, earlier_ref, out_ref):
    for head in range(mine_ref.shape[0]):
        mine = mine_ref[head]
        both = dot(mine[:, :LANES], earlier_ref[head])
        out_ref[head, :, :LANES] = both[:, :LANES].astype(bf16)
        out_ref[head, :, LANES:] = (both[:, LANES:] + mine[:, LANES:].astype(f32)).astype(bf16)


def final_kernel(blocks, me_ref, qp_ref, o_ref, near_ref, far_ref, gate_ref, gain_ref, out_ref):
    heads, seq_rows, dim = qp_ref.shape
    rows = seq_rows // blocks
    me = me_ref[0]
    for head in range(heads):
        near = near_ref[head]
        start = near[:, dim:].astype(f32) + dot(near[:, :dim], far_ref[head])
        start = start.astype(bf16)
        lanes = slice(head * dim, (head + 1) * dim)
        for m in range(blocks):
            at = pl.multiple_of(lax.bitwise_xor(me, m) * rows, 8)
            y = o_ref[head, pl.ds(at, rows)] + dot(qp_ref[head, pl.ds(at, rows)], start)
            scale = lax.rsqrt(jnp.mean(y * y, axis=-1, keepdims=True) + EPS)
            gate = gate_ref[m * rows:(m + 1) * rows, lanes]
            y = y * scale * gain_ref[...] * silu(gate)
            out_ref[pl.ds(at, rows), lanes] = y.astype(bf16)


def shifted(value, axis, distance):
    count = lax.axis_size(axis)
    return lax.ppermute(value, axis, [(i, i + distance) for i in range(count - distance)])


def per_device(hidden, w_qkv, w_gate, w_decay_beta, conv_weight, decay_rate, dt_bias, norm_gain):
    model_width = hidden.shape[1]
    heads = decay_rate.shape[0]
    dim = norm_gain.shape[0]
    columns = heads * dim
    blocks = lax.axis_size("tp")
    seq_count = lax.axis_size("seq")
    me = lax.axis_index("tp")
    index = jnp.full((1,), me, jnp.int32)
    qkv_matrix = w_qkv.reshape(model_width, 3 * columns)
    small = jnp.pad(
        w_decay_beta.reshape(model_width, 2 * heads), ((0, 0), (0, LANES - 2 * heads))
    )
    tokens = jnp.concatenate(gather_blocks(hidden, "tp"), axis=0)
    rows = hidden.shape[0]
    seq_rows = tokens.shape[0]
    projected = jnp.dot(tokens, qkv_matrix, preferred_element_type=f32).astype(bf16)
    last = lax.bitwise_xor(me, blocks - 1)
    rim = lax.dynamic_slice(projected, (last * rows + rows - RIM, 0), (RIM, 3 * columns))
    rim = shifted(rim, "seq", 1)
    scalars = jnp.dot(tokens, small, preferred_element_type=f32)
    gate = jnp.dot(tokens, w_gate, preferred_element_type=f32)
    taps = conv_weight.reshape(conv_weight.shape[0], 3 * columns).astype(f32)
    vectors = jnp.pad(jnp.stack([-decay_rate, dt_bias]), ((0, 6), (0, LANES - heads)))
    chunks = seq_rows // CHUNK
    cost = functools.partial(pl.CostEstimate, transcendentals=0, bytes_accessed=4 << 20)
    own, reach, base = pl.pallas_call(
        functools.partial(delta_kernel, heads, blocks),
        out_shape=(
            jax.ShapeDtypeStruct((heads, dim, 2 * dim), bf16),
            jax.ShapeDtypeStruct((heads, seq_rows, dim), bf16),
            jax.ShapeDtypeStruct((heads, seq_rows, dim), f32),
        ),
        in_specs=[whole(pltpu.SMEM)] + [whole()] * 5,
        out_specs=(whole(),) * 3,
        scratch_shapes=[
            pltpu.VMEM((seq_rows + RIM, 3 * columns), f32),
            pltpu.VMEM((3, heads, seq_rows, dim), bf16),
            pltpu.VMEM((seq_rows, LANES), f32),
            pltpu.VMEM((chunks, CHUNK, LANES), f32),
            pltpu.VMEM((CHUNK.bit_length() - 1, CHUNK, CHUNK), bf16),
        ],
        cost_estimate=cost(flops=2000000000),
        name="delta",
    )(index, projected, rim, taps, scalars, vectors)

    def join(mine, earlier):
        return pl.pallas_call(
            join_kernel,
            out_shape=jax.ShapeDtypeStruct(mine.shape, bf16),
            in_specs=[whole()] * 2,
            out_specs=whole(),
            cost_estimate=cost(flops=50000000),
            name="join",
        )(mine, earlier)

    run = own
    distance = 1
    while distance * 2 < seq_count:
        run = join(run, shifted(run, "seq", distance))
        distance *= 2
    near = shifted(run, "seq", 1)
    far = shifted(run[:, :, dim:], "seq", distance + 1)
    return pl.pallas_call(
        functools.partial(final_kernel, blocks),
        out_shape=jax.ShapeDtypeStruct((seq_rows, columns), bf16),
        in_specs=[whole(pltpu.SMEM)] + [whole()] * 6,
        out_specs=whole(),
        cost_estimate=cost(flops=200000000),
        name="final",
    )(index, reach, base, near, far, gate, norm_gain.reshape(1, dim))


def solution(mesh):
    return jax.shard_map(
        per_device,
        mesh=mesh,
        in_specs=(
            P(("seq", "tp"), None),
            P(None, None, "tp"),
            P(None, "tp"),
            P(None, None, "tp"),
            P(None, None, "tp"),
            P("tp"),
            P("tp"),
            P(),
        ),
        out_specs=P("seq", "tp"),
        check_vma=False,
    )
```

profile of v0, /device:TPU:0, one launch (start us, length us, event | category | flops | bytes accessed | tf_op | source)
XLA Modules:
  0.0 94.6 jit_solution(98630310390611142)
XLA Ops:
  0.0 3.0 %collective-permute-start = (bf16[128,2048]{1,0:T(8,128)(2,1)}, bf16[128,2048]{1,0:T(8,128)(2,1)S(1)}, u32[]{:S(2)}, u32[]{:S(2)}) collective-permute-start(bf16[128,2048]{1,0:T(8,128)(2,1)} %param.8), channel_id=1, source_target_pairs={{0,1},{1,0},{2,3},{3,2},{4,5},{5,4},{6,7},{7,6},{8,9},{9,8},{10,11... | collective-permute-start | bytes 1572872 | tf_op jit(solution)/shard_map/ppermute | solution.py:37
  3.0 1.5 %collective-permute-start.1 = (bf16[128,2048]{1,0:T(8,128)(2,1)}, bf16[128,2048]{1,0:T(8,128)(2,1)S(1)}, u32[]{:S(2)}, u32[]{:S(2)}) collective-permute-start(bf16[128,2048]{1,0:T(8,128)(2,1)} %param.8), channel_id=1, source_target_pairs={{0,2},{1,3},{2,0},{3,1},{4,6},{5,7},{6,4},{7,5},{8,10},{9,11},{10,... | collective-permute-start | bytes 1572872 | tf_op jit(solution)/shard_map/ppermute | solution.py:37
  4.5 9.0 %copy.10 = bf16[2048,3,512]{0,2,1:T(8,128)(2,1)} copy(bf16[2048,3,512]{2,0,1:T(8,128)(2,1)} %param.9) | data formatting | bytes 12582912 | tf_op args[1]
  14.7 1.1 %constant_dynamic-update-slice_fusion.4 = bf16[512,2048]{1,0:T(8,128)(2,1)S(1)} fusion(bf16[128,2048]{1,0:T(8,128)(2,1)} %param.8), kind=kLoop, calls=%fused_computation.7 | loop fusion | bytes 1048576
  15.8 0.7 collective-permute-done.1
  17.1 1.7 %collective-permute-start.3 = (bf16[64,2048]{1,0:T(8,128)(2,1)S(1)}, bf16[64,2048]{1,0:T(8,128)(2,1)S(1)}, u32[]{:S(2)}, u32[]{:S(2)}) collective-permute-start(bf16[64,2048]{1,0:T(8,128)(2,1)S(1)} %slice.13), channel_id=1, source_target_pairs={{0,2},{1,3},{2,0},{3,1},{4,6},{5,7},{6,4},{7,5},{8,10},{9,11},{10,... | collective-permute-start | bytes 786440 | tf_op jit(solution)/shard_map/ppermute | solution.py:37
  18.9 4.7 %collective-permute-done.2 = bf16[64,2048]{1,0:T(8,128)(2,1)S(1)} collective-permute-done((bf16[64,2048]{1,0:T(8,128)(2,1)S(1)}, bf16[64,2048]{1,0:T(8,128)(2,1)S(1)}, u32[]{:S(2)}, u32[]{:S(2)}) %collective-permute-start.2) | collective-permute-done | bytes 262176 | tf_op jit(solution)/shard_map/ppermute | solution.py:37
  24.1 7.1 %convolution_convert_fusion.p_ref = bf16[512,1536]{1,0:T(8,128)(2,1)S(1)} fusion(bf16[512,2048]{1,0:T(8,128)(2,1)S(1)} %constant_dynamic-update-slice_fusion, bf16[2048,1536]{0,1:T(8,128)(2,1)} %bitcast.15), kind=kOutput, calls=%fused_computation | convolution fusion | flops 3222011904 | bytes 9961472 | tf_op jit(solution)/shard_map/dot_general | solution.py:221
  31.2 1.5 %collective-permute-start.4 = (bf16[8,1536]{1,0:T(8,128)(2,1)S(1)}, bf16[8,1536]{1,0:T(8,128)(2,1)S(1)}, u32[]{:S(2)}, u32[]{:S(2)}) collective-permute-start(bf16[8,1536]{1,0:T(8,128)(2,1)S(1)} %constant_dynamic-slice_fusion), channel_id=1, source_target_pairs={{0,4},{4,8},{8,12},{12,16},{16,20},{20,24},{24,28},{1,5},{5,9},{9,... | collective-permute-start | bytes 73736 | tf_op jit(solution)/shard_map/ppermute | solution.py:202
  32.7 1.4 %fusion.sc_ref = f32[512,128]{1,0:T(8,128)} fusion(bf16[512,2048]{1,0:T(8,128)(2,1)S(1)} %constant_dynamic-update-slice_fusion, bf16[2048,8]{0,1:T(8,128)(2,1)S(1)} %reshape.13), kind=kOutput, calls=%fused_computation.1 | convolution fusion | flops 268435456 | bytes 2392064 | tf_op jit(solution)/shard_map/dot_general | solution.py:225
  34.7 19.3 %delta.1 = (bf16[4,128,256]{2,1,0:T(8,128)(2,1)}, bf16[4,512,128]{2,1,0:T(8,128)(2,1)}, f32[4,512,128]{2,1,0:T(8,128)}) custom-call(s32[1]{0:T(128)} %bitcast.me_ref, bf16[512,1536]{1,0:T(8,128)(2,1)} %copy-done.9, bf16[8,1536]{1,0:T(8,128)(2,1)} %copy-done.10, f32[4,1536]{1,0:T(4,128)} %convert.1.taps_ref, f32[512,128]{1,0:T(8,128)} %fusion.sc_ref, ...), custom_call_target="tpu_custom_call" | custom-call | flops 2000000000 | bytes 4194304 | tf_op jit(solution)/shard_map/delta/pallas_call | solution.py:231
  54.0 4.1 %collective-permute-start.5 = (bf16[4,128,256]{2,1,0:T(8,128)(2,1)}, bf16[4,128,256]{2,1,0:T(8,128)(2,1)S(1)}, u32[]{:S(2)}, u32[]{:S(2)}) collective-permute-start(bf16[4,128,256]{2,1,0:T(8,128)(2,1)} %get-tuple-element.10.mine_ref), channel_id=1, source_target_pairs={{0,4},{4,8},{8,12},{12,16},{16,20},{20,24},{24,28},{1,5},{5,9},{9,... | collective-permute-start | bytes 786440 | tf_op jit(solution)/shard_map/ppermute | solution.py:202
  58.1 1.3 %collective-permute-done.5.earlier_ref = bf16[4,128,256]{2,1,0:T(8,128)(2,1)S(1)} collective-permute-done((bf16[4,128,256]{2,1,0:T(8,128)(2,1)}, bf16[4,128,256]{2,1,0:T(8,128)(2,1)S(1)}, u32[]{:S(2)}, u32[]{:S(2)}) %collective-permute-start.5) | collective-permute-done | bytes 262176 | tf_op jit(solution)/shard_map/ppermute | solution.py:202
  59.4 0.7 copy-done.1
  60.1 1.9 %join.2.mine_ref = bf16[4,128,256]{2,1,0:T(8,128)(2,1)} custom-call(bf16[4,128,256]{2,1,0:T(8,128)(2,1)} %get-tuple-element.10.mine_ref, bf16[4,128,256]{2,1,0:T(8,128)(2,1)} %copy-done.1), custom_call_target="tpu_custom_call" | custom-call | flops 50000000 | bytes 4194304 | tf_op jit(solution)/shard_map/join/pallas_call | solution.py:252
  62.0 8.1 %collective-permute-start.6 = (bf16[4,128,256]{2,1,0:T(8,128)(2,1)}, bf16[4,128,256]{2,1,0:T(8,128)(2,1)S(1)}, u32[]{:S(2)}, u32[]{:S(2)}) collective-permute-start(bf16[4,128,256]{2,1,0:T(8,128)(2,1)} %join.2.mine_ref), channel_id=1, source_target_pairs={{0,8},{4,12},{8,16},{12,20},{16,24},{20,28},{1,9},{5,13},{9,17},{1... | collective-permute-start | bytes 786440 | tf_op jit(solution)/shard_map/ppermute | solution.py:202
  70.1 5.3 %collective-permute-done.6.earlier_ref = bf16[4,128,256]{2,1,0:T(8,128)(2,1)S(1)} collective-permute-done((bf16[4,128,256]{2,1,0:T(8,128)(2,1)}, bf16[4,128,256]{2,1,0:T(8,128)(2,1)S(1)}, u32[]{:S(2)}, u32[]{:S(2)}) %collective-permute-start.6) | collective-permute-done | bytes 262176 | tf_op jit(solution)/shard_map/ppermute | solution.py:202
  75.4 0.7 copy-done.2
  76.1 1.9 %join.3 = bf16[4,128,256]{2,1,0:T(8,128)(2,1)} custom-call(bf16[4,128,256]{2,1,0:T(8,128)(2,1)} %join.2.mine_ref, bf16[4,128,256]{2,1,0:T(8,128)(2,1)} %copy-done.2), custom_call_target="tpu_custom_call" | custom-call | flops 50000000 | bytes 4194304 | tf_op jit(solution)/shard_map/join/pallas_call | solution.py:252
  78.1 1.3 %collective-permute-start.7 = (bf16[4,128,256]{2,1,0:T(8,128)(2,1)}, bf16[4,128,256]{2,1,0:T(8,128)(2,1)S(1)}, u32[]{:S(2)}, u32[]{:S(2)}) collective-permute-start(bf16[4,128,256]{2,1,0:T(8,128)(2,1)} %join.3), channel_id=1, source_target_pairs={{0,4},{4,8},{8,12},{12,16},{16,20},{20,24},{24,28},{1,5},{5,9},{9,... | collective-permute-start | bytes 786440 | tf_op jit(solution)/shard_map/ppermute | solution.py:202
  79.4 0.9 slice.14
  80.3 6.1 %collective-permute-start.8 = (bf16[4,128,128]{2,1,0:T(8,128)(2,1)S(1)}, bf16[4,128,128]{2,1,0:T(8,128)(2,1)S(1)}, u32[]{:S(2)}, u32[]{:S(2)}) collective-permute-start(bf16[4,128,128]{2,1,0:T(8,128)(2,1)S(1)} %slice.14), channel_id=1, source_target_pairs={{0,20},{4,24},{8,28},{1,21},{5,25},{9,29},{2,22},{6,26},{10,30},{3... | collective-permute-start | bytes 393224 | tf_op jit(solution)/shard_map/ppermute | solution.py:202
  86.4 3.8 %fusion.3.gate_ref = f32[512,512]{1,0:T(8,128)} fusion(bf16[512,2048]{1,0:T(8,128)(2,1)} %copy-done.4, bf16[2048,512]{1,0:T(8,128)(2,1)S(1)} %copy-done), kind=kOutput, calls=%fused_computation.14 | convolution fusion | flops 1073741824 | bytes 5242880 | tf_op jit(solution)/shard_map/dot_general | solution.py:226
  91.0 3.6 %final.1 = bf16[512,512]{1,0:T(8,128)(2,1)} custom-call(s32[1]{0:T(128)} %bitcast.me_ref, bf16[4,512,128]{2,1,0:T(8,128)(2,1)} %get-tuple-element.8.qp_ref, f32[4,512,128]{2,1,0:T(8,128)} %get-tuple-element.9.o_ref, bf16[4,128,256]{2,1,0:T(8,128)(2,1)} %copy-done.3, bf16[4,128,128]{2,1,0:T(8,128)(2,1)} %copy-done.5, f32[512,512]{1,0:T(8,128)} %fusion.3.gate_ref, ...), custom_call_target="tpu_custom_call" | custom-call | flops 200000000 | bytes 4194304 | tf_op jit(solution)/shard_map/final/pallas_call | solution.py:268
  (39 shorter events, 3.7 us)
Async XLA Ops:
  0.0 86.4 %copy-start = (bf16[2048,512]{1,0:T(8,128)(2,1)S(1)}, bf16[2048,512]{1,0:T(8,128)(2,1)}, u32[]{:S(2)}) copy-start(bf16[2048,512]{1,0:T(8,128)(2,1)} %param.10) | copy-start | bytes 6291460
  0.0 17.0 %collective-permute-start = (bf16[128,2048]{1,0:T(8,128)(2,1)}, bf16[128,2048]{1,0:T(8,128)(2,1)S(1)}, u32[]{:S(2)}, u32[]{:S(2)}) collective-permute-start(bf16[128,2048]{1,0:T(8,128)(2,1)} %param.8), channel_id=1, source_target_pairs={{0,1},{1,0},{2,3},{3,2},{4,5},{5,4},{6,7},{7,6},{8,9},{9,8},{10,11... | collective-permute-start | bytes 1572872 | tf_op jit(solution)/shard_map/ppermute | solution.py:37
  3.0 13.6 %collective-permute-start.1 = (bf16[128,2048]{1,0:T(8,128)(2,1)}, bf16[128,2048]{1,0:T(8,128)(2,1)S(1)}, u32[]{:S(2)}, u32[]{:S(2)}) collective-permute-start(bf16[128,2048]{1,0:T(8,128)(2,1)} %param.8), channel_id=1, source_target_pairs={{0,2},{1,3},{2,0},{3,1},{4,6},{5,7},{6,4},{7,5},{8,10},{9,11},{10,... | collective-permute-start | bytes 1572872 | tf_op jit(solution)/shard_map/ppermute | solution.py:37
  4.5 9.0 %copy-start.7 = (bf16[4,3,512]{2,0,1:T(4,128)(2,1)S(1)}, bf16[4,3,512]{2,0,1:T(4,128)(2,1)}, u32[]{:S(2)}) copy-start(bf16[4,3,512]{2,0,1:T(4,128)(2,1)} %param.12) | copy-start | bytes 36868
  4.5 9.6 %copy-start.6 = (bf16[2048,2,4]{0,2,1:T(4,128)(2,1)S(1)}, bf16[2048,2,4]{0,2,1:T(4,128)(2,1)}, u32[]{:S(2)}) copy-start(bf16[2048,2,4]{0,2,1:T(4,128)(2,1)} %param.11) | copy-start | bytes 98308
  4.5 9.6 %copy-start.11 = (f32[4]{0:T(128)S(1)}, f32[4]{0:T(128)}, u32[]{:S(2)}) copy-start(f32[4]{0:T(128)} %param.13) | copy-start | bytes 52
  4.5 9.6 %copy-start.8 = (f32[4]{0:T(128)S(1)}, f32[4]{0:T(128)}, u32[]{:S(2)}) copy-start(f32[4]{0:T(128)} %param.14) | copy-start | bytes 52
  16.6 7.0 %collective-permute-start.2 = (bf16[64,2048]{1,0:T(8,128)(2,1)S(1)}, bf16[64,2048]{1,0:T(8,128)(2,1)S(1)}, u32[]{:S(2)}, u32[]{:S(2)}) collective-permute-start(bf16[64,2048]{1,0:T(8,128)(2,1)S(1)} %slice.12), channel_id=1, source_target_pairs={{0,1},{1,0},{2,3},{3,2},{4,5},{5,4},{6,7},{7,6},{8,9},{9,8},{10,11... | collective-permute-start | bytes 786440 | tf_op jit(solution)/shard_map/ppermute | solution.py:37
  17.1 7.0 %collective-permute-start.3 = (bf16[64,2048]{1,0:T(8,128)(2,1)S(1)}, bf16[64,2048]{1,0:T(8,128)(2,1)S(1)}, u32[]{:S(2)}, u32[]{:S(2)}) collective-permute-start(bf16[64,2048]{1,0:T(8,128)(2,1)S(1)} %slice.13), channel_id=1, source_target_pairs={{0,2},{1,3},{2,0},{3,1},{4,6},{5,7},{6,4},{7,5},{8,10},{9,11},{10,... | collective-permute-start | bytes 786440 | tf_op jit(solution)/shard_map/ppermute | solution.py:37
  24.1 8.6 %copy-start.4 = (bf16[512,2048]{1,0:T(8,128)(2,1)}, bf16[512,2048]{1,0:T(8,128)(2,1)S(1)}, u32[]{:S(2)}) copy-start(bf16[512,2048]{1,0:T(8,128)(2,1)S(1)} %constant_dynamic-update-slice_fusion) | copy-start | bytes 6291460
  31.2 2.9 %copy-start.9 = (bf16[512,1536]{1,0:T(8,128)(2,1)}, bf16[512,1536]{1,0:T(8,128)(2,1)S(1)}, u32[]{:S(2)}) copy-start(bf16[512,1536]{1,0:T(8,128)(2,1)S(1)} %convolution_convert_fusion.p_ref) | copy-start | bytes 4718596
  31.2 2.9 %collective-permute-start.4 = (bf16[8,1536]{1,0:T(8,128)(2,1)S(1)}, bf16[8,1536]{1,0:T(8,128)(2,1)S(1)}, u32[]{:S(2)}, u32[]{:S(2)}) collective-permute-start(bf16[8,1536]{1,0:T(8,128)(2,1)S(1)} %constant_dynamic-slice_fusion), channel_id=1, source_target_pairs={{0,4},{4,8},{8,12},{12,16},{16,20},{20,24},{24,28},{1,5},{5,9},{9,... | collective-permute-start | bytes 73736 | tf_op jit(solution)/shard_map/ppermute | solution.py:202
  34.1 0.6 copy-start.10
  54.0 5.4 %collective-permute-start.5 = (bf16[4,128,256]{2,1,0:T(8,128)(2,1)}, bf16[4,128,256]{2,1,0:T(8,128)(2,1)S(1)}, u32[]{:S(2)}, u32[]{:S(2)}) collective-permute-start(bf16[4,128,256]{2,1,0:T(8,128)(2,1)} %get-tuple-element.10.mine_ref), channel_id=1, source_target_pairs={{0,4},{4,8},{8,12},{12,16},{16,20},{20,24},{24,28},{1,5},{5,9},{9,... | collective-permute-start | bytes 786440 | tf_op jit(solution)/shard_map/ppermute | solution.py:202
  59.4 0.7 copy-start.1
  62.0 13.4 %collective-permute-start.6 = (bf16[4,128,256]{2,1,0:T(8,128)(2,1)}, bf16[4,128,256]{2,1,0:T(8,128)(2,1)S(1)}, u32[]{:S(2)}, u32[]{:S(2)}) collective-permute-start(bf16[4,128,256]{2,1,0:T(8,128)(2,1)} %join.2.mine_ref), channel_id=1, source_target_pairs={{0,8},{4,12},{8,16},{12,20},{16,24},{20,28},{1,9},{5,13},{9,17},{1... | collective-permute-start | bytes 786440 | tf_op jit(solution)/shard_map/ppermute | solution.py:202
  75.4 0.7 copy-start.2
  78.1 12.1 %collective-permute-start.7 = (bf16[4,128,256]{2,1,0:T(8,128)(2,1)}, bf16[4,128,256]{2,1,0:T(8,128)(2,1)S(1)}, u32[]{:S(2)}, u32[]{:S(2)}) collective-permute-start(bf16[4,128,256]{2,1,0:T(8,128)(2,1)} %join.3), channel_id=1, source_target_pairs={{0,4},{4,8},{8,12},{12,16},{16,20},{20,24},{24,28},{1,5},{5,9},{9,... | collective-permute-start | bytes 786440 | tf_op jit(solution)/shard_map/ppermute | solution.py:202
  80.3 9.9 %collective-permute-start.8 = (bf16[4,128,128]{2,1,0:T(8,128)(2,1)S(1)}, bf16[4,128,128]{2,1,0:T(8,128)(2,1)S(1)}, u32[]{:S(2)}, u32[]{:S(2)}) collective-permute-start(bf16[4,128,128]{2,1,0:T(8,128)(2,1)S(1)} %slice.14), channel_id=1, source_target_pairs={{0,20},{4,24},{8,28},{1,21},{5,25},{9,29},{2,22},{6,26},{10,30},{3... | collective-permute-start | bytes 393224 | tf_op jit(solution)/shard_map/ppermute | solution.py:202
  90.2 0.6 copy-start.5
  90.2 0.8 copy-start.3
where the time goes:
time: 95.3 us; the launch traced here: 94.6 us
  starting transfers between devices  27.7 us (29%)
  Pallas kernels  26.8 us (28%)
  local copies, waits for them, and re-layouts  13.9 us (15%)
  waiting for transfers between devices  12.5 us (13%)
  matrix products  12.3 us (13%)
  other arithmetic  1.21 us (1%)
    ppermute x5, starting transfers between devices, shifted(): lax.ppermute(value, axis, [(i, i + distance) for i in range(count - dista...  21 us
    pallas_call x1, Pallas kernels, per_device(): pl.pallas_call(functools.partial(delta_kernel, heads, blocks), out_shape=...  19.3 us
    unnamed x29, local copies, waits for them, and re-layouts  12.9 us
    dot_general x1, matrix products, per_device(): jnp.dot(tokens, qkv_matrix, preferred_element_type=f32).astype(bf16)  7.09 us
    ppermute x4, starting transfers between devices, swap(): return lax.ppermute(value, axis, [(i, i ^ step) for i in range(count)])  6.67 us
    ppermute x5, waiting for transfers between devices, shifted(): lax.ppermute(value, axis, [(i, i + distance) for i in range(count - dista...  6.66 us
    ppermute x4, waiting for transfers between devices, swap(): return lax.ppermute(value, axis, [(i, i ^ step) for i in range(count)])  5.89 us
    pallas_call x2, Pallas kernels, join(): pl.pallas_call(join_kernel, out_shape=jax.ShapeDtypeStruct(mine.shape, bf...  3.89 us
  transfers between devices with their start and end apart: 9, of which 5 were waited for; matrix products, arithmetic and copies ran while one was open for 19% of the time, Pallas kernels for 0%

commit v1 on v0

--- a/solution.py
+++ b/solution.py
@@ -57,37 +57,53 @@
     return x / (1.0 + jnp.exp(-x))
 
 
+def block_diagonal(left, right):
+    hole = jnp.zeros_like(left)
+    return jnp.concatenate(
+        [jnp.concatenate([left, hole], axis=1), jnp.concatenate([hole, right], axis=1)], axis=0
+    )
+
+
+def beside(left, right):
+    return jnp.concatenate([left, right], axis=1)
+
+
 def delta_kernel(
     heads, blocks, me_ref, p_ref, rim_ref, taps_ref, sc_ref, vec_ref,
-    x_ref, qp_ref, o_ref, xp, act, sc, cols, masks,
+    x_ref, qp_ref, o_ref, xp, act, sc, cols, rows_of, masks, mixes, solves, attends,
 ):
     seq_rows, width = p_ref.shape
-    columns = width // 3
+    tiles = width // LANES
     rows = seq_rows // blocks
     chunks = seq_rows // CHUNK
-    taps = taps_ref.shape[0]
+    taps = taps_ref.shape[1]
     me = me_ref[0]
 
-    xp[:RIM] = rim_ref[...].astype(f32)
+    for tile in range(tiles):
+        lanes = slice(tile * LANES, (tile + 1) * LANES)
+        xp[tile, :RIM] = rim_ref[:, lanes].astype(f32)
+        for m in range(blocks):
+            at = pl.multiple_of(RIM + lax.bitwise_xor(me, m) * rows, 8)
+            xp[tile, pl.ds(at, rows)] = p_ref[m * rows:(m + 1) * rows, lanes].astype(f32)
     for m in range(blocks):
-        at = lax.bitwise_xor(me, m) * rows
-        xp[pl.ds(pl.multiple_of(RIM + at, 8), rows)] = p_ref[m * rows:(m + 1) * rows].astype(f32)
-        sc[pl.ds(pl.multiple_of(at, 8), rows)] = sc_ref[m * rows:(m + 1) * rows]
+        at = pl.multiple_of(lax.bitwise_xor(me, m) * rows, 8)
+        sc[pl.ds(at, rows)] = sc_ref[m * rows:(m + 1) * rows]
 
     ri = lax.broadcasted_iota(jnp.int32, (CHUNK, CHUNK), 0)
     ci = lax.broadcasted_iota(jnp.int32, (CHUNK, CHUNK), 1)
-    strict = ri > ci
     upto = ri >= ci
     lower = upto.astype(f32)
     levels = CHUNK.bit_length() - 1
     for level in range(levels):
         hit = ((ri >> (level + 1)) == (ci >> (level + 1))) & ((ri >> level) > (ci >> level))
-        masks[level] = hit.astype(f32).astype(bf16)
-
-    root = 1.0 / math.sqrt(columns // heads)
-    for chunk in range(chunks):
-        base = chunk * CHUNK
-        raw = sc[base:base + CHUNK]
+        hit = hit.astype(f32).astype(bf16)
+        masks[level] = beside(hit, hit)
+
+    root = 1.0 / math.sqrt(LANES)
+
+    def prepare(chunk, carry):
+        base = pl.multiple_of(chunk * CHUNK, CHUNK)
+        raw = sc[pl.ds(base, CHUNK)]
         shifted = raw + vec_ref[1:2]
         soft = jnp.maximum(shifted, 0.0) + jnp.log1p(jnp.exp(-jnp.abs(shifted)))
         decay = dot(lower, vec_ref[0:1] * soft, precision=lax.Precision.HIGHEST)
@@ -96,14 +112,13 @@
         for head in range(heads):
             norms = []
             for branch in range(3):
-                lane = branch * columns + head * LANES
+                tile = branch * heads + head
                 total = None
                 for i in range(taps):
-                    start = RIM - taps + 1 + base + i
-                    term = xp[start:start + CHUNK, lane:lane + LANES] * taps_ref[i:i + 1, lane:lane + LANES]
+                    term = xp[tile, pl.ds(base + (RIM - taps + 1 + i), CHUNK)] * taps_ref[tile, i:i + 1]
                     total = term if total is None else total + term
                 value = silu(total).astype(bf16)
-                act[branch, head, base:base + CHUNK] = value
+                act[tile, pl.ds(base, CHUNK)] = value
                 if branch < 2:
                     wide = value.astype(f32)
                     norms.append(lax.rsqrt(jnp.sum(wide * wide, axis=-1, keepdims=True) + EPS))
@@ -112,63 +127,85 @@
             comb = jnp.where(ci == 2 * heads + head, norms[0] * root, comb)
             comb = jnp.where(ci == 3 * heads + head, norms[1], comb)
         cols[chunk] = comb
-
-    pairs = [(head, chunk) for head in range(heads) for chunk in range(chunks)]
+        rows_of[chunk] = comb.T
+        return carry
+
+    lax.fori_loop(0, chunks, prepare, 0)
+
+    def part(branch, head, chunk):
+        return act[branch * heads + head, chunk * CHUNK:(chunk + 1) * CHUNK]
+
+    def col(kind, head, chunk):
+        lane = kind * heads + head
+        return cols[chunk, :, lane:lane + 1]
+
+    def row(kind, head, chunk):
+        lane = kind * heads + head
+        return rows_of[chunk, lane:lane + 1, :]
+
+    sets = [(head, chunk) for head in range(heads) for chunk in range(0, chunks, 2)]
+    for s, (head, first) in enumerate(sets):
+        two = (first, first + 1)
+        keys = [part(1, head, c) for c in two]
+        turned = block_diagonal(*[k.T for k in keys])
+        gram = dot(beside(*keys), turned)
+        score = dot(beside(*[part(0, head, c) for c in two]), turned)
+        mix, solve = [], []
+        for i, c in enumerate(two):
+            lanes = slice(i * LANES, (i + 1) * LANES)
+            gap = col(0, head, c) - row(0, head, c)
+            weight = jnp.where(upto, jnp.exp(jnp.minimum(gap, 0.0)) * row(1, head, c), 0.0)
+            mix.append((weight * gram[:, lanes] * col(3, head, c)).astype(bf16))
+            attends[head, c] = (weight * score[:, lanes] * col(2, head, c)).astype(bf16)
+        mix = beside(*mix)
+        mixes[s] = mix
+        eye = jnp.where(ri == ci, 1.0, 0.0)
+        solves[s] = beside(eye, eye) - (mix * masks[0]).astype(f32)
+    for level in range(1, levels):
+        lows, mids = [], []
+        for s in range(len(sets)):
+            lows.append(solves[s].astype(bf16))
+            low = lows[s]
+            mids.append(dot(mixes[s] * masks[level], block_diagonal(low[:, :LANES], low[:, LANES:])).astype(bf16))
+        for s in range(len(sets)):
+            mid = mids[s]
+            solves[s] = solves[s] - dot(lows[s], block_diagonal(mid[:, :LANES], mid[:, LANES:]))
+    change, inner = {}, {}
+    for s, (head, first) in enumerate(sets):
+        two = (first, first + 1)
+        solve = solves[s]
+        new = dot(solve.astype(bf16), block_diagonal(*[part(2, head, c) for c in two]))
+        grown = beside(*[jnp.exp(row(0, head, c)) * row(3, head, c) for c in two])
+        back = dot((solve * grown).astype(bf16), block_diagonal(*[part(1, head, c) for c in two]))
+        for i, c in enumerate(two):
+            lanes = slice(i * LANES, (i + 1) * LANES)
+            both = beside(back[:, lanes], new[:, lanes])
+            decay = col(0, head, c)
+            tail = col(1, head, c) * jnp.exp(decay[CHUNK - 1:] - decay)
+            change[head, c] = dot(part(1, head, c), (both * tail).astype(bf16), (0, 0))
+            inner[head, c] = dot(attends[head, c], both.astype(bf16))
+    runs = {}
+    for c in range(chunks):
+        at = slice(c * CHUNK, (c + 1) * CHUNK)
+        for head in range(heads):
+            decay = col(0, head, c)
+            last = jnp.exp(decay[CHUNK - 1:])
+            eff = (jnp.exp(decay) * col(2, head, c)) * part(0, head, c).astype(f32) - inner[head, c][:, :LANES]
+            if c == 0:
+                qp_ref[head, at] = eff.astype(bf16)
+                o_ref[head, at] = inner[head, c][:, LANES:]
+                runs[head] = beside(
+                    jnp.where(ri == ci, last, 0.0) - change[head, c][:, :LANES], change[head, c][:, LANES:]
+                )
+            else:
+                low = runs[head].astype(bf16)
+                ahead = dot(eff.astype(bf16), low)
+                qp_ref[head, at] = ahead[:, :LANES].astype(bf16)
+                o_ref[head, at] = inner[head, c][:, LANES:] + ahead[:, LANES:]
+                run = last * runs[head] - dot(change[head, c][:, :LANES].astype(bf16), low)
+                runs[head] = beside(run[:, :LANES], run[:, LANES:] + change[head, c][:, LANES:])
     for head in range(heads):
-        todo = list(range(chunks))
-        turned = {}
-        state = {}
-        for chunk in todo:
-            at = slice(chunk * CHUNK, (chunk + 1) * CHUNK)
-            col = cols[chunk]
-            row = col.T
-            k = act[1, head, at]
-            q = act[0, head, at]
-            gap = col[:, head:head + 1] - row[head:head + 1]
-            weight = jnp.exp(jnp.where(upto, gap, 0.0)) * row[heads + head:heads + head + 1]
-            gram = dot(k, k, (1, 1))
-            score = dot(q, k, (1, 1))
-            key_norm = col[:, 3 * heads + head:3 * heads + head + 1]
-            mix = (weight * gram * key_norm).astype(bf16)
-            attend = jnp.where(upto, weight * score * col[:, 2 * heads + head:2 * heads + head + 1], 0.0)
-            x = jnp.where(ri == ci, 1.0, 0.0) - (mix * masks[0]).astype(f32)
-            state[chunk] = [mix, x, attend.astype(bf16), col, row]
-        for level in range(1, levels):
-            low = {c: state[c][1].astype(bf16) for c in todo}
-            mid = {c: dot(state[c][0] * masks[level], low[c]).astype(bf16) for c in todo}
-            for c in todo:
-                state[c][1] = state[c][1] - dot(low[c], mid[c])
-        p_run, r_run = None, None
-        for chunk in todo:
-            mix, x, attend, col, row = state[chunk]
-            at = slice(chunk * CHUNK, (chunk + 1) * CHUNK)
-            k, q, v = act[1, head, at], act[0, head, at], act[2, head, at]
-            decay = col[:, head:head + 1]
-            last = col[CHUNK - 1:CHUNK, head:head + 1]
-            key_norm_row = row[3 * heads + head:3 * heads + head + 1]
-            grown = jnp.exp(row[head:head + 1]) * key_norm_row
-            new = dot(x.astype(bf16), v)
-            back = dot((x * grown).astype(bf16), k)
-            tail = col[:, heads + head:heads + head + 1] * jnp.exp(last - decay)
-            both = jnp.concatenate([back, new], axis=1)
-            change = dot(k, (both * tail).astype(bf16), (0, 0))
-            inner = dot(attend, both.astype(bf16))
-            eff = (jnp.exp(decay) * col[:, 2 * heads + head:2 * heads + head + 1]) * q.astype(f32) - inner[:, :LANES]
-            if chunk == 0:
-                qp_ref[head, at] = eff.astype(bf16)
-                o_ref[head, at] = inner[:, LANES:]
-                p_run = jnp.where(ri == ci, jnp.exp(last), 0.0) - change[:, :LANES]
-                r_run = change[:, LANES:]
-            else:
-                run = jnp.concatenate([p_run, r_run], axis=1)
-                low_run = run.astype(bf16)
-                ahead = dot(eff.astype(bf16), low_run)
-                qp_ref[head, at] = ahead[:, :LANES].astype(bf16)
-                o_ref[head, at] = inner[:, LANES:] + ahead[:, LANES:]
-                run = jnp.exp(last) * run - dot(change[:, :LANES].astype(bf16), low_run)
-                p_run = run[:, :LANES]
-                r_run = run[:, LANES:] + change[:, LANES:]
-        x_ref[head] = jnp.concatenate([p_run, r_run], axis=1).astype(bf16)
+        x_ref[head] = runs[head].astype(bf16)
 
 
 def join_kernel(mine_ref, earlier_ref, out_ref):
@@ -224,7 +261,8 @@
     rim = shifted(rim, "seq", 1)
     scalars = jnp.dot(tokens, small, preferred_element_type=f32)
     gate = jnp.dot(tokens, w_gate, preferred_element_type=f32)
-    taps = conv_weight.reshape(conv_weight.shape[0], 3 * columns).astype(f32)
+    count = conv_weight.shape[0]
+    taps = conv_weight.reshape(count, 3 * heads, dim).transpose(1, 0, 2).astype(f32)
     vectors = jnp.pad(jnp.stack([-decay_rate, dt_bias]), ((0, 6), (0, LANES - heads)))
     chunks = seq_rows // CHUNK
     cost = functools.partial(pl.CostEstimate, transcendentals=0, bytes_accessed=4 << 20)
@@ -238,11 +276,15 @@
         in_specs=[whole(pltpu.SMEM)] + [whole()] * 5,
         out_specs=(whole(),) * 3,
         scratch_shapes=[
-            pltpu.VMEM((seq_rows + RIM, 3 * columns), f32),
-            pltpu.VMEM((3, heads, seq_rows, dim), bf16),
+            pltpu.VMEM((3 * heads, seq_rows + RIM, dim), f32),
+            pltpu.VMEM((3 * heads, seq_rows, dim), bf16),
             pltpu.VMEM((seq_rows, LANES), f32),
             pltpu.VMEM((chunks, CHUNK, LANES), f32),
-            pltpu.VMEM((CHUNK.bit_length() - 1, CHUNK, CHUNK), bf16),
+            pltpu.VMEM((chunks, CHUNK, LANES), f32),
+            pltpu.VMEM((CHUNK.bit_length() - 1, CHUNK, 2 * CHUNK), bf16),
+            pltpu.VMEM((heads * chunks // 2, CHUNK, 2 * CHUNK), bf16),
+            pltpu.VMEM((heads * chunks // 2, CHUNK, 2 * CHUNK), f32),
+            pltpu.VMEM((heads, chunks, CHUNK, CHUNK), bf16),
         ],
         cost_estimate=cost(flops=2000000000),
         name="delta",

time: 95.3 us -> 88.2 us (0.925)
  Pallas kernels: 26.8 us -> 19.7 us
    pallas_call x1, Pallas kernels: 19.3 us -> 12.2 us  [per_device(): pl.pallas_call(functools.partial(delta_kernel, heads, blocks), out_shape=...]
  transfers between devices with their start and end apart: 9 -> 9, of which waited for: 5 -> 5; matrix products, arithmetic and copies ran while one was open for 19% -> 20% of each run, Pallas kernels for 0% -> 0%
where the time goes in v1:
time: 88.2 us; the launch traced here: 87.5 us
  starting transfers between devices  27.6 us (31%)
  Pallas kernels  19.7 us (22%)
  local copies, waits for them, and re-layouts  13.9 us (16%)
  waiting for transfers between devices  12.6 us (14%)
  matrix products  12.3 us (14%)
  other arithmetic  1.21 us (1%)
    ppermute x5, starting transfers between devices, shifted(): lax.ppermute(value, axis, [(i, i + distance) for i in range(count - dista...  21 us
    unnamed x29, local copies, waits for them, and re-layouts  12.9 us
    pallas_call x1, Pallas kernels, per_device(): pl.pallas_call(functools.partial(delta_kernel, heads, blocks), out_shape=...  12.2 us
    dot_general x1, matrix products, per_device(): jnp.dot(tokens, qkv_matrix, preferred_element_type=f32).astype(bf16)  7.09 us
    ppermute x5, waiting for transfers between devices, shifted(): lax.ppermute(value, axis, [(i, i + distance) for i in range(count - dista...  6.67 us
    ppermute x4, starting transfers between devices, swap(): return lax.ppermute(value, axis, [(i, i ^ step) for i in range(count)])  6.67 us
    ppermute x4, waiting for transfers between devices, swap(): return lax.ppermute(value, axis, [(i, i ^ step) for i in range(count)])  5.89 us
    pallas_call x2, Pallas kernels, join(): pl.pallas_call(join_kernel, out_shape=jax.ShapeDtypeStruct(mine.shape, bf...  3.89 us
  transfers between devices with their start and end apart: 9, of which 5 were waited for; matrix products, arithmetic and copies ran while one was open for 20% of the time, Pallas kernels for 0%

profile of v1, /device:TPU:0, one launch (start us, length us, event | category | flops | bytes accessed | tf_op | source)
XLA Modules:
  0.0 87.5 jit_solution(8675141040201186423)
XLA Ops:
  0.0 3.0 %collective-permute-start = (bf16[128,2048]{1,0:T(8,128)(2,1)}, bf16[128,2048]{1,0:T(8,128)(2,1)S(1)}, u32[]{:S(2)}, u32[]{:S(2)}) collective-permute-start(bf16[128,2048]{1,0:T(8,128)(2,1)} %param.8), channel_id=1, source_target_pairs={{0,1},{1,0},{2,3},{3,2},{4,5},{5,4},{6,7},{7,6},{8,9},{9,8},{10,11... | collective-permute-start | bytes 1572872 | tf_op jit(solution)/shard_map/ppermute | solution.py:37
  3.0 1.5 %collective-permute-start.1 = (bf16[128,2048]{1,0:T(8,128)(2,1)}, bf16[128,2048]{1,0:T(8,128)(2,1)S(1)}, u32[]{:S(2)}, u32[]{:S(2)}) collective-permute-start(bf16[128,2048]{1,0:T(8,128)(2,1)} %param.8), channel_id=1, source_target_pairs={{0,2},{1,3},{2,0},{3,1},{4,6},{5,7},{6,4},{7,5},{8,10},{9,11},{10,... | collective-permute-start | bytes 1572872 | tf_op jit(solution)/shard_map/ppermute | solution.py:37
  4.5 9.0 %copy.9 = bf16[2048,3,512]{0,2,1:T(8,128)(2,1)} copy(bf16[2048,3,512]{2,0,1:T(8,128)(2,1)} %param.9) | data formatting | bytes 12582912 | tf_op args[1]
  14.7 1.1 %constant_dynamic-update-slice_fusion.4 = bf16[512,2048]{1,0:T(8,128)(2,1)S(1)} fusion(bf16[128,2048]{1,0:T(8,128)(2,1)} %param.8), kind=kLoop, calls=%fused_computation.8 | loop fusion | bytes 1048576
  15.8 0.7 collective-permute-done.1
  17.1 1.7 %collective-permute-start.3 = (bf16[64,2048]{1,0:T(8,128)(2,1)S(1)}, bf16[64,2048]{1,0:T(8,128)(2,1)S(1)}, u32[]{:S(2)}, u32[]{:S(2)}) collective-permute-start(bf16[64,2048]{1,0:T(8,128)(2,1)S(1)} %slice.13), channel_id=1, source_target_pairs={{0,2},{1,3},{2,0},{3,1},{4,6},{5,7},{6,4},{7,5},{8,10},{9,11},{10,... | collective-permute-start | bytes 786440 | tf_op jit(solution)/shard_map/ppermute | solution.py:37
  18.9 4.7 %collective-permute-done.2 = bf16[64,2048]{1,0:T(8,128)(2,1)S(1)} collective-permute-done((bf16[64,2048]{1,0:T(8,128)(2,1)S(1)}, bf16[64,2048]{1,0:T(8,128)(2,1)S(1)}, u32[]{:S(2)}, u32[]{:S(2)}) %collective-permute-start.2) | collective-permute-done | bytes 262176 | tf_op jit(solution)/shard_map/ppermute | solution.py:37
  24.1 7.1 %convolution_convert_fusion.p_ref = bf16[512,1536]{1,0:T(8,128)(2,1)S(1)} fusion(bf16[512,2048]{1,0:T(8,128)(2,1)S(1)} %constant_dynamic-update-slice_fusion, bf16[2048,1536]{0,1:T(8,128)(2,1)} %bitcast.17), kind=kOutput, calls=%fused_computation | convolution fusion | flops 3222011904 | bytes 9961472 | tf_op jit(solution)/shard_map/dot_general | solution.py:258
  31.2 1.3 %collective-permute-start.4 = (bf16[8,1536]{1,0:T(8,128)(2,1)S(1)}, bf16[8,1536]{1,0:T(8,128)(2,1)S(1)}, u32[]{:S(2)}, u32[]{:S(2)}) collective-permute-start(bf16[8,1536]{1,0:T(8,128)(2,1)S(1)} %constant_dynamic-slice_fusion), channel_id=1, source_target_pairs={{0,4},{4,8},{8,12},{12,16},{16,20},{20,24},{24,28},{1,5},{5,9},{9,... | collective-permute-start | bytes 73736 | tf_op jit(solution)/shard_map/ppermute | solution.py:239
  32.5 1.4 %fusion.sc_ref = f32[512,128]{1,0:T(8,128)} fusion(bf16[512,2048]{1,0:T(8,128)(2,1)S(1)} %constant_dynamic-update-slice_fusion, bf16[2048,8]{0,1:T(8,128)(2,1)S(1)} %reshape.13), kind=kOutput, calls=%fused_computation.1 | convolution fusion | flops 268435456 | bytes 2392064 | tf_op jit(solution)/shard_map/dot_general | solution.py:262
  34.5 12.2 %delta.1 = (bf16[4,128,256]{2,1,0:T(8,128)(2,1)}, bf16[4,512,128]{2,1,0:T(8,128)(2,1)}, f32[4,512,128]{2,1,0:T(8,128)}) custom-call(s32[1]{0:T(128)} %bitcast.me_ref, bf16[512,1536]{1,0:T(8,128)(2,1)} %copy-done.9, bf16[8,1536]{1,0:T(8,128)(2,1)} %copy-done.10, f32[12,4,128]{2,1,0:T(4,128)} %convert_bitcast_fusion.taps_ref, f32[512,128]{1,0:T(8,128)} %fusion.sc_ref, ...), custom_call_target="tpu_custom_call" | custom-call | flops 2000000000 | bytes 4194304 | tf_op jit(solution)/shard_map/delta/pallas_call | solution.py:269
  46.7 4.1 %collective-permute-start.5 = (bf16[4,128,256]{2,1,0:T(8,128)(2,1)}, bf16[4,128,256]{2,1,0:T(8,128)(2,1)S(1)}, u32[]{:S(2)}, u32[]{:S(2)}) collective-permute-start(bf16[4,128,256]{2,1,0:T(8,128)(2,1)} %get-tuple-element.10.mine_ref), channel_id=1, source_target_pairs={{0,4},{4,8},{8,12},{12,16},{16,20},{20,24},{24,28},{1,5},{5,9},{9,... | collective-permute-start | bytes 786440 | tf_op jit(solution)/shard_map/ppermute | solution.py:239
  50.8 1.3 %collective-permute-done.5.earlier_ref = bf16[4,128,256]{2,1,0:T(8,128)(2,1)S(1)} collective-permute-done((bf16[4,128,256]{2,1,0:T(8,128)(2,1)}, bf16[4,128,256]{2,1,0:T(8,128)(2,1)S(1)}, u32[]{:S(2)}, u32[]{:S(2)}) %collective-permute-start.5) | collective-permute-done | bytes 262176 | tf_op jit(solution)/shard_map/ppermute | solution.py:239
  52.1 0.7 copy-done.1
  52.8 1.9 %join.2.mine_ref = bf16[4,128,256]{2,1,0:T(8,128)(2,1)} custom-call(bf16[4,128,256]{2,1,0:T(8,128)(2,1)} %get-tuple-element.10.mine_ref, bf16[4,128,256]{2,1,0:T(8,128)(2,1)} %copy-done.1), custom_call_target="tpu_custom_call" | custom-call | flops 50000000 | bytes 4194304 | tf_op jit(solution)/shard_map/join/pallas_call | solution.py:294
  54.8 8.3 %collective-permute-start.6 = (bf16[4,128,256]{2,1,0:T(8,128)(2,1)}, bf16[4,128,256]{2,1,0:T(8,128)(2,1)S(1)}, u32[]{:S(2)}, u32[]{:S(2)}) collective-permute-start(bf16[4,128,256]{2,1,0:T(8,128)(2,1)} %join.2.mine_ref), channel_id=1, source_target_pairs={{0,8},{4,12},{8,16},{12,20},{16,24},{20,28},{1,9},{5,13},{9,17},{1... | collective-permute-start | bytes 786440 | tf_op jit(solution)/shard_map/ppermute | solution.py:239
  63.0 5.3 %collective-permute-done.6.earlier_ref = bf16[4,128,256]{2,1,0:T(8,128)(2,1)S(1)} collective-permute-done((bf16[4,128,256]{2,1,0:T(8,128)(2,1)}, bf16[4,128,256]{2,1,0:T(8,128)(2,1)S(1)}, u32[]{:S(2)}, u32[]{:S(2)}) %collective-permute-start.6) | collective-permute-done | bytes 262176 | tf_op jit(solution)/shard_map/ppermute | solution.py:239
  68.4 0.7 copy-done.2
  69.1 1.9 %join.3 = bf16[4,128,256]{2,1,0:T(8,128)(2,1)} custom-call(bf16[4,128,256]{2,1,0:T(8,128)(2,1)} %join.2.mine_ref, bf16[4,128,256]{2,1,0:T(8,128)(2,1)} %copy-done.2), custom_call_target="tpu_custom_call" | custom-call | flops 50000000 | bytes 4194304 | tf_op jit(solution)/shard_map/join/pallas_call | solution.py:294
  71.0 1.3 %collective-permute-start.7 = (bf16[4,128,256]{2,1,0:T(8,128)(2,1)}, bf16[4,128,256]{2,1,0:T(8,128)(2,1)S(1)}, u32[]{:S(2)}, u32[]{:S(2)}) collective-permute-start(bf16[4,128,256]{2,1,0:T(8,128)(2,1)} %join.3), channel_id=1, source_target_pairs={{0,4},{4,8},{8,12},{12,16},{16,20},{20,24},{24,28},{1,5},{5,9},{9,... | collective-permute-start | bytes 786440 | tf_op jit(solution)/shard_map/ppermute | solution.py:239
  72.3 0.9 %slice.14 = bf16[4,128,128]{2,1,0:T(8,128)(2,1)S(1)} slice(bf16[4,128,256]{2,1,0:T(8,128)(2,1)} %join.3), slice={[0:4], [0:128], [128:256]} | slice | bytes 262144 | tf_op jit(solution)/shard_map/slice | solution.py:309
  73.2 6.0 %collective-permute-start.8 = (bf16[4,128,128]{2,1,0:T(8,128)(2,1)S(1)}, bf16[4,128,128]{2,1,0:T(8,128)(2,1)S(1)}, u32[]{:S(2)}, u32[]{:S(2)}) collective-permute-start(bf16[4,128,128]{2,1,0:T(8,128)(2,1)S(1)} %slice.14), channel_id=1, source_target_pairs={{0,20},{4,24},{8,28},{1,21},{5,25},{9,29},{2,22},{6,26},{10,30},{3... | collective-permute-start | bytes 393224 | tf_op jit(solution)/shard_map/ppermute | solution.py:239
  79.3 3.8 %fusion.3.gate_ref = f32[512,512]{1,0:T(8,128)} fusion(bf16[512,2048]{1,0:T(8,128)(2,1)} %copy-done.4, bf16[2048,512]{1,0:T(8,128)(2,1)S(1)} %copy-done), kind=kOutput, calls=%fused_computation.15 | convolution fusion | flops 1073741824 | bytes 5242880 | tf_op jit(solution)/shard_map/dot_general | solution.py:263
  83.9 3.6 %final.1 = bf16[512,512]{1,0:T(8,128)(2,1)} custom-call(s32[1]{0:T(128)} %bitcast.me_ref, bf16[4,512,128]{2,1,0:T(8,128)(2,1)} %get-tuple-element.8.qp_ref, f32[4,512,128]{2,1,0:T(8,128)} %get-tuple-element.9.o_ref, bf16[4,128,256]{2,1,0:T(8,128)(2,1)} %copy-done.3, bf16[4,128,128]{2,1,0:T(8,128)(2,1)} %copy-done.5, f32[512,512]{1,0:T(8,128)} %fusion.3.gate_ref, ...), custom_call_target="tpu_custom_call" | custom-call | flops 200000000 | bytes 4194304 | tf_op jit(solution)/shard_map/final/pallas_call | solution.py:310
  (39 shorter events, 3.7 us)
Async XLA Ops:
  0.0 79.3 %copy-start = (bf16[2048,512]{1,0:T(8,128)(2,1)S(1)}, bf16[2048,512]{1,0:T(8,128)(2,1)}, u32[]{:S(2)}) copy-start(bf16[2048,512]{1,0:T(8,128)(2,1)} %param.10) | copy-start | bytes 6291460
  0.0 17.0 %collective-permute-start = (bf16[128,2048]{1,0:T(8,128)(2,1)}, bf16[128,2048]{1,0:T(8,128)(2,1)S(1)}, u32[]{:S(2)}, u32[]{:S(2)}) collective-permute-start(bf16[128,2048]{1,0:T(8,128)(2,1)} %param.8), channel_id=1, source_target_pairs={{0,1},{1,0},{2,3},{3,2},{4,5},{5,4},{6,7},{7,6},{8,9},{9,8},{10,11... | collective-permute-start | bytes 1572872 | tf_op jit(solution)/shard_map/ppermute | solution.py:37
  3.0 13.6 %collective-permute-start.1 = (bf16[128,2048]{1,0:T(8,128)(2,1)}, bf16[128,2048]{1,0:T(8,128)(2,1)S(1)}, u32[]{:S(2)}, u32[]{:S(2)}) collective-permute-start(bf16[128,2048]{1,0:T(8,128)(2,1)} %param.8), channel_id=1, source_target_pairs={{0,2},{1,3},{2,0},{3,1},{4,6},{5,7},{6,4},{7,5},{8,10},{9,11},{10,... | collective-permute-start | bytes 1572872 | tf_op jit(solution)/shard_map/ppermute | solution.py:37
  4.5 9.0 %copy-start.6 = (bf16[2048,2,4]{0,2,1:T(4,128)(2,1)S(1)}, bf16[2048,2,4]{0,2,1:T(4,128)(2,1)}, u32[]{:S(2)}) copy-start(bf16[2048,2,4]{0,2,1:T(4,128)(2,1)} %param.11) | copy-start | bytes 98308
  4.5 9.0 %copy-start.11 = (f32[4]{0:T(128)S(1)}, f32[4]{0:T(128)}, u32[]{:S(2)}) copy-start(f32[4]{0:T(128)} %param.13) | copy-start | bytes 52
  4.5 9.0 %copy-start.8 = (f32[4]{0:T(128)S(1)}, f32[4]{0:T(128)}, u32[]{:S(2)}) copy-start(f32[4]{0:T(128)} %param.14) | copy-start | bytes 52
  4.5 9.6 %copy-start.7 = (bf16[4,3,512]{2,0,1:T(4,128)(2,1)S(1)}, bf16[4,3,512]{2,0,1:T(4,128)(2,1)}, u32[]{:S(2)}) copy-start(bf16[4,3,512]{2,0,1:T(4,128)(2,1)} %param.12) | copy-start | bytes 36868
  16.6 7.0 %collective-permute-start.2 = (bf16[64,2048]{1,0:T(8,128)(2,1)S(1)}, bf16[64,2048]{1,0:T(8,128)(2,1)S(1)}, u32[]{:S(2)}, u32[]{:S(2)}) collective-permute-start(bf16[64,2048]{1,0:T(8,128)(2,1)S(1)} %slice.12), channel_id=1, source_target_pairs={{0,1},{1,0},{2,3},{3,2},{4,5},{5,4},{6,7},{7,6},{8,9},{9,8},{10,11... | collective-permute-start | bytes 786440 | tf_op jit(solution)/shard_map/ppermute | solution.py:37
  17.1 7.0 %collective-permute-start.3 = (bf16[64,2048]{1,0:T(8,128)(2,1)S(1)}, bf16[64,2048]{1,0:T(8,128)(2,1)S(1)}, u32[]{:S(2)}, u32[]{:S(2)}) collective-permute-start(bf16[64,2048]{1,0:T(8,128)(2,1)S(1)} %slice.13), channel_id=1, source_target_pairs={{0,2},{1,3},{2,0},{3,1},{4,6},{5,7},{6,4},{7,5},{8,10},{9,11},{10,... | collective-permute-start | bytes 786440 | tf_op jit(solution)/shard_map/ppermute | solution.py:37
  24.1 8.4 %copy-start.4 = (bf16[512,2048]{1,0:T(8,128)(2,1)}, bf16[512,2048]{1,0:T(8,128)(2,1)S(1)}, u32[]{:S(2)}) copy-start(bf16[512,2048]{1,0:T(8,128)(2,1)S(1)} %constant_dynamic-update-slice_fusion) | copy-start | bytes 6291460
  31.2 2.7 %copy-start.9 = (bf16[512,1536]{1,0:T(8,128)(2,1)}, bf16[512,1536]{1,0:T(8,128)(2,1)S(1)}, u32[]{:S(2)}) copy-start(bf16[512,1536]{1,0:T(8,128)(2,1)S(1)} %convolution_convert_fusion.p_ref) | copy-start | bytes 4718596
  31.2 2.7 %collective-permute-start.4 = (bf16[8,1536]{1,0:T(8,128)(2,1)S(1)}, bf16[8,1536]{1,0:T(8,128)(2,1)S(1)}, u32[]{:S(2)}, u32[]{:S(2)}) collective-permute-start(bf16[8,1536]{1,0:T(8,128)(2,1)S(1)} %constant_dynamic-slice_fusion), channel_id=1, source_target_pairs={{0,4},{4,8},{8,12},{12,16},{16,20},{20,24},{24,28},{1,5},{5,9},{9,... | collective-permute-start | bytes 73736 | tf_op jit(solution)/shard_map/ppermute | solution.py:239
  33.9 0.6 copy-start.10
  46.7 5.4 %collective-permute-start.5 = (bf16[4,128,256]{2,1,0:T(8,128)(2,1)}, bf16[4,128,256]{2,1,0:T(8,128)(2,1)S(1)}, u32[]{:S(2)}, u32[]{:S(2)}) collective-permute-start(bf16[4,128,256]{2,1,0:T(8,128)(2,1)} %get-tuple-element.10.mine_ref), channel_id=1, source_target_pairs={{0,4},{4,8},{8,12},{12,16},{16,20},{20,24},{24,28},{1,5},{5,9},{9,... | collective-permute-start | bytes 786440 | tf_op jit(solution)/shard_map/ppermute | solution.py:239
  52.1 0.7 copy-start.1
  54.8 13.6 %collective-permute-start.6 = (bf16[4,128,256]{2,1,0:T(8,128)(2,1)}, bf16[4,128,256]{2,1,0:T(8,128)(2,1)S(1)}, u32[]{:S(2)}, u32[]{:S(2)}) collective-permute-start(bf16[4,128,256]{2,1,0:T(8,128)(2,1)} %join.2.mine_ref), channel_id=1, source_target_pairs={{0,8},{4,12},{8,16},{12,20},{16,24},{20,28},{1,9},{5,13},{9,17},{1... | collective-permute-start | bytes 786440 | tf_op jit(solution)/shard_map/ppermute | solution.py:239
  68.4 0.7 copy-start.2
  71.0 12.1 %collective-permute-start.7 = (bf16[4,128,256]{2,1,0:T(8,128)(2,1)}, bf16[4,128,256]{2,1,0:T(8,128)(2,1)S(1)}, u32[]{:S(2)}, u32[]{:S(2)}) collective-permute-start(bf16[4,128,256]{2,1,0:T(8,128)(2,1)} %join.3), channel_id=1, source_target_pairs={{0,4},{4,8},{8,12},{12,16},{16,20},{20,24},{24,28},{1,5},{5,9},{9,... | collective-permute-start | bytes 786440 | tf_op jit(solution)/shard_map/ppermute | solution.py:239
  73.2 9.9 %collective-permute-start.8 = (bf16[4,128,128]{2,1,0:T(8,128)(2,1)S(1)}, bf16[4,128,128]{2,1,0:T(8,128)(2,1)S(1)}, u32[]{:S(2)}, u32[]{:S(2)}) collective-permute-start(bf16[4,128,128]{2,1,0:T(8,128)(2,1)S(1)} %slice.14), channel_id=1, source_target_pairs={{0,20},{4,24},{8,28},{1,21},{5,25},{9,29},{2,22},{6,26},{10,30},{3... | collective-permute-start | bytes 393224 | tf_op jit(solution)/shard_map/ppermute | solution.py:239
  83.1 0.6 copy-start.5
  83.1 0.8 copy-start.3

commit v2 on v1

v2 whole, which is shorter than its diff:
```python
import functools
import math

import jax
import jax.numpy as jnp
from jax import lax
from jax.experimental import pallas as pl
from jax.experimental.pallas import tpu as pltpu
from jax.sharding import PartitionSpec as P

CHUNK = 128
LANES = 128
RIM = 16
EPS = 1e-6
PROJECT_FLOPS = 3000000000
DELTA_FLOPS = 3000000000
REACH_FLOPS = 2000000000
SMALL_FLOPS = 50000000

f32 = jnp.float32
bf16 = jnp.bfloat16


def dot(left, right, contract=(1, 0), precision=None):
    dims = (((contract[0],), (contract[1],)), ((), ()))
    return lax.dot_general(left, right, dims, precision=precision, preferred_element_type=f32)


def whole(memory=pltpu.VMEM):
    return pl.BlockSpec(memory_space=memory)


def gather_blocks(block, axis):
    count = lax.axis_size(axis)
    bits = count.bit_length() - 1
    half = block.shape[0] // 2

    def swap(value, bit):
        step = 1 << bit
        return lax.ppermute(value, axis, [(i, i ^ step) for i in range(count)])

    found = {0: block}
    for bit in range(bits):
        found[1 << bit] = swap(block, bit)
    halves = []
    for number, order in enumerate((range(bits), range(bits - 1, -1, -1))):
        part = {m: value[number * half:(number + 1) * half] for m, value in found.items()}
        for bit in order:
            for mask in list(part):
                if mask | (1 << bit) not in part:
                    part[mask | (1 << bit)] = swap(part[mask], bit)
        halves.append(part)
    early = [found[m] if m in found else (halves[0][m], halves[1][m]) for m in range(count - 1)]
    flat = []
    for item in early:
        flat.extend(item if isinstance(item, tuple) else (item,))
    return flat, [halves[0][count - 1], halves[1][count - 1]]


def rim_rows(block, count):
    seq_count, tp_count = lax.axis_size("seq"), lax.axis_size("tp")
    tail = block[-count:]
    total = None
    for j in range(tp_count):
        route = [(s * tp_count - 1, s * tp_count + j) for s in range(1, seq_count)]
        part = lax.ppermute(tail, ("seq", "tp"), route)
        total = part if total is None else total + part
    return total


def silu(x):
    return x / (1.0 + jnp.exp(-x))


def block_diagonal(left, right):
    hole = jnp.zeros_like(left)
    return jnp.concatenate(
        [jnp.concatenate([left, hole], axis=1), jnp.concatenate([hole, right], axis=1)], axis=0
    )


def beside(left, right):
    return jnp.concatenate([left, right], axis=1)


def project_kernel(count, *refs):
    blocks, rim_ref, w_ref, small_ref = refs[:count], *refs[count:count + 3]
    p_ref, rim_out, sc_ref = refs[count + 3:]
    rows = p_ref.shape[1]
    tokens = jnp.concatenate([ref[...] for ref in blocks] + [rim_ref[...]], axis=0)
    sc_ref[...] = dot(tokens, small_ref[...])[:rows]

    def one(branch, carry):
        out = dot(tokens, w_ref[branch]).astype(bf16)
        p_ref[branch] = out[:rows]
        rim_out[branch] = out[rows:]
        return carry

    lax.fori_loop(0, w_ref.shape[0], one, 0)


def block_diagonal(left, right):
    hole = jnp.zeros_like(left)
    return jnp.concatenate(
        [jnp.concatenate([left, hole], axis=1), jnp.concatenate([hole, right], axis=1)], axis=0
    )


def beside(left, right):
    return jnp.concatenate([left, right], axis=1)


def grid_index(shape):
    return lax.broadcasted_iota(jnp.int32, shape, 0), lax.broadcasted_iota(jnp.int32, shape, 1)


def delta_kernel(
    heads, blocks, me_ref, p_ref, rim_ref, sc_ref, late0_ref, late1_ref, w_ref, small_ref,
    taps_ref, vec_ref, x_ref, both_ref, low_ref, act, cols, rows_of,
    xp, sc, masks, mixes, solves,
):
    seq_rows = act.shape[1]
    rows = seq_rows // blocks
    chunks = seq_rows // CHUNK
    taps = taps_ref.shape[1]
    me = me_ref[0]

    def place(m, offset=0):
        return pl.multiple_of(offset + lax.bitwise_xor(me, m) * rows, 8)

    late = jnp.concatenate([late0_ref[...], late1_ref[...]], axis=0)
    sc[pl.ds(place(blocks - 1), rows)] = dot(late, small_ref[...])
    for m in range(blocks - 1):
        sc[pl.ds(place(m), rows)] = sc_ref[m * rows:(m + 1) * rows]

    def fill(branch, carry):
        made = dot(late, w_ref[branch]).astype(bf16).astype(f32)
        for head in range(heads):
            tile = branch * heads + head
            lanes = slice(head * LANES, (head + 1) * LANES)
            xp[tile, :RIM] = rim_ref[branch, :, lanes].astype(f32)
            xp[tile, pl.ds(place(blocks - 1, RIM), rows)] = made[:, lanes]
            for m in range(blocks - 1):
                xp[tile, pl.ds(place(m, RIM), rows)] = p_ref[branch, m * rows:(m + 1) * rows, lanes].astype(f32)
        return carry

    lax.fori_loop(0, 3, fill, 0)

    ri, ci = grid_index((CHUNK, CHUNK))
    upto = ri >= ci
    lower = upto.astype(f32)
    levels = CHUNK.bit_length() - 1
    for level in range(levels):
        hit = ((ri >> (level + 1)) == (ci >> (level + 1))) & ((ri >> level) > (ci >> level))
        hit = hit.astype(f32).astype(bf16)
        masks[level] = beside(hit, hit)

    root = 1.0 / math.sqrt(LANES)

    def prepare(chunk, carry):
        base = pl.multiple_of(chunk * CHUNK, CHUNK)
        raw = sc[pl.ds(base, CHUNK)]
        shifted = raw + vec_ref[1:2]
        soft = jnp.maximum(shifted, 0.0) + jnp.log1p(jnp.exp(-jnp.abs(shifted)))
        decay = dot(lower, vec_ref[0:1] * soft, precision=lax.Precision.HIGHEST)
        beta = 1.0 / (1.0 + jnp.exp(-raw))
        comb = jnp.where(ci < heads, decay, 0.0)
        for head in range(heads):
            norms = []
            for branch in range(3):
                tile = branch * heads + head
                total = None
                for i in range(taps):
                    term = xp[tile, pl.ds(base + (RIM - taps + 1 + i), CHUNK)] * taps_ref[tile, i:i + 1]
                    total = term if total is None else total + term
                value = silu(total).astype(bf16)
                act[tile, pl.ds(base, CHUNK)] = value
                if branch < 2:
                    wide = value.astype(f32)
                    norms.append(lax.rsqrt(jnp.sum(wide * wide, axis=-1, keepdims=True) + EPS))
            scaled = beta[:, heads + head:heads + head + 1] * norms[1]
            comb = jnp.where(ci == heads + head, scaled, comb)
            comb = jnp.where(ci == 2 * heads + head, norms[0] * root, comb)
            comb = jnp.where(ci == 3 * heads + head, norms[1], comb)
        cols[chunk] = comb
        rows_of[chunk] = comb.T
        return carry

    lax.fori_loop(0, chunks, prepare, 0)

    def part(branch, head, chunk):
        return act[branch * heads + head, chunk * CHUNK:(chunk + 1) * CHUNK]

    def col(kind, head, chunk):
        lane = kind * heads + head
        return cols[chunk, :, lane:lane + 1]

    def row(kind, head, chunk):
        lane = kind * heads + head
        return rows_of[chunk, lane:lane + 1, :]

    sets = [(head, chunk) for head in range(heads) for chunk in range(0, chunks, 2)]
    for s, (head, first) in enumerate(sets):
        two = (first, first + 1)
        keys = [part(1, head, c) for c in two]
        gram = dot(beside(*keys), block_diagonal(*[k.T for k in keys]))
        mix = []
        for i, c in enumerate(two):
            lanes = slice(i * LANES, (i + 1) * LANES)
            gap = col(0, head, c) - row(0, head, c)
            weight = jnp.exp(jnp.minimum(gap, 0.0)) * row(1, head, c)
            mix.append((weight * gram[:, lanes] * col(3, head, c)).astype(bf16))
        mix = beside(*mix)
        mixes[s] = mix
        eye = jnp.where(ri == ci, 1.0, 0.0)
        solves[s] = beside(eye, eye) - (mix * masks[0]).astype(f32)
    for level in range(1, levels):
        lows, mids = [], []
        for s in range(len(sets)):
            low = solves[s].astype(bf16)
            lows.append(low)
            mids.append(dot(mixes[s] * masks[level], block_diagonal(low[:, :LANES], low[:, LANES:])).astype(bf16))
        for s in range(len(sets)):
            mid = mids[s]
            solves[s] = solves[s] - dot(lows[s], block_diagonal(mid[:, :LANES], mid[:, LANES:]))
    change = {}
    for s, (head, first) in enumerate(sets):
        two = (first, first + 1)
        solve = solves[s]
        new = dot(solve.astype(bf16), block_diagonal(*[part(2, head, c) for c in two]))
        grown = beside(*[jnp.exp(row(0, head, c)) * row(3, head, c) for c in two])
        back = dot((solve * grown).astype(bf16), block_diagonal(*[part(1, head, c) for c in two]))
        for i, c in enumerate(two):
            lanes = slice(i * LANES, (i + 1) * LANES)
            both = beside(back[:, lanes], new[:, lanes])
            decay = col(0, head, c)
            tail = col(1, head, c) * jnp.exp(decay[CHUNK - 1:] - decay)
            change[head, c] = dot(part(1, head, c), (both * tail).astype(bf16), (0, 0))
            both_ref[head, c] = both.astype(bf16)
    runs = {}
    for c in range(chunks):
        for head in range(heads):
            last = jnp.exp(col(0, head, c)[CHUNK - 1:])
            if c == 0:
                runs[head] = beside(
                    jnp.where(ri == ci, last, 0.0) - change[head, c][:, :LANES], change[head, c][:, LANES:]
                )
            else:
                low = runs[head].astype(bf16)
                low_ref[head, c - 1] = low
                run = last * runs[head] - dot(change[head, c][:, :LANES].astype(bf16), low)
                runs[head] = beside(run[:, :LANES], run[:, LANES:] + change[head, c][:, LANES:])
    for head in range(heads):
        x_ref[head] = runs[head].astype(bf16)


def reach_kernel(
    heads, blocks, count, me_ref, both_ref, low_ref, act, cols, rows_of, w_ref, *refs
):
    tokens_refs, (qp_ref, o_ref, gate_ref) = refs[:count], refs[count:]
    seq_rows = act.shape[1]
    rows = seq_rows // blocks
    chunks = seq_rows // CHUNK
    me = me_ref[0]
    tokens = jnp.concatenate([ref[...] for ref in tokens_refs], axis=0)
    gate = silu(dot(tokens, w_ref[...]))
    for m in range(blocks):
        at = pl.multiple_of(lax.bitwise_xor(me, m) * rows, 8)
        gate_ref[pl.ds(at, rows)] = gate[m * rows:(m + 1) * rows]
    ri, ci = grid_index((CHUNK, CHUNK))
    upto = ri >= ci
    for head in range(heads):
        for c in range(chunks):
            at = slice(c * CHUNK, (c + 1) * CHUNK)

            def col(kind):
                lane = kind * heads + head
                return cols[c, :, lane:lane + 1]

            def row(kind):
                lane = kind * heads + head
                return rows_of[c, lane:lane + 1, :]

            q = act[head, at]
            score = dot(q, act[heads + head, at], (1, 1))
            weight = jnp.exp(jnp.minimum(col(0) - row(0), 0.0)) * row(1)
            attend = jnp.where(upto, weight * score * col(2), 0.0).astype(bf16)
            inner = dot(attend, both_ref[head, c])
            eff = (jnp.exp(col(0)) * col(2)) * q.astype(f32) - inner[:, :LANES]
            if c == 0:
                qp_ref[head, at] = eff.astype(bf16)
                o_ref[head, at] = inner[:, LANES:]
            else:
                ahead = dot(eff.astype(bf16), low_ref[head, c - 1])
                qp_ref[head, at] = ahead[:, :LANES].astype(bf16)
                o_ref[head, at] = inner[:, LANES:] + ahead[:, LANES:]


def pair_kernel(share, core_ref, mine_ref, other_ref, out_ref):
    core = core_ref[0]
    heads = mine_ref.shape[0]
    for j in range(out_ref.shape[0]):
        head = core * out_ref.shape[0] + j if share else j
        mine, other = mine_ref[head], other_ref[head]
        first = jnp.where(core == 0, mine, other)
        second = jnp.where(core == 0, other, mine)
        both = dot(second[:, :LANES], first)
        out_ref[j, :, :LANES] = both[:, :LANES].astype(bf16)
        out_ref[j, :, LANES:] = (both[:, LANES:] + second[:, LANES:].astype(f32)).astype(bf16)


def fold_kernel(*refs):
    out_ref = refs[-1]
    for j in range(out_ref.shape[0]):
        state = refs[0][j].astype(f32)
        for ref in refs[1:-1]:
            step = ref[j]
            state = step[:, LANES:].astype(f32) + dot(step[:, :LANES], state.astype(bf16))
        out_ref[j] = state.astype(bf16)


def final_kernel(share, core_ref, qp_ref, o_ref, pair_ref, mine_ref, other_ref, gate_ref, gain_ref, out_ref):
    heads, seq_rows, dim = qp_ref.shape
    core = core_ref[0]
    part = mine_ref.shape[0]
    for head in range(heads):
        start = mine_ref[head % part]
        if share:
            start = jnp.where(core == head // part, start, other_ref[head % part])
        pair = pair_ref[head]
        moved = pair[:, dim:].astype(f32) + dot(pair[:, :dim], start)
        start = jnp.where(core == 0, start.astype(f32), moved).astype(bf16)
        lanes = slice(head * dim, (head + 1) * dim)
        y = o_ref[head] + dot(qp_ref[head], start)
        scale = lax.rsqrt(jnp.mean(y * y, axis=-1, keepdims=True) + EPS)
        out_ref[:, lanes] = (y * scale * gain_ref[...] * gate_ref[:, lanes]).astype(bf16)


def call(kernel, name, out, operands, scalars=1, flops=0, scratch=(), limit=24):
    single = not isinstance(out, tuple)
    return pl.pallas_call(
        kernel,
        out_shape=out,
        in_specs=[whole(pltpu.SMEM)] * scalars + [whole()] * (len(operands) - scalars),
        out_specs=whole() if single else (whole(),) * len(out),
        scratch_shapes=scratch,
        cost_estimate=pl.CostEstimate(flops=flops, transcendentals=0, bytes_accessed=1 << 20),
        compiler_params=pltpu.CompilerParams(vmem_limit_bytes=limit << 20),
        name=name,
    )(*operands)


def per_device(hidden, w_qkv, w_gate, w_decay_beta, conv_weight, decay_rate, dt_bias, norm_gain):
    model_width = hidden.shape[1]
    heads = decay_rate.shape[0]
    dim = norm_gain.shape[0]
    columns = heads * dim
    blocks = lax.axis_size("tp")
    seq_count = lax.axis_size("seq")
    rows = hidden.shape[0]
    seq_rows = rows * blocks
    chunks = seq_rows // CHUNK
    me = jnp.full((1,), lax.axis_index("tp"), jnp.int32)
    core = jnp.full((1,), lax.axis_index("seq") % 2, jnp.int32)
    shape = jax.ShapeDtypeStruct

    w_three = w_qkv.transpose(1, 0, 2)
    small = jnp.pad(
        w_decay_beta.reshape(model_width, 2 * heads), ((0, 0), (0, LANES - 2 * heads))
    )
    taps = conv_weight.reshape(conv_weight.shape[0], 3 * heads, dim).transpose(1, 0, 2).astype(f32)
    vectors = jnp.pad(jnp.stack([-decay_rate, dt_bias]), ((0, 6), (0, LANES - heads)))

    early, late = gather_blocks(hidden, "tp")
    rim = rim_rows(hidden, RIM)
    early_rows = seq_rows - rows
    projected, rim, scalars = call(
        functools.partial(project_kernel, len(early)), "project",
        (
            shape((3, early_rows, columns), bf16),
            shape((3, RIM, columns), bf16),
            shape((early_rows, LANES), f32),
        ),
        [*early, rim, w_three, small], scalars=0, flops=PROJECT_FLOPS,
    )
    own, both, low, act, cols, rows_of = call(
        functools.partial(delta_kernel, heads, blocks), "delta",
        (
            shape((heads, dim, 2 * dim), bf16),
            shape((heads, chunks, CHUNK, 2 * dim), bf16),
            shape((heads, chunks - 1, dim, 2 * dim), bf16),
            shape((3 * heads, seq_rows, dim), bf16),
            shape((chunks, CHUNK, LANES), f32),
            shape((chunks, CHUNK, LANES), f32),
        ),
        [me, projected, rim, scalars, *late, w_three, small, taps, vectors],
        flops=DELTA_FLOPS, limit=32,
        scratch=[
            pltpu.VMEM((3 * heads, seq_rows + RIM, dim), f32),
            pltpu.VMEM((seq_rows, LANES), f32),
            pltpu.VMEM((CHUNK.bit_length() - 1, CHUNK, 2 * CHUNK), bf16),
            pltpu.VMEM((heads * chunks // 2, CHUNK, 2 * CHUNK), bf16),
            pltpu.VMEM((heads * chunks // 2, CHUNK, 2 * CHUNK), f32),
        ],
    )
    tokens = [*early, *late]
    reach, base, gate = call(
        functools.partial(reach_kernel, heads, blocks, len(tokens)), "reach",
        (
            shape((heads, seq_rows, dim), bf16),
            shape((heads, seq_rows, dim), f32),
            shape((seq_rows, columns), f32),
        ),
        [me, both, low, act, cols, rows_of, w_gate, *tokens], flops=REACH_FLOPS,
    )

    share = heads % 2 == 0
    part = heads // 2 if share else heads
    swap = [(i, i ^ 1) for i in range(seq_count)]
    other = lax.ppermute(own, "seq", swap)
    joined = call(
        functools.partial(pair_kernel, share), "pair",
        shape((part, dim, 2 * dim), bf16), [core, own, other], flops=SMALL_FLOPS, limit=4,
    )
    steps = []
    for distance in range(seq_count // 2 - 1, 0, -1):
        sent = joined if steps else joined[:, :, dim:]
        route = [(i, i + 2 * distance) for i in range(seq_count - 2 * distance)]
        steps.append(lax.ppermute(sent, "seq", route))
    state = call(
        fold_kernel, "fold", shape((part, dim, dim), bf16), steps,
        scalars=0, flops=SMALL_FLOPS, limit=4,
    )
    back = lax.ppermute(state, "seq", swap) if share else state
    return call(
        functools.partial(final_kernel, share), "final", shape((seq_rows, columns), bf16),
        [core, reach, base, other, state, back, gate, norm_gain.reshape(1, dim)],
        flops=SMALL_FLOPS, limit=12,
    )


def solution(mesh):
    return jax.shard_map(
        per_device,
        mesh=mesh,
        in_specs=(
            P(("seq", "tp"), None),
            P(None, None, "tp"),
            P(None, "tp"),
            P(None, None, "tp"),
            P(None, None, "tp"),
            P("tp"),
            P("tp"),
            P(),
        ),
        out_specs=P("seq", "tp"),
        check_vma=False,
    )
```

time: 88.2 us -> 83.3 us (0.944)
  the two profiles are of different devices: /device:TPU:0 before, /device:TPU:27 now
where the time goes in v2:
time: 83.3 us; the launch traced here: 82.6 us
  waiting for transfers between devices  22.6 us (27%)
  Pallas kernels  21.5 us (26%)
  starting transfers between devices  18.3 us (22%)
  local copies, waits for them, and re-layouts  18 us (22%)
  other arithmetic  2.05 us (2%)
    pallas_call x6, Pallas kernels, call(): pl.pallas_call(kernel, out_shape=out, in_specs=[whole(pltpu.SMEM)] * scal...  21.5 us
    unnamed x40, local copies, waits for them, and re-layouts  15.9 us
    ppermute x3, waiting for transfers between devices, per_device(): steps.append(lax.ppermute(sent, 'seq', route))  12.7 us
    ppermute x4, waiting for transfers between devices, swap(): return lax.ppermute(value, axis, [(i, i ^ step) for i in range(count)])  7.02 us
    ppermute x1, starting transfers between devices, per_device(): other = lax.ppermute(own, 'seq', swap)  5.04 us
    ppermute x4, starting transfers between devices, swap(): return lax.ppermute(value, axis, [(i, i ^ step) for i in range(count)])  4.6 us
    ppermute x3, starting transfers between devices, per_device(): steps.append(lax.ppermute(sent, 'seq', route))  4.06 us
    ppermute x4, starting transfers between devices, rim_rows(): part = lax.ppermute(tail, ('seq', 'tp'), route)  3.27 us
  transfers between devices with their start and end apart: 13, of which 5 were waited for; matrix products, arithmetic and copies ran while one was open for 4% of the time, Pallas kernels for 9%

profile of v2, /device:TPU:27, one launch (start us, length us, event | category | flops | bytes accessed | tf_op | source)
XLA Modules:
  0.0 82.6 jit_solution(13758109155786941766)
XLA Ops:
  2.3 1.3 %collective-permute-start.3 = (bf16[16,2048]{1,0:T(8,128)(2,1)S(1)}, bf16[16,2048]{1,0:T(8,128)(2,1)S(1)}, u32[]{:S(2)}, u32[]{:S(2)}) collective-permute-start(bf16[16,2048]{1,0:T(8,128)(2,1)S(1)} %slice.12), channel_id=1, source_target_pairs={{3,5},{7,9},{11,13},{15,17},{19,21},{23,25},{27,29}} | collective-permute-start | bytes 196616 | tf_op jit(solution)/shard_map/ppermute | solution.py:66
  4.2 1.3 %collective-permute-start.1 = (bf16[128,2048]{1,0:T(8,128)(2,1)}, bf16[128,2048]{1,0:T(8,128)(2,1)S(1)}, u32[]{:S(2)}, u32[]{:S(2)}) collective-permute-start(bf16[128,2048]{1,0:T(8,128)(2,1)} %refs_0_.3), channel_id=1, source_target_pairs={{0,2},{1,3},{2,0},{3,1},{4,6},{5,7},{6,4},{7,5},{8,10},{9,11},{10,... | collective-permute-start | bytes 1572872 | tf_op jit(solution)/shard_map/ppermute | solution.py:40
  9.1 1.5 %collective-permute-done.3 = bf16[16,2048]{1,0:T(8,128)(2,1)S(1)} collective-permute-done((bf16[16,2048]{1,0:T(8,128)(2,1)S(1)}, bf16[16,2048]{1,0:T(8,128)(2,1)S(1)}, u32[]{:S(2)}, u32[]{:S(2)}) %collective-permute-start.3) | collective-permute-done | bytes 65568 | tf_op jit(solution)/shard_map/ppermute | solution.py:66
  10.6 7.0 %collective-permute-done.1.refs_2_ = bf16[128,2048]{1,0:T(8,128)(2,1)S(1)} collective-permute-done((bf16[128,2048]{1,0:T(8,128)(2,1)}, bf16[128,2048]{1,0:T(8,128)(2,1)S(1)}, u32[]{:S(2)}, u32[]{:S(2)}) %collective-permute-start.1) | collective-permute-done | bytes 524320 | tf_op jit(solution)/shard_map/ppermute | solution.py:40
  17.6 1.4 %collective-permute-start.6 = (bf16[64,2048]{1,0:T(8,128)(2,1)S(1)}, bf16[64,2048]{1,0:T(8,128)(2,1)S(1)}, u32[]{:S(2)}, u32[]{:S(2)}) collective-permute-start(bf16[64,2048]{1,0:T(8,128)(2,1)S(1)} %slice.16), channel_id=1, source_target_pairs={{0,1},{1,0},{2,3},{3,2},{4,5},{5,4},{6,7},{7,6},{8,9},{9,8},{10,11... | collective-permute-start | bytes 786440 | tf_op jit(solution)/shard_map/ppermute | solution.py:40
  19.1 1.5 %collective-permute-start.7 = (bf16[64,2048]{1,0:T(8,128)(2,1)S(1)}, bf16[64,2048]{1,0:T(8,128)(2,1)S(1)}, u32[]{:S(2)}, u32[]{:S(2)}) collective-permute-start(bf16[64,2048]{1,0:T(8,128)(2,1)S(1)} %slice.17), channel_id=1, source_target_pairs={{0,2},{1,3},{2,0},{3,1},{4,6},{5,7},{6,4},{7,5},{8,10},{9,11},{10,... | collective-permute-start | bytes 786440 | tf_op jit(solution)/shard_map/ppermute | solution.py:40
  20.6 2.8 %copy-done.18 = bf16[2048,3,512]{2,0,1:T(8,128)(2,1)S(1)} copy-done((bf16[2048,3,512]{2,0,1:T(8,128)(2,1)S(1)}, bf16[2048,3,512]{2,0,1:T(8,128)(2,1)}, u32[]{:S(2)}) %copy-start.18) | copy-done | bytes 6291480
  23.4 3.6 %project.1 = (bf16[3,384,512]{2,1,0:T(8,128)(2,1)S(1)}, bf16[3,16,512]{2,1,0:T(8,128)(2,1)S(1)}, f32[384,128]{1,0:T(8,128)S(1)}) custom-call(bf16[128,2048]{1,0:T(8,128)(2,1)S(1)} %copy-done.7, bf16[128,2048]{1,0:T(8,128)(2,1)S(1)} %collective-permute-done.refs_1_, bf16[128,2048]{1,0:T(8,128)(2,1)S(1)} %collective-permute-done.1.refs_2_, ...), custom_call_target="tpu_custom_call" | custom-call | flops 3000000000 | bytes 1048576 | tf_op jit(solution)/shard_map/project/pallas_call | solution.py:341
  27.1 11.4 %delta.1 = (bf16[4,128,256]{2,1,0:T(8,128)(2,1)}, bf16[4,4,128,256]{3,2,1,0:T(8,128)(2,1)S(1)}, bf16[4,3,128,256]{3,2,1,0:T(8,128)(2,1)S(1)}, bf16[12,512,128]{2...) custom-call(s32[1]{0:T(128)} %bitcast.1.me_ref, ...), custom_call_target="tpu_custom_call" | custom-call | flops 3000000000 | bytes 1048576 | tf_op jit(solution)/shard_map/delta/pallas_call | solution.py:341
  38.5 1.2 %copy-done.1 = bf16[12,512,128]{2,1,0:T(8,128)(2,1)} copy-done((bf16[12,512,128]{2,1,0:T(8,128)(2,1)}, bf16[12,512,128]{2,1,0:T(8,128)(2,1)S(1)}, u32[]{:S(2)}) %copy-start.1) | copy-done | bytes 1572888
  42.9 5.0 %collective-permute-start.8 = (bf16[4,128,256]{2,1,0:T(8,128)(2,1)}, bf16[4,128,256]{2,1,0:T(8,128)(2,1)S(1)}, u32[]{:S(2)}, u32[]{:S(2)}) collective-permute-start(bf16[4,128,256]{2,1,0:T(8,128)(2,1)} %get-tuple-element.27.mine_ref), channel_id=1, source_target_pairs={{0,4},{4,0},{8,12},{12,8},{16,20},{20,16},{24,28},{28,24},{1,5},{5... | collective-permute-start | bytes 786440 | tf_op jit(solution)/shard_map/ppermute | solution.py:420
  48.0 1.4 %collective-permute-done.8.other_ref.pair_ref = bf16[4,128,256]{2,1,0:T(8,128)(2,1)S(1)} collective-permute-done((bf16[4,128,256]{2,1,0:T(8,128)(2,1)}, bf16[4,128,256]{2,1,0:T(8,128)(2,1)S(1)}, u32[]{:S(2)}, u32[]{:S(2)}) %collective-permute-start.8) | collective-permute-done | bytes 262176 | tf_op jit(solution)/shard_map/ppermute | solution.py:420
  49.3 1.1 %pair.1 = bf16[2,128,256]{2,1,0:T(8,128)(2,1)S(1)} custom-call(s32[1]{0:T(128)} %bitcast.core_ref, bf16[4,128,256]{2,1,0:T(8,128)(2,1)} %get-tuple-element.27.mine_ref, bf16[4,128,256]{2,1,0:T(8,128)(2,1)S(1)} %collective-permute-done.8.other_ref.pair_ref), custom_call_target="tpu_custom_call" | custom-call | flops 50000000 | bytes 1048576 | tf_op jit(solution)/shard_map/pair/pallas_call | solution.py:341
  50.5 1.3 %collective-permute-start.11 = (bf16[2,128,256]{2,1,0:T(8,128)(2,1)S(1)}, bf16[2,128,256]{2,1,0:T(8,128)(2,1)S(1)}, u32[]{:S(2)}, u32[]{:S(2)}) collective-permute-start(bf16[2,128,256]{2,1,0:T(8,128)(2,1)S(1)} %pair.1), channel_id=1, source_target_pairs={{0,8},{4,12},{8,16},{12,20},{16,24},{20,28},{1,9},{5,13},{9,17},{1... | collective-permute-start | bytes 393224 | tf_op jit(solution)/shard_map/ppermute | solution.py:429
  51.8 1.3 %collective-permute-start.10 = (bf16[2,128,256]{2,1,0:T(8,128)(2,1)S(1)}, bf16[2,128,256]{2,1,0:T(8,128)(2,1)S(1)}, u32[]{:S(2)}, u32[]{:S(2)}) collective-permute-start(bf16[2,128,256]{2,1,0:T(8,128)(2,1)S(1)} %pair.1), channel_id=1, source_target_pairs={{0,16},{4,20},{8,24},{12,28},{1,17},{5,21},{9,25},{13,29},{2,18},{... | collective-permute-start | bytes 393224 | tf_op jit(solution)/shard_map/ppermute | solution.py:429
  53.1 1.5 %collective-permute-start.9 = (bf16[2,128,128]{2,1,0:T(8,128)(2,1)S(1)}, bf16[2,128,128]{2,1,0:T(8,128)(2,1)S(1)}, u32[]{:S(2)}, u32[]{:S(2)}) collective-permute-start(bf16[2,128,128]{2,1,0:T(8,128)(2,1)S(1)} %slice.18), channel_id=1, source_target_pairs={{0,24},{4,28},{1,25},{5,29},{2,26},{6,30},{3,27},{7,31}} | collective-permute-start | bytes 196616 | tf_op jit(solution)/shard_map/ppermute | solution.py:429
  54.6 9.7 %collective-permute-done.9.refs_0_ = bf16[2,128,128]{2,1,0:T(8,128)(2,1)S(1)} collective-permute-done((bf16[2,128,128]{2,1,0:T(8,128)(2,1)S(1)}, bf16[2,128,128]{2,1,0:T(8,128)(2,1)S(1)}, u32[]{:S(2)}, u32[]{:S(2)}) %collective-permute-start.9) | collective-permute-done | bytes 65568 | tf_op jit(solution)/shard_map/ppermute | solution.py:429
  64.3 3.0 %collective-permute-done.10.refs_1_ = bf16[2,128,256]{2,1,0:T(8,128)(2,1)S(1)} collective-permute-done((bf16[2,128,256]{2,1,0:T(8,128)(2,1)S(1)}, bf16[2,128,256]{2,1,0:T(8,128)(2,1)S(1)}, u32[]{:S(2)}, u32[]{:S(2)}) %collective-permute-start.10) | collective-permute-done | bytes 131104 | tf_op jit(solution)/shard_map/ppermute | solution.py:429
  67.6 1.3 %collective-permute-start.12 = (bf16[2,128,128]{2,1,0:T(8,128)(2,1)S(1)}, bf16[2,128,128]{2,1,0:T(8,128)(2,1)S(1)}, u32[]{:S(2)}, u32[]{:S(2)}) collective-permute-start(bf16[2,128,128]{2,1,0:T(8,128)(2,1)S(1)} %fold.1.mine_ref), channel_id=1, source_target_pairs={{0,4},{4,0},{8,12},{12,8},{16,20},{20,16},{24,28},{28,24},{1,5},{5... | collective-permute-start | bytes 196616 | tf_op jit(solution)/shard_map/ppermute | solution.py:434
  68.9 1.4 %copy-done.2 = bf16[12,512,128]{2,1,0:T(8,128)(2,1)S(1)} copy-done((bf16[12,512,128]{2,1,0:T(8,128)(2,1)S(1)}, bf16[12,512,128]{2,1,0:T(8,128)(2,1)}, u32[]{:S(2)}) %copy-start.2) | copy-done | bytes 1572888
  70.3 1.2 %copy-done.4 = bf16[4,4,128,256]{3,2,1,0:T(8,128)(2,1)S(1)} copy-done((bf16[4,4,128,256]{3,2,1,0:T(8,128)(2,1)S(1)}, bf16[4,4,128,256]{3,2,1,0:T(8,128)(2,1)}, u32[]{:S(2)}) %copy-start.4) | copy-done | bytes 1048600
  71.5 1.1 %copy-done.6 = bf16[4,3,128,256]{3,2,1,0:T(8,128)(2,1)S(1)} copy-done((bf16[4,3,128,256]{3,2,1,0:T(8,128)(2,1)S(1)}, bf16[4,3,128,256]{3,2,1,0:T(8,128)(2,1)}, u32[]{:S(2)}) %copy-start.6) | copy-done | bytes 786456
  77.5 3.5 %reach.1 = (bf16[4,512,128]{2,1,0:T(8,128)(2,1)S(1)}, f32[4,512,128]{2,1,0:T(8,128)S(1)}, f32[512,512]{1,0:T(8,128)S(1)}) custom-call(s32[1]{0:T(128)} %bitcast.1.me_ref, bf16[4,4,128,256]{3,2,1,0:T(8,128)(2,1)S(1)} %copy-done.4, bf16[4,3,128,256]{3,2,1,0:T(8,128)(2,1)S(1)} %copy-done.6, bf16[12,512,128]{2,1,0:T(8,128)(2,1)S(1)} %copy-done.2, ...), custom_call_target="tpu_custom_call" | custom-call | flops 2000000000 | bytes 1048576 | tf_op jit(solution)/shard_map/reach/pallas_call | solution.py:341
  81.0 1.6 %final.1 = bf16[512,512]{1,0:T(8,128)(2,1)} custom-call(s32[1]{0:T(128)} %bitcast.core_ref, bf16[4,512,128]{2,1,0:T(8,128)(2,1)S(1)} %get-tuple-element.25.qp_ref, f32[4,512,128]{2,1,0:T(8,128)S(1)} %get-tuple-element.26.o_ref, bf16[4,128,256]{2,1,0:T(8,128)(2,1)S(1)} %collective-permute-done.8.other_ref.pair_ref, bf16[2,128,128]{2,1,0:T(8,128)(2,1)S(1)} %fold.1.mine_ref, ...), custom_call_target="tpu_custom_call" | custom-call | flops 50000000 | bytes 1048576 | tf_op jit(solution)/shard_map/final/pallas_call | solution.py:341
  (59 shorter events, 14.9 us)
Async XLA Ops:
  0.0 20.6 %copy-start.7 = (bf16[128,2048]{1,0:T(8,128)(2,1)S(1)}, bf16[128,2048]{1,0:T(8,128)(2,1)}, u32[]{:S(2)}) copy-start(bf16[128,2048]{1,0:T(8,128)(2,1)} %refs_0_.3) | copy-start | bytes 1572868
  0.9 7.1 %collective-permute-start.5 = (bf16[16,2048]{1,0:T(8,128)(2,1)S(1)}, bf16[16,2048]{1,0:T(8,128)(2,1)S(1)}, u32[]{:S(2)}, u32[]{:S(2)}) collective-permute-start(bf16[16,2048]{1,0:T(8,128)(2,1)S(1)} %slice.12), channel_id=1, source_target_pairs={{3,7},{7,11},{11,15},{15,19},{19,23},{23,27},{27,31}} | collective-permute-start | bytes 196616 | tf_op jit(solution)/shard_map/ppermute | solution.py:66
  1.6 7.5 %collective-permute-start.4 = (bf16[16,2048]{1,0:T(8,128)(2,1)S(1)}, bf16[16,2048]{1,0:T(8,128)(2,1)S(1)}, u32[]{:S(2)}, u32[]{:S(2)}) collective-permute-start(bf16[16,2048]{1,0:T(8,128)(2,1)S(1)} %slice.12), channel_id=1, source_target_pairs={{3,6},{7,10},{11,14},{15,18},{19,22},{23,26},{27,30}} | collective-permute-start | bytes 196616 | tf_op jit(solution)/shard_map/ppermute | solution.py:66
  2.3 8.3 %collective-permute-start.3 = (bf16[16,2048]{1,0:T(8,128)(2,1)S(1)}, bf16[16,2048]{1,0:T(8,128)(2,1)S(1)}, u32[]{:S(2)}, u32[]{:S(2)}) collective-permute-start(bf16[16,2048]{1,0:T(8,128)(2,1)S(1)} %slice.12), channel_id=1, source_target_pairs={{3,5},{7,9},{11,13},{15,17},{19,21},{23,25},{27,29}} | collective-permute-start | bytes 196616 | tf_op jit(solution)/shard_map/ppermute | solution.py:66
  3.6 7.0 %collective-permute-start.2 = (bf16[16,2048]{1,0:T(8,128)(2,1)S(1)}, bf16[16,2048]{1,0:T(8,128)(2,1)S(1)}, u32[]{:S(2)}, u32[]{:S(2)}) collective-permute-start(bf16[16,2048]{1,0:T(8,128)(2,1)S(1)} %slice.12), channel_id=1, source_target_pairs={{3,4},{7,8},{11,12},{15,16},{19,20},{23,24},{27,28}} | collective-permute-start | bytes 196616 | tf_op jit(solution)/shard_map/ppermute | solution.py:66
  4.2 13.4 %collective-permute-start.1 = (bf16[128,2048]{1,0:T(8,128)(2,1)}, bf16[128,2048]{1,0:T(8,128)(2,1)S(1)}, u32[]{:S(2)}, u32[]{:S(2)}) collective-permute-start(bf16[128,2048]{1,0:T(8,128)(2,1)} %refs_0_.3), channel_id=1, source_target_pairs={{0,2},{1,3},{2,0},{3,1},{4,6},{5,7},{6,4},{7,5},{8,10},{9,11},{10,... | collective-permute-start | bytes 1572872 | tf_op jit(solution)/shard_map/ppermute | solution.py:40
  8.1 11.0 %collective-permute-start = (bf16[128,2048]{1,0:T(8,128)(2,1)}, bf16[128,2048]{1,0:T(8,128)(2,1)S(1)}, u32[]{:S(2)}, u32[]{:S(2)}) collective-permute-start(bf16[128,2048]{1,0:T(8,128)(2,1)} %refs_0_.3), channel_id=1, source_target_pairs={{0,1},{1,0},{2,3},{3,2},{4,5},{5,4},{6,7},{7,6},{8,9},{9,8},{10,11... | collective-permute-start | bytes 1572872 | tf_op jit(solution)/shard_map/ppermute | solution.py:40
  17.6 9.4 %collective-permute-start.6 = (bf16[64,2048]{1,0:T(8,128)(2,1)S(1)}, bf16[64,2048]{1,0:T(8,128)(2,1)S(1)}, u32[]{:S(2)}, u32[]{:S(2)}) collective-permute-start(bf16[64,2048]{1,0:T(8,128)(2,1)S(1)} %slice.16), channel_id=1, source_target_pairs={{0,1},{1,0},{2,3},{3,2},{4,5},{5,4},{6,7},{7,6},{8,9},{9,8},{10,11... | collective-permute-start | bytes 786440 | tf_op jit(solution)/shard_map/ppermute | solution.py:40
  19.1 8.0 %collective-permute-start.7 = (bf16[64,2048]{1,0:T(8,128)(2,1)S(1)}, bf16[64,2048]{1,0:T(8,128)(2,1)S(1)}, u32[]{:S(2)}, u32[]{:S(2)}) collective-permute-start(bf16[64,2048]{1,0:T(8,128)(2,1)S(1)} %slice.17), channel_id=1, source_target_pairs={{0,2},{1,3},{2,0},{3,1},{4,6},{5,7},{6,4},{7,5},{8,10},{9,11},{10,... | collective-permute-start | bytes 786440 | tf_op jit(solution)/shard_map/ppermute | solution.py:40
  20.6 2.8 %copy-start.18 = (bf16[2048,3,512]{2,0,1:T(8,128)(2,1)S(1)}, bf16[2048,3,512]{2,0,1:T(8,128)(2,1)}, u32[]{:S(2)}) copy-start(bf16[2048,3,512]{2,0,1:T(8,128)(2,1)} %param.9) | copy-start | bytes 18874372
  23.4 3.7 %copy-start.19 = (bf16[2048,3,512]{2,0,1:T(8,128)(2,1)S(1)}, bf16[2048,3,512]{2,0,1:T(8,128)(2,1)}, u32[]{:S(2)}) copy-start(bf16[2048,3,512]{2,0,1:T(8,128)(2,1)} %param.9) | copy-start | bytes 18874372
  27.0 11.4 %copy-start.9 = (bf16[64,2048]{1,0:T(8,128)(2,1)}, bf16[64,2048]{1,0:T(8,128)(2,1)S(1)}, u32[]{:S(2)}) copy-start(bf16[64,2048]{1,0:T(8,128)(2,1)S(1)} %collective-permute-done.6.late0_ref.refs_3_) | copy-start | bytes 786436
  27.1 11.4 %copy-start.11 = (bf16[64,2048]{1,0:T(8,128)(2,1)}, bf16[64,2048]{1,0:T(8,128)(2,1)S(1)}, u32[]{:S(2)}) copy-start(bf16[64,2048]{1,0:T(8,128)(2,1)S(1)} %collective-permute-done.7.late1_ref.refs_4_) | copy-start | bytes 786436
  27.1 41.8 %copy-start = (bf16[2048,512]{1,0:T(8,128)(2,1)S(1)}, bf16[2048,512]{1,0:T(8,128)(2,1)}, u32[]{:S(2)}) copy-start(bf16[2048,512]{1,0:T(8,128)(2,1)} %w_ref.1) | copy-start | bytes 6291460
  38.5 1.2 %copy-start.1 = (bf16[12,512,128]{2,1,0:T(8,128)(2,1)}, bf16[12,512,128]{2,1,0:T(8,128)(2,1)S(1)}, u32[]{:S(2)}) copy-start(bf16[12,512,128]{2,1,0:T(8,128)(2,1)S(1)} %get-tuple-element.22.act) | copy-start | bytes 4718596
  42.9 6.4 %collective-permute-start.8 = (bf16[4,128,256]{2,1,0:T(8,128)(2,1)}, bf16[4,128,256]{2,1,0:T(8,128)(2,1)S(1)}, u32[]{:S(2)}, u32[]{:S(2)}) collective-permute-start(bf16[4,128,256]{2,1,0:T(8,128)(2,1)} %get-tuple-element.27.mine_ref), channel_id=1, source_target_pairs={{0,4},{4,0},{8,12},{12,8},{16,20},{20,16},{24,28},{28,24},{1,5},{5... | collective-permute-start | bytes 786440 | tf_op jit(solution)/shard_map/ppermute | solution.py:420
  50.5 13.8 %collective-permute-start.11 = (bf16[2,128,256]{2,1,0:T(8,128)(2,1)S(1)}, bf16[2,128,256]{2,1,0:T(8,128)(2,1)S(1)}, u32[]{:S(2)}, u32[]{:S(2)}) collective-permute-start(bf16[2,128,256]{2,1,0:T(8,128)(2,1)S(1)} %pair.1), channel_id=1, source_target_pairs={{0,8},{4,12},{8,16},{12,20},{16,24},{20,28},{1,9},{5,13},{9,17},{1... | collective-permute-start | bytes 393224 | tf_op jit(solution)/shard_map/ppermute | solution.py:429
  51.8 15.5 %collective-permute-start.10 = (bf16[2,128,256]{2,1,0:T(8,128)(2,1)S(1)}, bf16[2,128,256]{2,1,0:T(8,128)(2,1)S(1)}, u32[]{:S(2)}, u32[]{:S(2)}) collective-permute-start(bf16[2,128,256]{2,1,0:T(8,128)(2,1)S(1)} %pair.1), channel_id=1, source_target_pairs={{0,16},{4,20},{8,24},{12,28},{1,17},{5,21},{9,25},{13,29},{2,18},{... | collective-permute-start | bytes 393224 | tf_op jit(solution)/shard_map/ppermute | solution.py:429
  53.1 11.2 %collective-permute-start.9 = (bf16[2,128,128]{2,1,0:T(8,128)(2,1)S(1)}, bf16[2,128,128]{2,1,0:T(8,128)(2,1)S(1)}, u32[]{:S(2)}, u32[]{:S(2)}) collective-permute-start(bf16[2,128,128]{2,1,0:T(8,128)(2,1)S(1)} %slice.18), channel_id=1, source_target_pairs={{0,24},{4,28},{1,25},{5,29},{2,26},{6,30},{3,27},{7,31}} | collective-permute-start | bytes 196616 | tf_op jit(solution)/shard_map/ppermute | solution.py:429
  67.6 13.5 %collective-permute-start.12 = (bf16[2,128,128]{2,1,0:T(8,128)(2,1)S(1)}, bf16[2,128,128]{2,1,0:T(8,128)(2,1)S(1)}, u32[]{:S(2)}, u32[]{:S(2)}) collective-permute-start(bf16[2,128,128]{2,1,0:T(8,128)(2,1)S(1)} %fold.1.mine_ref), channel_id=1, source_target_pairs={{0,4},{4,0},{8,12},{12,8},{16,20},{20,16},{24,28},{28,24},{1,5},{5... | collective-permute-start | bytes 196616 | tf_op jit(solution)/shard_map/ppermute | solution.py:434
  68.8 1.4 %copy-start.2 = (bf16[12,512,128]{2,1,0:T(8,128)(2,1)S(1)}, bf16[12,512,128]{2,1,0:T(8,128)(2,1)}, u32[]{:S(2)}) copy-start(bf16[12,512,128]{2,1,0:T(8,128)(2,1)} %copy-done.1) | copy-start | bytes 4718596
  70.3 1.2 %copy-start.4 = (bf16[4,4,128,256]{3,2,1,0:T(8,128)(2,1)S(1)}, bf16[4,4,128,256]{3,2,1,0:T(8,128)(2,1)}, u32[]{:S(2)}) copy-start(bf16[4,4,128,256]{3,2,1,0:T(8,128)(2,1)} %copy-done.3) | copy-start | bytes 3145732
  71.5 1.1 %copy-start.6 = (bf16[4,3,128,256]{3,2,1,0:T(8,128)(2,1)S(1)}, bf16[4,3,128,256]{3,2,1,0:T(8,128)(2,1)}, u32[]{:S(2)}) copy-start(bf16[4,3,128,256]{3,2,1,0:T(8,128)(2,1)} %copy-done.5) | copy-start | bytes 2359300
  77.5 3.6 %copy-start.17 = (f32[128]{0:T(128)S(1)}, f32[128]{0:T(128)}, u32[]{:S(2)}) copy-start(f32[128]{0:T(128)} %param.15) | copy-start | bytes 1540
  (9 other events, 8.1 us)

commit v3 on v2

--- a/solution.py
+++ b/solution.py
@@ -7,6 +7,7 @@
 from jax.experimental import pallas as pl
 from jax.experimental.pallas import tpu as pltpu
 from jax.sharding import PartitionSpec as P
+
 
 CHUNK = 128
 LANES = 128
@@ -52,7 +53,7 @@
         halves.append(part)
     early = [found[m] if m in found else (halves[0][m], halves[1][m]) for m in range(count - 1)]
     flat = []
-    for item in early:
+    for item in early[1:]:
         flat.extend(item if isinstance(item, tuple) else (item,))
     return flat, [halves[0][count - 1], halves[1][count - 1]]
 
@@ -72,6 +73,22 @@
     return x / (1.0 + jnp.exp(-x))
 
 
+def project_kernel(count, *refs):
+    blocks = refs[:count]
+    w_ref, gate_w_ref, small_ref = refs[count:count + 3]
+    p_ref, gate_ref, sc_ref = refs[count + 3:count + 6]
+    rows = sc_ref.shape[0]
+    tokens = jnp.concatenate([ref[...] for ref in blocks], axis=0)
+    sc_ref[...] = dot(tokens, small_ref[...])[:rows]
+    gate_ref[...] = silu(dot(tokens, gate_w_ref[...])[:rows])
+
+    def one(branch, carry):
+        p_ref[branch] = dot(tokens, w_ref[branch]).astype(bf16)
+        return carry
+
+    lax.fori_loop(0, w_ref.shape[0], one, 0)
+
+
 def block_diagonal(left, right):
     hole = jnp.zeros_like(left)
     return jnp.concatenate(
@@ -83,65 +100,42 @@
     return jnp.concatenate([left, right], axis=1)
 
 
-def project_kernel(count, *refs):
-    blocks, rim_ref, w_ref, small_ref = refs[:count], *refs[count:count + 3]
-    p_ref, rim_out, sc_ref = refs[count + 3:]
-    rows = p_ref.shape[1]
-    tokens = jnp.concatenate([ref[...] for ref in blocks] + [rim_ref[...]], axis=0)
-    sc_ref[...] = dot(tokens, small_ref[...])[:rows]
-
-    def one(branch, carry):
-        out = dot(tokens, w_ref[branch]).astype(bf16)
-        p_ref[branch] = out[:rows]
-        rim_out[branch] = out[rows:]
-        return carry
-
-    lax.fori_loop(0, w_ref.shape[0], one, 0)
-
-
-def block_diagonal(left, right):
-    hole = jnp.zeros_like(left)
-    return jnp.concatenate(
-        [jnp.concatenate([left, hole], axis=1), jnp.concatenate([hole, right], axis=1)], axis=0
-    )
-
-
-def beside(left, right):
-    return jnp.concatenate([left, right], axis=1)
-
-
 def grid_index(shape):
     return lax.broadcasted_iota(jnp.int32, shape, 0), lax.broadcasted_iota(jnp.int32, shape, 1)
 
 
 def delta_kernel(
-    heads, blocks, me_ref, p_ref, rim_ref, sc_ref, late0_ref, late1_ref, w_ref, small_ref,
-    taps_ref, vec_ref, x_ref, both_ref, low_ref, act, cols, rows_of,
+    heads, blocks, own_ref, own_sc_ref, p_ref, sc_ref, late0_ref, late1_ref, w_ref,
+    gate_w_ref, small_ref, taps_ref, vec_ref, x_ref, both_ref, low_ref, act, cols, rows_of, gate_ref,
     xp, sc, masks, mixes, solves,
 ):
     seq_rows = act.shape[1]
     rows = seq_rows // blocks
     chunks = seq_rows // CHUNK
     taps = taps_ref.shape[1]
-    me = me_ref[0]
+    me = lax.axis_index("tp")
 
     def place(m, offset=0):
         return pl.multiple_of(offset + lax.bitwise_xor(me, m) * rows, 8)
 
     late = jnp.concatenate([late0_ref[...], late1_ref[...]], axis=0)
     sc[pl.ds(place(blocks - 1), rows)] = dot(late, small_ref[...])
-    for m in range(blocks - 1):
-        sc[pl.ds(place(m), rows)] = sc_ref[m * rows:(m + 1) * rows]
+    gate_ref[...] = silu(dot(late, gate_w_ref[...]))
+    sc[pl.ds(place(0), rows)] = own_sc_ref[...]
+    for m in range(1, blocks - 1):
+        sc[pl.ds(place(m), rows)] = sc_ref[(m - 1) * rows:m * rows]
 
     def fill(branch, carry):
         made = dot(late, w_ref[branch]).astype(bf16).astype(f32)
         for head in range(heads):
             tile = branch * heads + head
             lanes = slice(head * LANES, (head + 1) * LANES)
-            xp[tile, :RIM] = rim_ref[branch, :, lanes].astype(f32)
+            xp[tile, :RIM] = p_ref[branch, (blocks - 2) * rows:, lanes].astype(f32)
+            xp[tile, pl.ds(place(0, RIM), rows)] = own_ref[branch, :, lanes].astype(f32)
             xp[tile, pl.ds(place(blocks - 1, RIM), rows)] = made[:, lanes]
-            for m in range(blocks - 1):
-                xp[tile, pl.ds(place(m, RIM), rows)] = p_ref[branch, m * rows:(m + 1) * rows, lanes].astype(f32)
+            for m in range(1, blocks - 1):
+                block = p_ref[branch, (m - 1) * rows:m * rows, lanes]
+                xp[tile, pl.ds(place(m, RIM), rows)] = block.astype(f32)
         return carry
 
     lax.fori_loop(0, 3, fill, 0)
@@ -254,19 +248,8 @@
         x_ref[head] = runs[head].astype(bf16)
 
 
-def reach_kernel(
-    heads, blocks, count, me_ref, both_ref, low_ref, act, cols, rows_of, w_ref, *refs
-):
-    tokens_refs, (qp_ref, o_ref, gate_ref) = refs[:count], refs[count:]
-    seq_rows = act.shape[1]
-    rows = seq_rows // blocks
-    chunks = seq_rows // CHUNK
-    me = me_ref[0]
-    tokens = jnp.concatenate([ref[...] for ref in tokens_refs], axis=0)
-    gate = silu(dot(tokens, w_ref[...]))
-    for m in range(blocks):
-        at = pl.multiple_of(lax.bitwise_xor(me, m) * rows, 8)
-        gate_ref[pl.ds(at, rows)] = gate[m * rows:(m + 1) * rows]
+def reach_kernel(heads, both_ref, low_ref, act, cols, rows_of, qp_ref, o_ref):
+    chunks = act.shape[1] // CHUNK
     ri, ci = grid_index((CHUNK, CHUNK))
     upto = ri >= ci
     for head in range(heads):
@@ -296,9 +279,8 @@
                 o_ref[head, at] = inner[:, LANES:] + ahead[:, LANES:]
 
 
-def pair_kernel(share, core_ref, mine_ref, other_ref, out_ref):
-    core = core_ref[0]
-    heads = mine_ref.shape[0]
+def pair_kernel(share, mine_ref, other_ref, out_ref):
+    core = lax.axis_index("seq") & 1
     for j in range(out_ref.shape[0]):
         head = core * out_ref.shape[0] + j if share else j
         mine, other = mine_ref[head], other_ref[head]
@@ -309,19 +291,50 @@
         out_ref[j, :, LANES:] = (both[:, LANES:] + second[:, LANES:].astype(f32)).astype(bf16)
 
 
-def fold_kernel(*refs):
+def climb_kernel(bit, inside_ref, block_ref, sent_ref, inside_out, block_out):
+    upper = (lax.axis_index("seq") >> (bit + 1)) & 1
+    for j in range(block_ref.shape[0]):
+        sent = sent_ref[j]
+        for ref, out in ((inside_ref, inside_out), (block_ref, block_out)):
+            mine = ref[j]
+            both = dot(mine[:, :LANES], sent)
+            left = jnp.where(upper == 1, both[:, :LANES], mine[:, :LANES].astype(f32))
+            right = mine[:, LANES:].astype(f32) + both[:, LANES:]
+            out[j] = jnp.concatenate([left, right], axis=1).astype(bf16)
+
+
+def first_kernel(block_ref, sent_ref, inside_out, block_out):
+    upper = (lax.axis_index("seq") >> 1) & 1
+    ri, ci = grid_index((LANES, LANES))
+    eye = jnp.where(ri == ci, 1.0, 0.0)
+    for j in range(block_ref.shape[0]):
+        sent, mine = sent_ref[j], block_ref[j]
+        both = dot(mine[:, :LANES], sent)
+        left = jnp.where(upper == 1, both[:, :LANES], mine[:, :LANES].astype(f32))
+        right = mine[:, LANES:].astype(f32) + both[:, LANES:]
+        block_out[j] = jnp.concatenate([left, right], axis=1).astype(bf16)
+        inside = jnp.where(upper == 1, sent[:, :LANES].astype(f32), eye)
+        inside_out[j] = jnp.concatenate([inside.astype(bf16), sent[:, LANES:]], axis=1)
+
+
+def fold_kernel(inside_ref, *refs):
     out_ref = refs[-1]
     for j in range(out_ref.shape[0]):
-        state = refs[0][j].astype(f32)
+        state = refs[0][j]
         for ref in refs[1:-1]:
-            step = ref[j]
-            state = step[:, LANES:].astype(f32) + dot(step[:, :LANES], state.astype(bf16))
+            state = state + ref[j]
+        inside = inside_ref[j]
+        state = inside[:, LANES:].astype(f32) + dot(inside[:, :LANES], state)
         out_ref[j] = state.astype(bf16)
 
 
-def final_kernel(share, core_ref, qp_ref, o_ref, pair_ref, mine_ref, other_ref, gate_ref, gain_ref, out_ref):
+def final_kernel(
+    share, blocks, qp_ref, o_ref, pair_ref, mine_ref, other_ref,
+    own_gate_ref, gate_ref, late_gate_ref, gain_ref, out_ref,
+):
     heads, seq_rows, dim = qp_ref.shape
-    core = core_ref[0]
+    rows = seq_rows // blocks
+    core, me = lax.axis_index("seq") & 1, lax.axis_index("tp")
     part = mine_ref.shape[0]
     for head in range(heads):
         start = mine_ref[head % part]
@@ -331,22 +344,29 @@
         moved = pair[:, dim:].astype(f32) + dot(pair[:, :dim], start)
         start = jnp.where(core == 0, start.astype(f32), moved).astype(bf16)
         lanes = slice(head * dim, (head + 1) * dim)
-        y = o_ref[head] + dot(qp_ref[head], start)
-        scale = lax.rsqrt(jnp.mean(y * y, axis=-1, keepdims=True) + EPS)
-        out_ref[:, lanes] = (y * scale * gain_ref[...] * gate_ref[:, lanes]).astype(bf16)
-
-
-def call(kernel, name, out, operands, scalars=1, flops=0, scratch=(), limit=24):
+        for m in range(blocks):
+            if m == 0:
+                gate = own_gate_ref[:, lanes]
+            elif m < blocks - 1:
+                gate = gate_ref[(m - 1) * rows:m * rows, lanes]
+            else:
+                gate = late_gate_ref[:, lanes]
+            at = pl.ds(pl.multiple_of(lax.bitwise_xor(me, m) * rows, 8), rows)
+            y = o_ref[head, at] + dot(qp_ref[head, at], start)
+            scale = lax.rsqrt(jnp.mean(y * y, axis=-1, keepdims=True) + EPS)
+            out_ref[at, lanes] = (y * scale * gain_ref[...] * gate).astype(bf16)
+
+
+def call(kernel, out, operands, flops=0, scratch=(), limit=24):
     single = not isinstance(out, tuple)
     return pl.pallas_call(
         kernel,
         out_shape=out,
-        in_specs=[whole(pltpu.SMEM)] * scalars + [whole()] * (len(operands) - scalars),
+        in_specs=[whole()] * len(operands),
         out_specs=whole() if single else (whole(),) * len(out),
         scratch_shapes=scratch,
         cost_estimate=pl.CostEstimate(flops=flops, transcendentals=0, bytes_accessed=1 << 20),
         compiler_params=pltpu.CompilerParams(vmem_limit_bytes=limit << 20),
-        name=name,
     )(*operands)
 
 
@@ -360,8 +380,6 @@
     rows = hidden.shape[0]
     seq_rows = rows * blocks
     chunks = seq_rows // CHUNK
-    me = jnp.full((1,), lax.axis_index("tp"), jnp.int32)
-    core = jnp.full((1,), lax.axis_index("seq") % 2, jnp.int32)
     shape = jax.ShapeDtypeStruct
 
     w_three = w_qkv.transpose(1, 0, 2)
@@ -373,18 +391,23 @@
 
     early, late = gather_blocks(hidden, "tp")
     rim = rim_rows(hidden, RIM)
-    early_rows = seq_rows - rows
-    projected, rim, scalars = call(
-        functools.partial(project_kernel, len(early)), "project",
-        (
-            shape((3, early_rows, columns), bf16),
-            shape((3, RIM, columns), bf16),
-            shape((early_rows, LANES), f32),
-        ),
-        [*early, rim, w_three, small], scalars=0, flops=PROJECT_FLOPS,
-    )
-    own, both, low, act, cols, rows_of = call(
-        functools.partial(delta_kernel, heads, blocks), "delta",
+    weights = [w_three, w_gate, small]
+
+    def project(tokens, count, extra=0):
+        return call(
+            functools.partial(project_kernel, len(tokens)),
+            (
+                shape((3, count + extra, columns), bf16),
+                shape((count, columns), f32),
+                shape((count, LANES), f32),
+            ),
+            [*tokens, *weights], flops=PROJECT_FLOPS, limit=20,
+        )
+
+    own_p, own_gate, own_sc = project([hidden], rows)
+    mid_p, mid_gate, mid_sc = project([*early, rim], seq_rows - 2 * rows, RIM)
+    own, both, low, act, cols, rows_of, late_gate = call(
+        functools.partial(delta_kernel, heads, blocks),
         (
             shape((heads, dim, 2 * dim), bf16),
             shape((heads, chunks, CHUNK, 2 * dim), bf16),
@@ -392,8 +415,9 @@
             shape((3 * heads, seq_rows, dim), bf16),
             shape((chunks, CHUNK, LANES), f32),
             shape((chunks, CHUNK, LANES), f32),
+            shape((rows, columns), f32),
         ),
-        [me, projected, rim, scalars, *late, w_three, small, taps, vectors],
+        [own_p, own_sc, mid_p, mid_sc, *late, *weights, taps, vectors],
         flops=DELTA_FLOPS, limit=32,
         scratch=[
             pltpu.VMEM((3 * heads, seq_rows + RIM, dim), f32),
@@ -403,38 +427,50 @@
             pltpu.VMEM((heads * chunks // 2, CHUNK, 2 * CHUNK), f32),
         ],
     )
-    tokens = [*early, *late]
-    reach, base, gate = call(
-        functools.partial(reach_kernel, heads, blocks, len(tokens)), "reach",
-        (
-            shape((heads, seq_rows, dim), bf16),
-            shape((heads, seq_rows, dim), f32),
-            shape((seq_rows, columns), f32),
-        ),
-        [me, both, low, act, cols, rows_of, w_gate, *tokens], flops=REACH_FLOPS,
+    reach, base = call(
+        functools.partial(reach_kernel, heads),
+        (shape((heads, seq_rows, dim), bf16), shape((heads, seq_rows, dim), f32)),
+        [both, low, act, cols, rows_of], flops=REACH_FLOPS, limit=12,
     )
 
     share = heads % 2 == 0
     part = heads // 2 if share else heads
     swap = [(i, i ^ 1) for i in range(seq_count)]
     other = lax.ppermute(own, "seq", swap)
-    joined = call(
-        functools.partial(pair_kernel, share), "pair",
-        shape((part, dim, 2 * dim), bf16), [core, own, other], flops=SMALL_FLOPS, limit=4,
-    )
-    steps = []
-    for distance in range(seq_count // 2 - 1, 0, -1):
-        sent = joined if steps else joined[:, :, dim:]
-        route = [(i, i + 2 * distance) for i in range(seq_count - 2 * distance)]
-        steps.append(lax.ppermute(sent, "seq", route))
+    block = call(
+        functools.partial(pair_kernel, share),
+        shape((part, dim, 2 * dim), bf16), [own, other], flops=SMALL_FLOPS, limit=4,
+    )
+    chips = seq_count // 2
+    levels = chips.bit_length() - 1
+    inside = None
+    for level in range(levels):
+        size = 1 << level
+        sent = block if level < levels - 1 or level == 0 else block[:, :, dim:]
+        parts = []
+        for target in range(size):
+            route = []
+            for top in range(size - 1, chips, 2 * size):
+                for c in range(2):
+                    route.append((2 * top + c, 2 * (top + 1 + target) + c))
+            parts.append(lax.ppermute(sent, "seq", route))
+        if level == levels - 1 and level > 0:
+            break
+        sent = sum(parts[1:], parts[0])
+        kernel, operands = first_kernel, [block, sent]
+        if level > 0:
+            kernel, operands = functools.partial(climb_kernel, level), [inside, block, sent]
+        inside, block = call(
+            kernel, (shape(block.shape, bf16),) * 2, operands, flops=SMALL_FLOPS, limit=4,
+        )
     state = call(
-        fold_kernel, "fold", shape((part, dim, dim), bf16), steps,
-        scalars=0, flops=SMALL_FLOPS, limit=4,
+        fold_kernel, shape((part, dim, dim), bf16), [inside, *parts],
+        flops=SMALL_FLOPS, limit=4,
     )
     back = lax.ppermute(state, "seq", swap) if share else state
     return call(
-        functools.partial(final_kernel, share), "final", shape((seq_rows, columns), bf16),
-        [core, reach, base, other, state, back, gate, norm_gain.reshape(1, dim)],
+        functools.partial(final_kernel, share, blocks), shape((seq_rows, columns), bf16),
+        [reach, base, other, state, back, own_gate, mid_gate, late_gate, norm_gain.reshape(1, dim)],
         flops=SMALL_FLOPS, limit=12,
     )
 

time: 83.3 us -> 73.8 us (0.89)
  the two profiles are of different devices: /device:TPU:27 before, /device:TPU:21 now
where the time goes in v3:
time: 73.8 us; the launch traced here: 73.3 us
  waiting for transfers between devices  29.3 us (40%)
  Pallas kernels  21 us (28%)
  starting transfers between devices  14.6 us (20%)
  local copies, waits for them, and re-layouts  7.46 us (10%)
  other arithmetic  0.74 us (1%)
    pallas_call x8, Pallas kernels, call(): pl.pallas_call(kernel, out_shape=out, in_specs=[whole()] * len(operands),...  21 us
    ppermute x4, waiting for transfers between devices, swap(): return lax.ppermute(value, axis, [(i, i ^ step) for i in range(count)])  18.7 us
    ppermute x3, waiting for transfers between devices, per_device(): parts.append(lax.ppermute(sent, 'seq', route))  9.4 us
    ppermute x4, starting transfers between devices, swap(): return lax.ppermute(value, axis, [(i, i ^ step) for i in range(count)])  5.86 us
    unnamed x16, local copies, waits for them, and re-layouts  5.43 us
    ppermute x3, starting transfers between devices, per_device(): parts.append(lax.ppermute(sent, 'seq', route))  3.43 us
    ppermute x4, starting transfers between devices, rim_rows(): part = lax.ppermute(tail, ('seq', 'tp'), route)  3.27 us
    ppermute x1, starting transfers between devices, per_device(): back = lax.ppermute(state, 'seq', swap) if share else state  1.56 us
  transfers between devices with their start and end apart: 13, of which 7 were waited for; matrix products, arithmetic and copies ran while one was open for 3% of the time, Pallas kernels for 11%

profile of v3, /device:TPU:21, one launch (start us, length us, event | category | flops | bytes accessed | tf_op | source)
XLA Modules:
  0.0 73.3 jit_solution(6087550562729848647)
XLA Ops:
  0.0 0.8 %slice.12 = bf16[16,2048]{1,0:T(8,128)(2,1)S(1)} slice(bf16[128,2048]{1,0:T(8,128)(2,1)} %refs_0_.1), slice={[112:128], [0:2048]} | slice | bytes 131072 | tf_op jit(solution)/shard_map/slice | solution.py:63
  1.5 1.3 %collective-permute-start.4 = (bf16[16,2048]{1,0:T(8,128)(2,1)S(1)}, bf16[16,2048]{1,0:T(8,128)(2,1)S(1)}, u32[]{:S(2)}, u32[]{:S(2)}) collective-permute-start(bf16[16,2048]{1,0:T(8,128)(2,1)S(1)} %slice.12), channel_id=1, source_target_pairs={{3,6},{7,10},{11,14},{15,18},{19,22},{23,26},{27,30}} | collective-permute-start | bytes 196616 | tf_op jit(solution)/shard_map/ppermute | solution.py:67
  2.8 0.7 collective-permute-start.3
  4.2 5.6 %collective-permute-start = (bf16[128,2048]{1,0:T(8,128)(2,1)}, bf16[128,2048]{1,0:T(8,128)(2,1)S(1)}, u32[]{:S(2)}, u32[]{:S(2)}) collective-permute-start(bf16[128,2048]{1,0:T(8,128)(2,1)} %refs_0_.1), channel_id=1, source_target_pairs={{0,1},{1,0},{2,3},{3,2},{4,5},{5,4},{6,7},{7,6},{8,9},{9,8},{10,11... | collective-permute-start | bytes 1572872 | tf_op jit(solution)/shard_map/ppermute | solution.py:41
  9.8 0.7 convert_bitcast_fusion.taps_ref
  10.5 0.8 %reshape.9 = bf16[2048,8]{0,1:T(8,128)(2,1)S(1)} reshape(bf16[2048,2,4]{0,2,1:T(4,128)(2,1)} %param.11) | data formatting | bytes 65536 | tf_op jit(solution)/shard_map/reshape | solution.py:387
  11.7 1.0 %copy-done = bf16[128,2048]{1,0:T(8,128)(2,1)S(1)} copy-done((bf16[128,2048]{1,0:T(8,128)(2,1)S(1)}, bf16[128,2048]{1,0:T(8,128)(2,1)}, u32[]{:S(2)}) %copy-start) | copy-done | bytes 524312
  12.7 2.8 %copy-done.2 = bf16[2048,3,512]{2,0,1:T(8,128)(2,1)S(1)} copy-done((bf16[2048,3,512]{2,0,1:T(8,128)(2,1)S(1)}, bf16[2048,3,512]{2,0,1:T(8,128)(2,1)}, u32[]{:S(2)}) %copy-start.2) | copy-done | bytes 6291480
  15.5 1.6 %copy-done.4 = bf16[2048,512]{1,0:T(8,128)(2,1)S(1)} copy-done((bf16[2048,512]{1,0:T(8,128)(2,1)S(1)}, bf16[2048,512]{1,0:T(8,128)(2,1)}, u32[]{:S(2)}) %copy-start.4) | copy-done | bytes 2097176
  17.1 1.9 %shard_map.82 = (bf16[3,128,512]{2,1,0:T(8,128)(2,1)S(1)}, f32[128,512]{1,0:T(8,128)S(1)}, f32[128,128]{1,0:T(8,128)S(1)}) custom-call(bf16[128,2048]{1,0:T(8,128)(2,1)S(1)} %copy-done, bf16[3,2048,512]{2,1,0:T(8,128)(2,1)S(1)} %bitcast.12, bf16[2048,512]{1,0:T(8,128)(2,1)S(1)} %copy-done.4, bf16[2048,128]{1,0:T(8,128)(2,1)S(1)} %pad.8.refs_3_.refs_5_.small_ref), custom_call_target="tpu_custom_call" | custom-call | flops 3000000000 | bytes 1048576 | tf_op jit(solution)/shard_map/pallas_call | solution.py:362
  19.2 3.3 %collective-permute-done.refs_0_ = bf16[128,2048]{1,0:T(8,128)(2,1)S(1)} collective-permute-done((bf16[128,2048]{1,0:T(8,128)(2,1)}, bf16[128,2048]{1,0:T(8,128)(2,1)S(1)}, u32[]{:S(2)}, u32[]{:S(2)}) %collective-permute-start) | collective-permute-done | bytes 524320 | tf_op jit(solution)/shard_map/ppermute | solution.py:41
  22.7 10.4 %collective-permute-done.1.refs_1_ = bf16[128,2048]{1,0:T(8,128)(2,1)S(1)} collective-permute-done((bf16[128,2048]{1,0:T(8,128)(2,1)S(1)}, bf16[128,2048]{1,0:T(8,128)(2,1)S(1)}, u32[]{:S(2)}, u32[]{:S(2)}) %collective-permute-start.1) | collective-permute-done | bytes 524320 | tf_op jit(solution)/shard_map/ppermute | solution.py:41
  33.2 3.3 %shard_map.83 = (bf16[3,272,512]{2,1,0:T(8,128)(2,1)S(1)}, f32[256,512]{1,0:T(8,128)S(1)}, f32[256,128]{1,0:T(8,128)S(1)}) custom-call(bf16[128,2048]{1,0:T(8,128)(2,1)S(1)} %collective-permute-done.refs_0_, bf16[128,2048]{1,0:T(8,128)(2,1)S(1)} %collective-permute-done.1.refs_1_, bf16[16,2048]{1,0:T(8,128)(2,1)S(1)} %add_add_fusion.refs_2_, ...), custom_call_target="tpu_custom_call" | custom-call | flops 3000000000 | bytes 1048576 | tf_op jit(solution)/shard_map/pallas_call | solution.py:362
  36.6 1.7 %collective-permute-done.7.late1_ref = bf16[64,2048]{1,0:T(8,128)(2,1)S(1)} collective-permute-done((bf16[64,2048]{1,0:T(8,128)(2,1)S(1)}, bf16[64,2048]{1,0:T(8,128)(2,1)S(1)}, u32[]{:S(2)}, u32[]{:S(2)}) %collective-permute-start.7) | collective-permute-done | bytes 262176 | tf_op jit(solution)/shard_map/ppermute | solution.py:41
  38.3 3.2 %collective-permute-done.6.late0_ref = bf16[64,2048]{1,0:T(8,128)(2,1)S(1)} collective-permute-done((bf16[64,2048]{1,0:T(8,128)(2,1)S(1)}, bf16[64,2048]{1,0:T(8,128)(2,1)S(1)}, u32[]{:S(2)}, u32[]{:S(2)}) %collective-permute-start.6) | collective-permute-done | bytes 262176 | tf_op jit(solution)/shard_map/ppermute | solution.py:41
  41.5 10.9 %shard_map.84 = (bf16[4,128,256]{2,1,0:T(8,128)(2,1)S(1)}, bf16[4,4,128,256]{3,2,1,0:T(8,128)(2,1)S(1)}, bf16[4,3,128,256]{3,2,1,0:T(8,128)(2,1)S(1)}, bf16[12,5...) custom-call(bf16[3,128,512]{2,1,0:T(8,128)(2,1)S(1)} %get-tuple-elem, ...), custom_call_target="tpu_custom_call" | custom-call | flops 3000000000 | bytes 1048576 | tf_op jit(solution)/shard_map/pallas_call | solution.py:362
  52.9 1.2 %collective-permute-done.8.other_ref.pair_ref = bf16[4,128,256]{2,1,0:T(8,128)(2,1)S(1)} collective-permute-done((bf16[4,128,256]{2,1,0:T(8,128)(2,1)S(1)}, bf16[4,128,256]{2,1,0:T(8,128)(2,1)S(1)}, u32[]{:S(2)}, u32[]{:S(2)}) %collective-permute-start.8) | collective-permute-done | bytes 262176 | tf_op jit(solution)/shard_map/ppermute | solution.py:439
  54.3 1.3 %collective-permute-start.9 = (bf16[2,128,256]{2,1,0:T(8,128)(2,1)S(1)}, bf16[2,128,256]{2,1,0:T(8,128)(2,1)S(1)}, u32[]{:S(2)}, u32[]{:S(2)}) collective-permute-start(bf16[2,128,256]{2,1,0:T(8,128)(2,1)S(1)} %shard_map.86.block_ref), channel_id=1, source_target_pairs={{0,8},{4,12},{16,24},{20,28},{1,9},{5,13},{17,25},{21,29},{2,10},{... | collective-permute-start | bytes 393224 | tf_op jit(solution)/shard_map/ppermute | solution.py:456
  55.6 2.7 %collective-permute-done.9.sent_ref = bf16[2,128,256]{2,1,0:T(8,128)(2,1)S(1)} collective-permute-done((bf16[2,128,256]{2,1,0:T(8,128)(2,1)S(1)}, bf16[2,128,256]{2,1,0:T(8,128)(2,1)S(1)}, u32[]{:S(2)}, u32[]{:S(2)}) %collective-permute-start.9) | collective-permute-done | bytes 131104 | tf_op jit(solution)/shard_map/ppermute | solution.py:456
  59.2 1.5 %collective-permute-start.10 = (bf16[2,128,128]{2,1,0:T(8,128)(2,1)S(1)}, bf16[2,128,128]{2,1,0:T(8,128)(2,1)S(1)}, u32[]{:S(2)}, u32[]{:S(2)}) collective-permute-start(bf16[2,128,128]{2,1,0:T(8,128)(2,1)S(1)} %slice.15), channel_id=1, source_target_pairs={{8,16},{12,20},{9,17},{13,21},{10,18},{14,22},{11,19},{15,23}} | collective-permute-start | bytes 196616 | tf_op jit(solution)/shard_map/ppermute | solution.py:456
  60.7 6.7 %collective-permute-done.10.refs_0_ = bf16[2,128,128]{2,1,0:T(8,128)(2,1)S(1)} collective-permute-done((bf16[2,128,128]{2,1,0:T(8,128)(2,1)S(1)}, bf16[2,128,128]{2,1,0:T(8,128)(2,1)S(1)}, u32[]{:S(2)}, u32[]{:S(2)}) %collective-permute-start.10) | collective-permute-done | bytes 65568 | tf_op jit(solution)/shard_map/ppermute | solution.py:456
  67.5 1.6 %collective-permute-start.12 = (bf16[2,128,128]{2,1,0:T(8,128)(2,1)S(1)}, bf16[2,128,128]{2,1,0:T(8,128)(2,1)S(1)}, u32[]{:S(2)}, u32[]{:S(2)}) collective-permute-start(bf16[2,128,128]{2,1,0:T(8,128)(2,1)S(1)} %shard_map.88.mine_ref), channel_id=1, source_target_pairs={{0,4},{4,0},{8,12},{12,8},{16,20},{20,16},{24,28},{28,24},{1,5},{5... | collective-permute-start | bytes 196616 | tf_op jit(solution)/shard_map/ppermute | solution.py:470
  69.1 2.4 %shard_map.85 = (bf16[4,512,128]{2,1,0:T(8,128)(2,1)S(1)}, f32[4,512,128]{2,1,0:T(8,128)S(1)}) custom-call(bf16[4,4,128,256]{3,2,1,0:T(8,128)(2,1)S(1)} %get-tuple-element.26.both_ref, bf16[4,3,128,256]{3,2,1,0:T(8,128)(2,1)S(1)} %get-tuple-element.27.low_ref, bf16[12,512,128]{2,1,0:T(8,128)(2,1)S(1)} %get-tuple-element.28.act, ...), custom_call_target="tpu_custom_call" | custom-call | flops 2000000000 | bytes 1048576 | tf_op jit(solution)/shard_map/pallas_call | solution.py:362
  71.5 1.8 %shard_map.89 = bf16[512,512]{1,0:T(8,128)(2,1)} custom-call(bf16[4,512,128]{2,1,0:T(8,128)(2,1)S(1)} %get-tuple-element.31.qp_ref, f32[4,512,128]{2,1,0:T(8,128)S(1)} %get-tuple-element.32.o_ref, bf16[4,128,256]{2,1,0:T(8,128)(2,1)S(1)} %collective-permute-done.8.other_ref.pair_ref, bf16[2,128,128]{2,1,0:T(8,128)(2,1)S(1)} %shard_map.88.mine_ref, ...), custom_call_target="tpu_custom_call" | custom-call | flops 50000000 | bytes 1048576 | tf_op jit(solution)/shard_map/pallas_call | solution.py:362
  (37 shorter events, 3.7 us)
Async XLA Ops:
  0.8 18.2 %collective-permute-start.5 = (bf16[16,2048]{1,0:T(8,128)(2,1)S(1)}, bf16[16,2048]{1,0:T(8,128)(2,1)S(1)}, u32[]{:S(2)}, u32[]{:S(2)}) collective-permute-start(bf16[16,2048]{1,0:T(8,128)(2,1)S(1)} %slice.12), channel_id=1, source_target_pairs={{3,7},{7,11},{11,15},{15,19},{19,23},{23,27},{27,31}} | collective-permute-start | bytes 196616 | tf_op jit(solution)/shard_map/ppermute | solution.py:67
  1.5 17.7 %collective-permute-start.4 = (bf16[16,2048]{1,0:T(8,128)(2,1)S(1)}, bf16[16,2048]{1,0:T(8,128)(2,1)S(1)}, u32[]{:S(2)}, u32[]{:S(2)}) collective-permute-start(bf16[16,2048]{1,0:T(8,128)(2,1)S(1)} %slice.12), channel_id=1, source_target_pairs={{3,6},{7,10},{11,14},{15,18},{19,22},{23,26},{27,30}} | collective-permute-start | bytes 196616 | tf_op jit(solution)/shard_map/ppermute | solution.py:67
  2.8 16.4 %collective-permute-start.3 = (bf16[16,2048]{1,0:T(8,128)(2,1)S(1)}, bf16[16,2048]{1,0:T(8,128)(2,1)S(1)}, u32[]{:S(2)}, u32[]{:S(2)}) collective-permute-start(bf16[16,2048]{1,0:T(8,128)(2,1)S(1)} %slice.12), channel_id=1, source_target_pairs={{3,5},{7,9},{11,13},{15,17},{19,21},{23,25},{27,29}} | collective-permute-start | bytes 196616 | tf_op jit(solution)/shard_map/ppermute | solution.py:67
  3.5 15.7 %collective-permute-start.2 = (bf16[16,2048]{1,0:T(8,128)(2,1)S(1)}, bf16[16,2048]{1,0:T(8,128)(2,1)S(1)}, u32[]{:S(2)}, u32[]{:S(2)}) collective-permute-start(bf16[16,2048]{1,0:T(8,128)(2,1)S(1)} %slice.12), channel_id=1, source_target_pairs={{3,4},{7,8},{11,12},{15,16},{19,20},{23,24},{27,28}} | collective-permute-start | bytes 196616 | tf_op jit(solution)/shard_map/ppermute | solution.py:67
  4.2 18.4 %collective-permute-start = (bf16[128,2048]{1,0:T(8,128)(2,1)}, bf16[128,2048]{1,0:T(8,128)(2,1)S(1)}, u32[]{:S(2)}, u32[]{:S(2)}) collective-permute-start(bf16[128,2048]{1,0:T(8,128)(2,1)} %refs_0_.1), channel_id=1, source_target_pairs={{0,1},{1,0},{2,3},{3,2},{4,5},{5,4},{6,7},{7,6},{8,9},{9,8},{10,11... | collective-permute-start | bytes 1572872 | tf_op jit(solution)/shard_map/ppermute | solution.py:41
  11.7 1.0 %copy-start = (bf16[128,2048]{1,0:T(8,128)(2,1)S(1)}, bf16[128,2048]{1,0:T(8,128)(2,1)}, u32[]{:S(2)}) copy-start(bf16[128,2048]{1,0:T(8,128)(2,1)} %refs_0_.1) | copy-start | bytes 1572868
  12.7 2.8 %copy-start.2 = (bf16[2048,3,512]{2,0,1:T(8,128)(2,1)S(1)}, bf16[2048,3,512]{2,0,1:T(8,128)(2,1)}, u32[]{:S(2)}) copy-start(bf16[2048,3,512]{2,0,1:T(8,128)(2,1)} %param.9) | copy-start | bytes 18874372
  15.5 1.6 %copy-start.4 = (bf16[2048,512]{1,0:T(8,128)(2,1)S(1)}, bf16[2048,512]{1,0:T(8,128)(2,1)}, u32[]{:S(2)}) copy-start(bf16[2048,512]{1,0:T(8,128)(2,1)} %gate_w_ref.1) | copy-start | bytes 6291460
  17.1 2.0 %copy-start.7 = (f32[4]{0:T(128)S(1)}, f32[4]{0:T(128)}, u32[]{:S(2)}) copy-start(f32[4]{0:T(128)} %param.13) | copy-start | bytes 52
  17.1 2.1 %copy-start.6 = (f32[4]{0:T(128)S(1)}, f32[4]{0:T(128)}, u32[]{:S(2)}) copy-start(f32[4]{0:T(128)} %param.14) | copy-start | bytes 52
  17.1 16.1 %copy-start.3 = (bf16[2048,3,512]{2,0,1:T(8,128)(2,1)S(1)}, bf16[2048,3,512]{2,0,1:T(8,128)(2,1)}, u32[]{:S(2)}) copy-start(bf16[2048,3,512]{2,0,1:T(8,128)(2,1)} %param.9) | copy-start | bytes 18874372
  17.1 16.1 %copy-start.5 = (bf16[2048,512]{1,0:T(8,128)(2,1)S(1)}, bf16[2048,512]{1,0:T(8,128)(2,1)}, u32[]{:S(2)}) copy-start(bf16[2048,512]{1,0:T(8,128)(2,1)} %gate_w_ref.1) | copy-start | bytes 6291460
  19.1 14.0 %collective-permute-start.1 = (bf16[128,2048]{1,0:T(8,128)(2,1)S(1)}, bf16[128,2048]{1,0:T(8,128)(2,1)S(1)}, u32[]{:S(2)}, u32[]{:S(2)}) collective-permute-start(bf16[128,2048]{1,0:T(8,128)(2,1)S(1)} %copy-done), channel_id=1, source_target_pairs={{0,2},{1,3},{2,0},{3,1},{4,6},{5,7},{6,4},{7,5},{8,10},{9,11},{10,... | collective-permute-start | bytes 1572872 | tf_op jit(solution)/shard_map/ppermute | solution.py:41
  22.6 15.7 %collective-permute-start.7 = (bf16[64,2048]{1,0:T(8,128)(2,1)S(1)}, bf16[64,2048]{1,0:T(8,128)(2,1)S(1)}, u32[]{:S(2)}, u32[]{:S(2)}) collective-permute-start(bf16[64,2048]{1,0:T(8,128)(2,1)S(1)} %slice.17), channel_id=1, source_target_pairs={{0,2},{1,3},{2,0},{3,1},{4,6},{5,7},{6,4},{7,5},{8,10},{9,11},{10,... | collective-permute-start | bytes 786440 | tf_op jit(solution)/shard_map/ppermute | solution.py:41
  33.1 8.4 %collective-permute-start.6 = (bf16[64,2048]{1,0:T(8,128)(2,1)S(1)}, bf16[64,2048]{1,0:T(8,128)(2,1)S(1)}, u32[]{:S(2)}, u32[]{:S(2)}) collective-permute-start(bf16[64,2048]{1,0:T(8,128)(2,1)S(1)} %slice.16), channel_id=1, source_target_pairs={{0,1},{1,0},{2,3},{3,2},{4,5},{5,4},{6,7},{7,6},{8,9},{9,8},{10,11... | collective-permute-start | bytes 786440 | tf_op jit(solution)/shard_map/ppermute | solution.py:41
  52.5 1.6 %collective-permute-start.8 = (bf16[4,128,256]{2,1,0:T(8,128)(2,1)S(1)}, bf16[4,128,256]{2,1,0:T(8,128)(2,1)S(1)}, u32[]{:S(2)}, u32[]{:S(2)}) collective-permute-start(bf16[4,128,256]{2,1,0:T(8,128)(2,1)S(1)} %get-tuple-element.33.mine_ref), channel_id=1, source_target_pairs={{0,4},{4,0},{8,12},{12,8},{16,20},{20,16},{24,28},{28,24},{1,5},{5... | collective-permute-start | bytes 786440 | tf_op jit(solution)/shard_map/ppermute | solution.py:439
  54.3 4.0 %collective-permute-start.9 = (bf16[2,128,256]{2,1,0:T(8,128)(2,1)S(1)}, bf16[2,128,256]{2,1,0:T(8,128)(2,1)S(1)}, u32[]{:S(2)}, u32[]{:S(2)}) collective-permute-start(bf16[2,128,256]{2,1,0:T(8,128)(2,1)S(1)} %shard_map.86.block_ref), channel_id=1, source_target_pairs={{0,8},{4,12},{16,24},{20,28},{1,9},{5,13},{17,25},{21,29},{2,10},{... | collective-permute-start | bytes 393224 | tf_op jit(solution)/shard_map/ppermute | solution.py:456
  58.5 2.2 %collective-permute-start.11 = (bf16[2,128,128]{2,1,0:T(8,128)(2,1)S(1)}, bf16[2,128,128]{2,1,0:T(8,128)(2,1)S(1)}, u32[]{:S(2)}, u32[]{:S(2)}) collective-permute-start(bf16[2,128,128]{2,1,0:T(8,128)(2,1)S(1)} %slice.15), channel_id=1, source_target_pairs={{8,24},{12,28},{9,25},{13,29},{10,26},{14,30},{11,27},{15,31}} | collective-permute-start | bytes 196616 | tf_op jit(solution)/shard_map/ppermute | solution.py:456
  59.2 8.2 %collective-permute-start.10 = (bf16[2,128,128]{2,1,0:T(8,128)(2,1)S(1)}, bf16[2,128,128]{2,1,0:T(8,128)(2,1)S(1)}, u32[]{:S(2)}, u32[]{:S(2)}) collective-permute-start(bf16[2,128,128]{2,1,0:T(8,128)(2,1)S(1)} %slice.15), channel_id=1, source_target_pairs={{8,16},{12,20},{9,17},{13,21},{10,18},{14,22},{11,19},{15,23}} | collective-permute-start | bytes 196616 | tf_op jit(solution)/shard_map/ppermute | solution.py:456
  67.5 4.0 %collective-permute-start.12 = (bf16[2,128,128]{2,1,0:T(8,128)(2,1)S(1)}, bf16[2,128,128]{2,1,0:T(8,128)(2,1)S(1)}, u32[]{:S(2)}, u32[]{:S(2)}) collective-permute-start(bf16[2,128,128]{2,1,0:T(8,128)(2,1)S(1)} %shard_map.88.mine_ref), channel_id=1, source_target_pairs={{0,4},{4,0},{8,12},{12,8},{16,20},{20,16},{24,28},{28,24},{1,5},{5... | collective-permute-start | bytes 196616 | tf_op jit(solution)/shard_map/ppermute | solution.py:470
  69.1 2.5 %copy-start.1 = (f32[128]{0:T(128)S(1)}, f32[128]{0:T(128)}, u32[]{:S(2)}) copy-start(f32[128]{0:T(128)} %param.15) | copy-start | bytes 1540

commit v4 on v3

--- a/solution.py
+++ b/solution.py
@@ -17,6 +17,7 @@
 DELTA_FLOPS = 3000000000
 REACH_FLOPS = 2000000000
 SMALL_FLOPS = 50000000
+
 
 f32 = jnp.float32
 bf16 = jnp.bfloat16
@@ -73,13 +74,28 @@
     return x / (1.0 + jnp.exp(-x))
 
 
+def scalar_weights(ref):
+    kinds, heads, width = ref.shape
+    rows = [ref[kind].astype(f32) for kind in range(kinds)]
+    rows.append(jnp.zeros((LANES - kinds * heads, width), f32))
+    return jnp.concatenate(rows, axis=0).astype(bf16)
+
+
+def lane_row(ref):
+    lane = lax.broadcasted_iota(jnp.int32, (1, LANES), 1)
+    row = jnp.zeros((1, LANES), f32)
+    for head in range(ref.shape[1]):
+        row = jnp.where(lane == head, ref[:, head:head + 1], row)
+    return row
+
+
 def project_kernel(count, *refs):
     blocks = refs[:count]
     w_ref, gate_w_ref, small_ref = refs[count:count + 3]
     p_ref, gate_ref, sc_ref = refs[count + 3:count + 6]
     rows = sc_ref.shape[0]
     tokens = jnp.concatenate([ref[...] for ref in blocks], axis=0)
-    sc_ref[...] = dot(tokens, small_ref[...])[:rows]
+    sc_ref[...] = dot(tokens, scalar_weights(small_ref), (1, 1))[:rows]
     gate_ref[...] = silu(dot(tokens, gate_w_ref[...])[:rows])
 
     def one(branch, carry):
@@ -106,7 +122,7 @@
 
 def delta_kernel(
     heads, blocks, own_ref, own_sc_ref, p_ref, sc_ref, late0_ref, late1_ref, w_ref,
-    gate_w_ref, small_ref, taps_ref, vec_ref, x_ref, both_ref, low_ref, act, cols, rows_of, gate_ref,
+    small_ref, taps_ref, rate_ref, bias_ref, x_ref, both_ref, low_ref, act, cols, rows_of,
     xp, sc, masks, mixes, solves,
 ):
     seq_rows = act.shape[1]
@@ -119,8 +135,7 @@
         return pl.multiple_of(offset + lax.bitwise_xor(me, m) * rows, 8)
 
     late = jnp.concatenate([late0_ref[...], late1_ref[...]], axis=0)
-    sc[pl.ds(place(blocks - 1), rows)] = dot(late, small_ref[...])
-    gate_ref[...] = silu(dot(late, gate_w_ref[...]))
+    sc[pl.ds(place(blocks - 1), rows)] = dot(late, scalar_weights(small_ref), (1, 1))
     sc[pl.ds(place(0), rows)] = own_sc_ref[...]
     for m in range(1, blocks - 1):
         sc[pl.ds(place(m), rows)] = sc_ref[(m - 1) * rows:m * rows]
@@ -150,22 +165,24 @@
         masks[level] = beside(hit, hit)
 
     root = 1.0 / math.sqrt(LANES)
+    rate, bias = -lane_row(rate_ref), lane_row(bias_ref)
 
     def prepare(chunk, carry):
         base = pl.multiple_of(chunk * CHUNK, CHUNK)
         raw = sc[pl.ds(base, CHUNK)]
-        shifted = raw + vec_ref[1:2]
+        shifted = raw + bias
         soft = jnp.maximum(shifted, 0.0) + jnp.log1p(jnp.exp(-jnp.abs(shifted)))
-        decay = dot(lower, vec_ref[0:1] * soft, precision=lax.Precision.HIGHEST)
+        decay = dot(lower, rate * soft, precision=lax.Precision.HIGHEST)
         beta = 1.0 / (1.0 + jnp.exp(-raw))
         comb = jnp.where(ci < heads, decay, 0.0)
         for head in range(heads):
             norms = []
             for branch in range(3):
                 tile = branch * heads + head
+                weights = taps_ref[branch, :, head * LANES:(head + 1) * LANES].astype(f32)
                 total = None
                 for i in range(taps):
-                    term = xp[tile, pl.ds(base + (RIM - taps + 1 + i), CHUNK)] * taps_ref[tile, i:i + 1]
+                    term = xp[tile, pl.ds(base + (RIM - taps + 1 + i), CHUNK)] * weights[i:i + 1]
                     total = term if total is None else total + term
                 value = silu(total).astype(bf16)
                 act[tile, pl.ds(base, CHUNK)] = value
@@ -248,7 +265,12 @@
         x_ref[head] = runs[head].astype(bf16)
 
 
-def reach_kernel(heads, both_ref, low_ref, act, cols, rows_of, qp_ref, o_ref):
+def reach_kernel(
+    heads, both_ref, low_ref, act, cols, rows_of, late0_ref, late1_ref, gate_w_ref,
+    qp_ref, o_ref, gate_ref,
+):
+    late = jnp.concatenate([late0_ref[...], late1_ref[...]], axis=0)
+    gate_ref[...] = silu(dot(late, gate_w_ref[...]))
     chunks = act.shape[1] // CHUNK
     ri, ci = grid_index((CHUNK, CHUNK))
     upto = ri >= ci
@@ -371,7 +393,6 @@
 
 
 def per_device(hidden, w_qkv, w_gate, w_decay_beta, conv_weight, decay_rate, dt_bias, norm_gain):
-    model_width = hidden.shape[1]
     heads = decay_rate.shape[0]
     dim = norm_gain.shape[0]
     columns = heads * dim
@@ -383,11 +404,9 @@
     shape = jax.ShapeDtypeStruct
 
     w_three = w_qkv.transpose(1, 0, 2)
-    small = jnp.pad(
-        w_decay_beta.reshape(model_width, 2 * heads), ((0, 0), (0, LANES - 2 * heads))
-    )
-    taps = conv_weight.reshape(conv_weight.shape[0], 3 * heads, dim).transpose(1, 0, 2).astype(f32)
-    vectors = jnp.pad(jnp.stack([-decay_rate, dt_bias]), ((0, 6), (0, LANES - heads)))
+    small = w_decay_beta.transpose(1, 2, 0)
+    taps = conv_weight.transpose(1, 0, 2)
+    rate, bias = decay_rate.reshape(1, heads), dt_bias.reshape(1, heads)
 
     early, late = gather_blocks(hidden, "tp")
     rim = rim_rows(hidden, RIM)
@@ -406,7 +425,7 @@
 
     own_p, own_gate, own_sc = project([hidden], rows)
     mid_p, mid_gate, mid_sc = project([*early, rim], seq_rows - 2 * rows, RIM)
-    own, both, low, act, cols, rows_of, late_gate = call(
+    own, both, low, act, cols, rows_of = call(
         functools.partial(delta_kernel, heads, blocks),
         (
             shape((heads, dim, 2 * dim), bf16),
@@ -415,9 +434,8 @@
             shape((3 * heads, seq_rows, dim), bf16),
             shape((chunks, CHUNK, LANES), f32),
             shape((chunks, CHUNK, LANES), f32),
-            shape((rows, columns), f32),
         ),
-        [own_p, own_sc, mid_p, mid_sc, *late, *weights, taps, vectors],
+        [own_p, own_sc, mid_p, mid_sc, *late, w_three, small, taps, rate, bias],
         flops=DELTA_FLOPS, limit=32,
         scratch=[
             pltpu.VMEM((3 * heads, seq_rows + RIM, dim), f32),
@@ -427,10 +445,14 @@
             pltpu.VMEM((heads * chunks // 2, CHUNK, 2 * CHUNK), f32),
         ],
     )
-    reach, base = call(
+    reach, base, late_gate = call(
         functools.partial(reach_kernel, heads),
-        (shape((heads, seq_rows, dim), bf16), shape((heads, seq_rows, dim), f32)),
-        [both, low, act, cols, rows_of], flops=REACH_FLOPS, limit=12,
+        (
+            shape((heads, seq_rows, dim), bf16),
+            shape((heads, seq_rows, dim), f32),
+            shape((rows, columns), f32),
+        ),
+        [both, low, act, cols, rows_of, *late, w_gate], flops=REACH_FLOPS, limit=12,
     )
 
     share = heads % 2 == 0

time: 73.8 us -> 64.7 us (0.88)
  the two profiles are of different devices: /device:TPU:21 before, /device:TPU:17 now
where the time goes in v4:
time: 64.7 us; the launch traced here: 64.3 us
  starting transfers between devices  21.5 us (33%)
  Pallas kernels  21 us (32%)
  waiting for transfers between devices  14.4 us (22%)
  local copies, waits for them, and re-layouts  7.13 us (11%)
    pallas_call x8, Pallas kernels, call(): pl.pallas_call(kernel, out_shape=out, in_specs=[whole()] * len(operands),...  21 us
    ppermute x4, starting transfers between devices, swap(): return lax.ppermute(value, axis, [(i, i ^ step) for i in range(count)])  11.9 us
    ppermute x3, waiting for transfers between devices, per_device(): parts.append(lax.ppermute(sent, 'seq', route))  9.38 us
    unnamed x22, local copies, waits for them, and re-layouts  6.24 us
    ppermute x4, waiting for transfers between devices, swap(): return lax.ppermute(value, axis, [(i, i ^ step) for i in range(count)])  3.81 us
    ppermute x3, starting transfers between devices, per_device(): parts.append(lax.ppermute(sent, 'seq', route))  3.43 us
    ppermute x4, starting transfers between devices, rim_rows(): part = lax.ppermute(tail, ('seq', 'tp'), route)  3.27 us
    ppermute x1, starting transfers between devices, per_device(): back = lax.ppermute(state, 'seq', swap) if share else state  1.58 us
  transfers between devices with their start and end apart: 13, of which 5 were waited for; matrix products, arithmetic and copies ran while one was open for 0% of the time, Pallas kernels for 12%

profile of v4, /device:TPU:17, one launch (start us, length us, event | category | flops | bytes accessed | tf_op | source)
XLA Modules:
  0.0 64.3 jit_solution(1508797287272282050)
XLA Ops:
  0.0 0.8 %slice.12 = bf16[16,2048]{1,0:T(8,128)(2,1)S(1)} slice(bf16[128,2048]{1,0:T(8,128)(2,1)} %refs_0_.1), slice={[112:128], [0:2048]} | slice | bytes 131072 | tf_op jit(solution)/shard_map/slice | solution.py:64
  1.5 0.7 %collective-permute-start.4 = (bf16[16,2048]{1,0:T(8,128)(2,1)S(1)}, bf16[16,2048]{1,0:T(8,128)(2,1)S(1)}, u32[]{:S(2)}, u32[]{:S(2)}) collective-permute-start(bf16[16,2048]{1,0:T(8,128)(2,1)S(1)} %slice.12), channel_id=1, source_target_pairs={{3,6},{7,10},{11,14},{15,18},{19,22},{23,26},{27,30}} | collective-permute-start | bytes 196616 | tf_op jit(solution)/shard_map/ppermute | solution.py:68
  2.9 1.3 %collective-permute-start.2 = (bf16[16,2048]{1,0:T(8,128)(2,1)S(1)}, bf16[16,2048]{1,0:T(8,128)(2,1)S(1)}, u32[]{:S(2)}, u32[]{:S(2)}) collective-permute-start(bf16[16,2048]{1,0:T(8,128)(2,1)S(1)} %slice.12), channel_id=1, source_target_pairs={{3,4},{7,8},{11,12},{15,16},{19,20},{23,24},{27,28}} | collective-permute-start | bytes 196616 | tf_op jit(solution)/shard_map/ppermute | solution.py:68
  4.2 1.3 %collective-permute-start = (bf16[128,2048]{1,0:T(8,128)(2,1)}, bf16[128,2048]{1,0:T(8,128)(2,1)S(1)}, u32[]{:S(2)}, u32[]{:S(2)}) collective-permute-start(bf16[128,2048]{1,0:T(8,128)(2,1)} %refs_0_.1), channel_id=1, source_target_pairs={{0,1},{1,0},{2,3},{3,2},{4,5},{5,4},{6,7},{7,6},{8,9},{9,8},{10,11... | collective-permute-start | bytes 1572872 | tf_op jit(solution)/shard_map/ppermute | solution.py:42
  5.4 5.6 %collective-permute-start.1 = (bf16[128,2048]{1,0:T(8,128)(2,1)}, bf16[128,2048]{1,0:T(8,128)(2,1)S(1)}, u32[]{:S(2)}, u32[]{:S(2)}) collective-permute-start(bf16[128,2048]{1,0:T(8,128)(2,1)} %refs_0_.1), channel_id=1, source_target_pairs={{0,2},{1,3},{2,0},{3,1},{4,6},{5,7},{6,4},{7,5},{8,10},{9,11},{10,... | collective-permute-start | bytes 1572872 | tf_op jit(solution)/shard_map/ppermute | solution.py:42
  11.0 1.1 %copy-done = bf16[128,2048]{1,0:T(8,128)(2,1)S(1)} copy-done((bf16[128,2048]{1,0:T(8,128)(2,1)S(1)}, bf16[128,2048]{1,0:T(8,128)(2,1)}, u32[]{:S(2)}) %copy-start) | copy-done | bytes 524312
  12.1 2.8 %copy-done.2 = bf16[2048,3,512]{2,0,1:T(8,128)(2,1)S(1)} copy-done((bf16[2048,3,512]{2,0,1:T(8,128)(2,1)S(1)}, bf16[2048,3,512]{2,0,1:T(8,128)(2,1)}, u32[]{:S(2)}) %copy-start.2) | copy-done | bytes 6291480
  14.9 1.6 %copy-done.4 = bf16[2048,512]{1,0:T(8,128)(2,1)S(1)} copy-done((bf16[2048,512]{1,0:T(8,128)(2,1)S(1)}, bf16[2048,512]{1,0:T(8,128)(2,1)}, u32[]{:S(2)}) %copy-start.4) | copy-done | bytes 2097176
  16.5 0.8 %copy-done.6 = bf16[2048,2,4]{0,2,1:T(4,128)(2,1)S(1)} copy-done((bf16[2048,2,4]{0,2,1:T(4,128)(2,1)S(1)}, bf16[2048,2,4]{0,2,1:T(4,128)(2,1)}, u32[]{:S(2)}) %copy-start.6) | copy-done | bytes 32792
  17.2 1.9 %shard_map.82 = (bf16[3,128,512]{2,1,0:T(8,128)(2,1)S(1)}, f32[128,512]{1,0:T(8,128)S(1)}, f32[128,128]{1,0:T(8,128)S(1)}) custom-call(bf16[128,2048]{1,0:T(8,128)(2,1)S(1)} %copy-done, bf16[3,2048,512]{2,1,0:T(8,128)(2,1)S(1)} %bitcast.7, bf16[2048,512]{1,0:T(8,128)(2,1)S(1)} %copy-done.4, bf16[2,4,2048]{2,1,0:T(4,128)(2,1)S(1)} %bitcast.10), custom_call_target="tpu_custom_call" | custom-call | flops 3000000000 | bytes 1048576 | tf_op jit(solution)/shard_map/pallas_call | solution.py:384
  19.3 4.7 %collective-permute-start.7 = (bf16[64,2048]{1,0:T(8,128)(2,1)S(1)}, bf16[64,2048]{1,0:T(8,128)(2,1)S(1)}, u32[]{:S(2)}, u32[]{:S(2)}) collective-permute-start(bf16[64,2048]{1,0:T(8,128)(2,1)S(1)} %slice.17), channel_id=1, source_target_pairs={{0,2},{1,3},{2,0},{3,1},{4,6},{5,7},{6,4},{7,5},{8,10},{9,11},{10,... | collective-permute-start | bytes 786440 | tf_op jit(solution)/shard_map/ppermute | solution.py:42
  24.4 3.3 %shard_map.83 = (bf16[3,272,512]{2,1,0:T(8,128)(2,1)S(1)}, f32[256,512]{1,0:T(8,128)S(1)}, f32[256,128]{1,0:T(8,128)S(1)}) custom-call(bf16[128,2048]{1,0:T(8,128)(2,1)S(1)} %collective-permute-done.refs_0_, bf16[128,2048]{1,0:T(8,128)(2,1)S(1)} %collective-permute-done.1.refs_1_, bf16[16,2048]{1,0:T(8,128)(2,1)S(1)} %add_add_fusion.refs_2_, ...), custom_call_target="tpu_custom_call" | custom-call | flops 3000000000 | bytes 1048576 | tf_op jit(solution)/shard_map/pallas_call | solution.py:384
  27.7 2.8 %collective-permute-done.7.late1_ref = bf16[64,2048]{1,0:T(8,128)(2,1)S(1)} collective-permute-done((bf16[64,2048]{1,0:T(8,128)(2,1)S(1)}, bf16[64,2048]{1,0:T(8,128)(2,1)S(1)}, u32[]{:S(2)}, u32[]{:S(2)}) %collective-permute-start.7) | collective-permute-done | bytes 262176 | tf_op jit(solution)/shard_map/ppermute | solution.py:42
  30.5 1.0 %collective-permute-done.6.late0_ref = bf16[64,2048]{1,0:T(8,128)(2,1)S(1)} collective-permute-done((bf16[64,2048]{1,0:T(8,128)(2,1)S(1)}, bf16[64,2048]{1,0:T(8,128)(2,1)S(1)}, u32[]{:S(2)}, u32[]{:S(2)}) %collective-permute-start.6) | collective-permute-done | bytes 262176 | tf_op jit(solution)/shard_map/ppermute | solution.py:42
  31.5 10.8 %shard_map.84 = (bf16[4,128,256]{2,1,0:T(8,128)(2,1)S(1)}, bf16[4,4,128,256]{3,2,1,0:T(8,128)(2,1)S(1)}, bf16[4,3,128,256]{3,2,1,0:T(8,128)(2,1)S(1)}, bf16[12,5...) custom-call(bf16[3,128,512]{2,1,0:T(8,128)(2,1)S(1)} %get-tuple-element.22.own_ref, ...), custom_call_target="tpu_custom_call" | custom-call | flops 3000000000 | bytes 1048576 | tf_op jit(solution)/shard_map/pallas_call | solution.py:384
  42.3 1.3 %collective-permute-start.8 = (bf16[4,128,256]{2,1,0:T(8,128)(2,1)S(1)}, bf16[4,128,256]{2,1,0:T(8,128)(2,1)S(1)}, u32[]{:S(2)}, u32[]{:S(2)}) collective-permute-start(bf16[4,128,256]{2,1,0:T(8,128)(2,1)S(1)} %get-tuple-element.33.mine_ref), channel_id=1, source_target_pairs={{0,4},{4,0},{8,12},{12,8},{16,20},{20,16},{24,28},{28,24},{1,5},{5... | collective-permute-start | bytes 786440 | tf_op jit(solution)/shard_map/ppermute | solution.py:461
  43.6 1.2 %collective-permute-done.8.other_ref.pair_ref = bf16[4,128,256]{2,1,0:T(8,128)(2,1)S(1)} collective-permute-done((bf16[4,128,256]{2,1,0:T(8,128)(2,1)S(1)}, bf16[4,128,256]{2,1,0:T(8,128)(2,1)S(1)}, u32[]{:S(2)}, u32[]{:S(2)}) %collective-permute-start.8) | collective-permute-done | bytes 262176 | tf_op jit(solution)/shard_map/ppermute | solution.py:461
  45.0 1.3 %collective-permute-start.9 = (bf16[2,128,256]{2,1,0:T(8,128)(2,1)S(1)}, bf16[2,128,256]{2,1,0:T(8,128)(2,1)S(1)}, u32[]{:S(2)}, u32[]{:S(2)}) collective-permute-start(bf16[2,128,256]{2,1,0:T(8,128)(2,1)S(1)} %shard_map.86.block_ref), channel_id=1, source_target_pairs={{0,8},{4,12},{16,24},{20,28},{1,9},{5,13},{17,25},{21,29},{2,10},{... | collective-permute-start | bytes 393224 | tf_op jit(solution)/shard_map/ppermute | solution.py:478
  46.3 2.7 %collective-permute-done.9.sent_ref = bf16[2,128,256]{2,1,0:T(8,128)(2,1)S(1)} collective-permute-done((bf16[2,128,256]{2,1,0:T(8,128)(2,1)S(1)}, bf16[2,128,256]{2,1,0:T(8,128)(2,1)S(1)}, u32[]{:S(2)}, u32[]{:S(2)}) %collective-permute-start.9) | collective-permute-done | bytes 131104 | tf_op jit(solution)/shard_map/ppermute | solution.py:478
  49.9 1.5 %collective-permute-start.10 = (bf16[2,128,128]{2,1,0:T(8,128)(2,1)S(1)}, bf16[2,128,128]{2,1,0:T(8,128)(2,1)S(1)}, u32[]{:S(2)}, u32[]{:S(2)}) collective-permute-start(bf16[2,128,128]{2,1,0:T(8,128)(2,1)S(1)} %slice.15), channel_id=1, source_target_pairs={{8,16},{12,20},{9,17},{13,21},{10,18},{14,22},{11,19},{15,23}} | collective-permute-start | bytes 196616 | tf_op jit(solution)/shard_map/ppermute | solution.py:478
  51.4 6.6 %collective-permute-done.10.refs_0_ = bf16[2,128,128]{2,1,0:T(8,128)(2,1)S(1)} collective-permute-done((bf16[2,128,128]{2,1,0:T(8,128)(2,1)S(1)}, bf16[2,128,128]{2,1,0:T(8,128)(2,1)S(1)}, u32[]{:S(2)}, u32[]{:S(2)}) %collective-permute-start.10) | collective-permute-done | bytes 65568 | tf_op jit(solution)/shard_map/ppermute | solution.py:478
  58.2 1.6 %collective-permute-start.12 = (bf16[2,128,128]{2,1,0:T(8,128)(2,1)S(1)}, bf16[2,128,128]{2,1,0:T(8,128)(2,1)S(1)}, u32[]{:S(2)}, u32[]{:S(2)}) collective-permute-start(bf16[2,128,128]{2,1,0:T(8,128)(2,1)S(1)} %shard_map.88.mine_ref), channel_id=1, source_target_pairs={{0,4},{4,0},{8,12},{12,8},{16,20},{20,16},{24,28},{28,24},{1,5},{5... | collective-permute-start | bytes 196616 | tf_op jit(solution)/shard_map/ppermute | solution.py:492
  59.8 2.7 %shard_map.85 = (bf16[4,512,128]{2,1,0:T(8,128)(2,1)S(1)}, f32[4,512,128]{2,1,0:T(8,128)S(1)}, f32[128,512]{1,0:T(8,128)S(1)}) custom-call(bf16[4,4,128,256]{3,2,1,0:T(8,128)(2,1)S(1)} %get-tuple-element.26.both_ref, bf16[4,3,128,256]{3,2,1,0:T(8,128)(2,1)S(1)} %get-tuple-element.27.low_ref, bf16[12,512,128]{2,1,0:T(8,128)(2,1)S(1)} %get-tuple-element.28.act, ...), custom_call_target="tpu_custom_call" | custom-call | flops 2000000000 | bytes 1048576 | tf_op jit(solution)/shard_map/pallas_call | solution.py:384
  62.5 1.8 %shard_map.89 = bf16[512,512]{1,0:T(8,128)(2,1)} custom-call(bf16[4,512,128]{2,1,0:T(8,128)(2,1)S(1)} %get-tuple-element.31.qp_ref, f32[4,512,128]{2,1,0:T(8,128)S(1)} %get-tuple-element.32.o_ref, bf16[4,128,256]{2,1,0:T(8,128)(2,1)S(1)} %collective-permute-done.8.other_ref.pair_ref, bf16[2,128,128]{2,1,0:T(8,128)(2,1)S(1)} %shard_map.88.mine_ref, ...), custom_call_target="tpu_custom_call" | custom-call | flops 50000000 | bytes 1048576 | tf_op jit(solution)/shard_map/pallas_call | solution.py:384
  (37 shorter events, 3.0 us)
Async XLA Ops:
  0.8 4.6 %collective-permute-start.5 = (bf16[16,2048]{1,0:T(8,128)(2,1)S(1)}, bf16[16,2048]{1,0:T(8,128)(2,1)S(1)}, u32[]{:S(2)}, u32[]{:S(2)}) collective-permute-start(bf16[16,2048]{1,0:T(8,128)(2,1)S(1)} %slice.12), channel_id=1, source_target_pairs={{3,7},{7,11},{11,15},{15,19},{19,23},{23,27},{27,31}} | collective-permute-start | bytes 196616 | tf_op jit(solution)/shard_map/ppermute | solution.py:68
  1.5 17.7 %collective-permute-start.4 = (bf16[16,2048]{1,0:T(8,128)(2,1)S(1)}, bf16[16,2048]{1,0:T(8,128)(2,1)S(1)}, u32[]{:S(2)}, u32[]{:S(2)}) collective-permute-start(bf16[16,2048]{1,0:T(8,128)(2,1)S(1)} %slice.12), channel_id=1, source_target_pairs={{3,6},{7,10},{11,14},{15,18},{19,22},{23,26},{27,30}} | collective-permute-start | bytes 196616 | tf_op jit(solution)/shard_map/ppermute | solution.py:68
  2.2 17.0 %collective-permute-start.3 = (bf16[16,2048]{1,0:T(8,128)(2,1)S(1)}, bf16[16,2048]{1,0:T(8,128)(2,1)S(1)}, u32[]{:S(2)}, u32[]{:S(2)}) collective-permute-start(bf16[16,2048]{1,0:T(8,128)(2,1)S(1)} %slice.12), channel_id=1, source_target_pairs={{3,5},{7,9},{11,13},{15,17},{19,21},{23,25},{27,29}} | collective-permute-start | bytes 196616 | tf_op jit(solution)/shard_map/ppermute | solution.py:68
  2.9 16.3 %collective-permute-start.2 = (bf16[16,2048]{1,0:T(8,128)(2,1)S(1)}, bf16[16,2048]{1,0:T(8,128)(2,1)S(1)}, u32[]{:S(2)}, u32[]{:S(2)}) collective-permute-start(bf16[16,2048]{1,0:T(8,128)(2,1)S(1)} %slice.12), channel_id=1, source_target_pairs={{3,4},{7,8},{11,12},{15,16},{19,20},{23,24},{27,28}} | collective-permute-start | bytes 196616 | tf_op jit(solution)/shard_map/ppermute | solution.py:68
  4.2 15.1 %collective-permute-start = (bf16[128,2048]{1,0:T(8,128)(2,1)}, bf16[128,2048]{1,0:T(8,128)(2,1)S(1)}, u32[]{:S(2)}, u32[]{:S(2)}) collective-permute-start(bf16[128,2048]{1,0:T(8,128)(2,1)} %refs_0_.1), channel_id=1, source_target_pairs={{0,1},{1,0},{2,3},{3,2},{4,5},{5,4},{6,7},{7,6},{8,9},{9,8},{10,11... | collective-permute-start | bytes 1572872 | tf_op jit(solution)/shard_map/ppermute | solution.py:42
  5.4 18.5 %collective-permute-start.1 = (bf16[128,2048]{1,0:T(8,128)(2,1)}, bf16[128,2048]{1,0:T(8,128)(2,1)S(1)}, u32[]{:S(2)}, u32[]{:S(2)}) collective-permute-start(bf16[128,2048]{1,0:T(8,128)(2,1)} %refs_0_.1), channel_id=1, source_target_pairs={{0,2},{1,3},{2,0},{3,1},{4,6},{5,7},{6,4},{7,5},{8,10},{9,11},{10,... | collective-permute-start | bytes 1572872 | tf_op jit(solution)/shard_map/ppermute | solution.py:42
  11.0 1.1 %copy-start = (bf16[128,2048]{1,0:T(8,128)(2,1)S(1)}, bf16[128,2048]{1,0:T(8,128)(2,1)}, u32[]{:S(2)}) copy-start(bf16[128,2048]{1,0:T(8,128)(2,1)} %refs_0_.1) | copy-start | bytes 1572868
  12.1 2.8 %copy-start.2 = (bf16[2048,3,512]{2,0,1:T(8,128)(2,1)S(1)}, bf16[2048,3,512]{2,0,1:T(8,128)(2,1)}, u32[]{:S(2)}) copy-start(bf16[2048,3,512]{2,0,1:T(8,128)(2,1)} %param.9) | copy-start | bytes 18874372
  14.9 1.6 %copy-start.4 = (bf16[2048,512]{1,0:T(8,128)(2,1)S(1)}, bf16[2048,512]{1,0:T(8,128)(2,1)}, u32[]{:S(2)}) copy-start(bf16[2048,512]{1,0:T(8,128)(2,1)} %gate_w_ref.1) | copy-start | bytes 6291460
  16.5 0.8 %copy-start.6 = (bf16[2048,2,4]{0,2,1:T(4,128)(2,1)S(1)}, bf16[2048,2,4]{0,2,1:T(4,128)(2,1)}, u32[]{:S(2)}) copy-start(bf16[2048,2,4]{0,2,1:T(4,128)(2,1)} %param.11) | copy-start | bytes 98308
  17.2 7.2 %copy-start.3 = (bf16[2048,3,512]{2,0,1:T(8,128)(2,1)S(1)}, bf16[2048,3,512]{2,0,1:T(8,128)(2,1)}, u32[]{:S(2)}) copy-start(bf16[2048,3,512]{2,0,1:T(8,128)(2,1)} %param.9) | copy-start | bytes 18874372
  17.2 7.2 %copy-start.5 = (bf16[2048,512]{1,0:T(8,128)(2,1)S(1)}, bf16[2048,512]{1,0:T(8,128)(2,1)}, u32[]{:S(2)}) copy-start(bf16[2048,512]{1,0:T(8,128)(2,1)} %gate_w_ref.1) | copy-start | bytes 6291460
  19.3 11.2 %collective-permute-start.7 = (bf16[64,2048]{1,0:T(8,128)(2,1)S(1)}, bf16[64,2048]{1,0:T(8,128)(2,1)S(1)}, u32[]{:S(2)}, u32[]{:S(2)}) collective-permute-start(bf16[64,2048]{1,0:T(8,128)(2,1)S(1)} %slice.17), channel_id=1, source_target_pairs={{0,2},{1,3},{2,0},{3,1},{4,6},{5,7},{6,4},{7,5},{8,10},{9,11},{10,... | collective-permute-start | bytes 786440 | tf_op jit(solution)/shard_map/ppermute | solution.py:42
  23.9 7.6 %copy-start.7 = (bf16[2048,2,4]{0,2,1:T(4,128)(2,1)S(1)}, bf16[2048,2,4]{0,2,1:T(4,128)(2,1)}, u32[]{:S(2)}) copy-start(bf16[2048,2,4]{0,2,1:T(4,128)(2,1)} %param.11) | copy-start | bytes 98308
  24.0 7.6 %copy-start.8 = (bf16[4,3,512]{2,0,1:T(4,128)(2,1)S(1)}, bf16[4,3,512]{2,0,1:T(4,128)(2,1)}, u32[]{:S(2)}) copy-start(bf16[4,3,512]{2,0,1:T(4,128)(2,1)} %param.12) | copy-start | bytes 36868
  24.0 7.6 %copy-start.9 = (f32[4]{0:T(128)S(1)}, f32[4]{0:T(128)}, u32[]{:S(2)}) copy-start(f32[4]{0:T(128)} %param.13) | copy-start | bytes 52
  24.0 7.6 %copy-start.10 = (f32[4]{0:T(128)S(1)}, f32[4]{0:T(128)}, u32[]{:S(2)}) copy-start(f32[4]{0:T(128)} %param.14) | copy-start | bytes 52
  24.0 7.5 %collective-permute-start.6 = (bf16[64,2048]{1,0:T(8,128)(2,1)S(1)}, bf16[64,2048]{1,0:T(8,128)(2,1)S(1)}, u32[]{:S(2)}, u32[]{:S(2)}) collective-permute-start(bf16[64,2048]{1,0:T(8,128)(2,1)S(1)} %slice.16), channel_id=1, source_target_pairs={{0,1},{1,0},{2,3},{3,2},{4,5},{5,4},{6,7},{7,6},{8,9},{9,8},{10,11... | collective-permute-start | bytes 786440 | tf_op jit(solution)/shard_map/ppermute | solution.py:42
  42.3 2.5 %collective-permute-start.8 = (bf16[4,128,256]{2,1,0:T(8,128)(2,1)S(1)}, bf16[4,128,256]{2,1,0:T(8,128)(2,1)S(1)}, u32[]{:S(2)}, u32[]{:S(2)}) collective-permute-start(bf16[4,128,256]{2,1,0:T(8,128)(2,1)S(1)} %get-tuple-element.33.mine_ref), channel_id=1, source_target_pairs={{0,4},{4,0},{8,12},{12,8},{16,20},{20,16},{24,28},{28,24},{1,5},{5... | collective-permute-start | bytes 786440 | tf_op jit(solution)/shard_map/ppermute | solution.py:461
  45.0 4.0 %collective-permute-start.9 = (bf16[2,128,256]{2,1,0:T(8,128)(2,1)S(1)}, bf16[2,128,256]{2,1,0:T(8,128)(2,1)S(1)}, u32[]{:S(2)}, u32[]{:S(2)}) collective-permute-start(bf16[2,128,256]{2,1,0:T(8,128)(2,1)S(1)} %shard_map.86.block_ref), channel_id=1, source_target_pairs={{0,8},{4,12},{16,24},{20,28},{1,9},{5,13},{17,25},{21,29},{2,10},{... | collective-permute-start | bytes 393224 | tf_op jit(solution)/shard_map/ppermute | solution.py:478
  49.2 2.2 %collective-permute-start.11 = (bf16[2,128,128]{2,1,0:T(8,128)(2,1)S(1)}, bf16[2,128,128]{2,1,0:T(8,128)(2,1)S(1)}, u32[]{:S(2)}, u32[]{:S(2)}) collective-permute-start(bf16[2,128,128]{2,1,0:T(8,128)(2,1)S(1)} %slice.15), channel_id=1, source_target_pairs={{8,24},{12,28},{9,25},{13,29},{10,26},{14,30},{11,27},{15,31}} | collective-permute-start | bytes 196616 | tf_op jit(solution)/shard_map/ppermute | solution.py:478
  49.9 8.1 %collective-permute-start.10 = (bf16[2,128,128]{2,1,0:T(8,128)(2,1)S(1)}, bf16[2,128,128]{2,1,0:T(8,128)(2,1)S(1)}, u32[]{:S(2)}, u32[]{:S(2)}) collective-permute-start(bf16[2,128,128]{2,1,0:T(8,128)(2,1)S(1)} %slice.15), channel_id=1, source_target_pairs={{8,16},{12,20},{9,17},{13,21},{10,18},{14,22},{11,19},{15,23}} | collective-permute-start | bytes 196616 | tf_op jit(solution)/shard_map/ppermute | solution.py:478
  58.2 4.3 %collective-permute-start.12 = (bf16[2,128,128]{2,1,0:T(8,128)(2,1)S(1)}, bf16[2,128,128]{2,1,0:T(8,128)(2,1)S(1)}, u32[]{:S(2)}, u32[]{:S(2)}) collective-permute-start(bf16[2,128,128]{2,1,0:T(8,128)(2,1)S(1)} %shard_map.88.mine_ref), channel_id=1, source_target_pairs={{0,4},{4,0},{8,12},{12,8},{16,20},{20,16},{24,28},{28,24},{1,5},{5... | collective-permute-start | bytes 196616 | tf_op jit(solution)/shard_map/ppermute | solution.py:492
  59.8 2.7 %copy-start.1 = (f32[128]{0:T(128)S(1)}, f32[128]{0:T(128)}, u32[]{:S(2)}) copy-start(f32[128]{0:T(128)} %param.15) | copy-start | bytes 1540

commit v5 on v4

--- a/solution.py
+++ b/solution.py
@@ -17,6 +17,7 @@
 DELTA_FLOPS = 3000000000
 REACH_FLOPS = 2000000000
 SMALL_FLOPS = 50000000
+MASKS_FLOPS = 8000000000
 
 
 f32 = jnp.float32
@@ -62,12 +63,13 @@
 def rim_rows(block, count):
     seq_count, tp_count = lax.axis_size("seq"), lax.axis_size("tp")
     tail = block[-count:]
-    total = None
+    parts = []
     for j in range(tp_count):
         route = [(s * tp_count - 1, s * tp_count + j) for s in range(1, seq_count)]
-        part = lax.ppermute(tail, ("seq", "tp"), route)
-        total = part if total is None else total + part
-    return total
+        parts.append(lax.ppermute(tail, ("seq", "tp"), route))
+    route = [(i, tp_count - 1 - i) for i in range(tp_count)]
+    across = lax.ppermute(tail, "tp", route)
+    return parts, across
 
 
 def silu(x):
@@ -301,6 +303,265 @@
                 o_ref[head, at] = inner[:, LANES:] + ahead[:, LANES:]
 
 
+def convolve(heads, xp, base, taps_ref, raw, rate, bias, keep):
+    ri, ci = grid_index((CHUNK, CHUNK))
+    taps = taps_ref.shape[1]
+    shifted = raw + bias
+    soft = jnp.maximum(shifted, 0.0) + jnp.log1p(jnp.exp(-jnp.abs(shifted)))
+    decay = dot((ri >= ci).astype(f32), rate * soft, precision=lax.Precision.HIGHEST)
+    beta = 1.0 / (1.0 + jnp.exp(-raw))
+    comb = jnp.where(ci < heads, decay, 0.0)
+    root = 1.0 / math.sqrt(LANES)
+    for head in range(heads):
+        norms = []
+        for branch in range(3):
+            tile = branch * heads + head
+            weights = taps_ref[branch, :, head * LANES:(head + 1) * LANES].astype(f32)
+            total = None
+            for i in range(taps):
+                term = xp[tile, pl.ds(base + (RIM - taps + 1 + i), CHUNK)] * weights[i:i + 1]
+                total = term if total is None else total + term
+            value = silu(total).astype(bf16)
+            keep(tile, value)
+            if branch < 2:
+                wide = value.astype(f32)
+                norms.append(lax.rsqrt(jnp.sum(wide * wide, axis=-1, keepdims=True) + EPS))
+        scaled = beta[:, heads + head:heads + head + 1] * norms[1]
+        comb = jnp.where(ci == heads + head, scaled, comb)
+        comb = jnp.where(ci == 2 * heads + head, norms[0] * root, comb)
+        comb = jnp.where(ci == 3 * heads + head, norms[1], comb)
+    return comb
+
+
+def early_kernel(heads, blocks, *refs):
+    count = blocks + 1
+    tokens_refs, part_ref = refs[:blocks], refs[blocks]
+    w_ref, small_ref, taps_ref, rate_ref, bias_ref = refs[count:count + 5]
+    act, cols, rows_of, raw_ref, raw_sc_ref, rims_ref, xp, tails = refs[count + 5:]
+    early = blocks - 1
+    mid = early * CHUNK
+    me = lax.axis_index("tp")
+    tokens = jnp.concatenate([ref[...] for ref in tokens_refs] + [part_ref[...]], axis=0)
+    raw = dot(tokens[:mid], scalar_weights(small_ref), (1, 1))
+    later = [m for m in range(early) if m != 1]
+    for slot, m in enumerate(later):
+        raw_sc_ref[slot * CHUNK:(slot + 1) * CHUNK] = raw[m * CHUNK:(m + 1) * CHUNK]
+
+    def fill(branch, carry):
+        made = dot(tokens, w_ref[branch]).astype(bf16).astype(f32)
+        for head in range(heads):
+            tile = branch * heads + head
+            lanes = slice(head * LANES, (head + 1) * LANES)
+            for m in range(early):
+                block = made[m * CHUNK:(m + 1) * CHUNK, lanes]
+                if m == 1:
+                    xp[tile, RIM:] = block
+                else:
+                    slot = later.index(m)
+                    raw_ref[tile, slot * CHUNK:(slot + 1) * CHUNK] = block
+                tails[m, tile] = block[CHUNK - RIM:]
+            tails[early, tile] = made[mid:mid + RIM, lanes]
+            tails[blocks, tile] = made[mid + RIM:, lanes]
+        return carry
+
+    lax.fori_loop(0, 3, fill, 0)
+    rate, bias = -lane_row(rate_ref), lane_row(bias_ref)
+
+    def ahead_of(m):
+        index = lax.bitwise_xor(me, m)
+        return jnp.where(index == 0, blocks, lax.bitwise_xor(me, jnp.maximum(index - 1, 0)))
+
+    for slot, m in enumerate(later + [early]):
+        rims_ref[slot] = tails[ahead_of(m)]
+    source = ahead_of(1)
+    for tile in range(3 * heads):
+        xp[tile, :RIM] = tails[source, tile]
+
+    def prepare(slot, carry):
+        def keep(tile, value):
+            act[tile] = value
+
+        base = pl.multiple_of(slot * CHUNK, CHUNK)
+        comb = convolve(heads, xp, base, taps_ref, raw[CHUNK:2 * CHUNK], rate, bias, keep)
+        cols[0] = comb
+        rows_of[0] = comb.T
+        return carry
+
+    prepare(0, 0)
+
+
+def masks_kernel(out_ref):
+    ri, ci = grid_index((CHUNK, CHUNK))
+    for level in range(out_ref.shape[0]):
+        hit = ((ri >> (level + 1)) == (ci >> (level + 1))) & ((ri >> level) > (ci >> level))
+        hit = hit.astype(f32).astype(bf16)
+        out_ref[level] = beside(hit, hit)
+
+
+def block_delta_kernel(
+    heads, blocks, act_e, cols_e, rows_e, raw_ref, raw_sc_ref, rims_ref, late0_ref, late1_ref, *refs
+):
+    me = lax.axis_index("tp")
+    part_refs = refs[:blocks - 1]
+    w_ref, small_ref, taps_ref, rate_ref, bias_ref, masks = refs[blocks - 1:blocks + 5]
+    x_ref, both_ref, low_ref, act_l, cols_l, rows_l = refs[blocks + 5:blocks + 11]
+    xp, sc, mixes, solves, changes, lasts = refs[blocks + 11:]
+    span = RIM + CHUNK
+    slots = blocks - 1
+    before = part_refs[0][...].astype(f32)
+    for ref in part_refs[1:]:
+        before = before + ref[...].astype(f32)
+    tokens = jnp.concatenate([late0_ref[...], late1_ref[...], before.astype(bf16)], axis=0)
+    sc[:(slots - 1) * CHUNK] = raw_sc_ref[...]
+    sc[(slots - 1) * CHUNK:] = dot(tokens[:CHUNK], scalar_weights(small_ref), (1, 1))
+
+    def fill(branch, carry):
+        made = dot(tokens, w_ref[branch]).astype(bf16).astype(f32)
+        for head in range(heads):
+            tile = branch * heads + head
+            lanes = slice(head * LANES, (head + 1) * LANES)
+            rim = made[CHUNK:, lanes]
+            for slot in range(slots):
+                at = slot * span
+                first = me == (slot + 1 if slot else 0)
+                xp[tile, at:at + RIM] = jnp.where(first, rim, rims_ref[slot, tile])
+                if slot == slots - 1:
+                    xp[tile, at + RIM:at + span] = made[:CHUNK, lanes]
+                else:
+                    xp[tile, at + RIM:at + span] = raw_ref[tile, slot * CHUNK:(slot + 1) * CHUNK]
+        return carry
+
+    lax.fori_loop(0, 3, fill, 0)
+    rate, bias = -lane_row(rate_ref), lane_row(bias_ref)
+
+    def prepare(slot, carry):
+        at = pl.ds(pl.multiple_of(slot * CHUNK, CHUNK), CHUNK)
+
+        def keep(tile, value):
+            act_l[tile, at] = value
+
+        base = pl.multiple_of(slot * span, 8)
+        comb = convolve(heads, xp, base, taps_ref, sc[at], rate, bias, keep)
+        cols_l[slot] = comb
+        rows_l[slot] = comb.T
+        return carry
+
+    lax.fori_loop(0, slots, prepare, 0)
+
+    ri, ci = grid_index((CHUNK, CHUNK))
+    levels = masks.shape[0]
+
+    def part(branch, head, m):
+        held, slot = (act_e, 0) if m == 1 else (act_l, max(m - 1, 0))
+        return held[branch * heads + head, slot * CHUNK:(slot + 1) * CHUNK]
+
+    def col(kind, head, m):
+        lane = kind * heads + head
+        held, slot = (cols_e, 0) if m == 1 else (cols_l, max(m - 1, 0))
+        return held[slot, :, lane:lane + 1]
+
+    def row(kind, head, m):
+        lane = kind * heads + head
+        held, slot = (rows_e, 0) if m == 1 else (rows_l, max(m - 1, 0))
+        return held[slot, lane:lane + 1, :]
+
+    for m in range(blocks):
+        held, slot = (cols_e, 0) if m == 1 else (cols_l, max(m - 1, 0))
+        lasts[m] = jnp.exp(held[slot, CHUNK - 8:])
+
+    sets = [(head, m) for m in range(0, blocks, 2) for head in range(heads)]
+    for s, (head, first) in enumerate(sets):
+        two = (first, first + 1)
+        keys = [part(1, head, m) for m in two]
+        gram = dot(beside(*keys), block_diagonal(*[k.T for k in keys]))
+        mix = []
+        for i, m in enumerate(two):
+            lanes = slice(i * LANES, (i + 1) * LANES)
+            gap = col(0, head, m) - row(0, head, m)
+            weight = jnp.exp(jnp.minimum(gap, 0.0)) * row(1, head, m)
+            mix.append((weight * gram[:, lanes] * col(3, head, m)).astype(bf16))
+        mix = beside(*mix)
+        mixes[s] = mix
+        eye = jnp.where(ri == ci, 1.0, 0.0)
+        solves[s] = beside(eye, eye) - (mix * masks[0]).astype(f32)
+    for level in range(1, levels):
+        lows, mids = [], []
+        for s in range(len(sets)):
+            low = solves[s].astype(bf16)
+            lows.append(low)
+            mids.append(dot(mixes[s] * masks[level], block_diagonal(low[:, :LANES], low[:, LANES:])).astype(bf16))
+        for s in range(len(sets)):
+            mid = mids[s]
+            solves[s] = solves[s] - dot(lows[s], block_diagonal(mid[:, :LANES], mid[:, LANES:]))
+    for s, (head, first) in enumerate(sets):
+        two = (first, first + 1)
+        solve = solves[s]
+        new = dot(solve.astype(bf16), block_diagonal(*[part(2, head, m) for m in two]))
+        grown = beside(*[jnp.exp(row(0, head, m)) * row(3, head, m) for m in two])
+        back = dot((solve * grown).astype(bf16), block_diagonal(*[part(1, head, m) for m in two]))
+        for i, m in enumerate(two):
+            lanes = slice(i * LANES, (i + 1) * LANES)
+            both = beside(back[:, lanes], new[:, lanes])
+            decay = col(0, head, m)
+            tail = col(1, head, m) * jnp.exp(decay[CHUNK - 1:] - decay)
+            changes[m, head] = dot(part(1, head, m), (both * tail).astype(bf16), (0, 0))
+            both_ref[head, m] = both.astype(bf16)
+    eye = jnp.where(ri == ci, 1.0, 0.0)
+    runs = {}
+    for step in range(blocks):
+        m = lax.bitwise_xor(me, step)
+        for head in range(heads):
+            last = lasts[m, 7:, head:head + 1]
+            change = changes[m, head]
+            if step == 0:
+                low_ref[head, m] = beside(eye, jnp.zeros_like(eye)).astype(bf16)
+                runs[head] = beside(last * eye - change[:, :LANES], change[:, LANES:])
+            else:
+                low = runs[head].astype(bf16)
+                low_ref[head, m] = low
+                run = last * runs[head] - dot(change[:, :LANES].astype(bf16), low)
+                runs[head] = beside(run[:, :LANES], run[:, LANES:] + change[:, LANES:])
+    for head in range(heads):
+        x_ref[head] = runs[head].astype(bf16)
+
+
+def block_reach_kernel(
+    heads, blocks, both_ref, low_ref, act_e, cols_e, rows_e, act_l, cols_l, rows_l,
+    qp_ref, o_ref,
+):
+    ri, ci = grid_index((CHUNK, CHUNK))
+    upto = ri >= ci
+    for head in range(heads):
+        for m in range(blocks):
+            at = slice(m * CHUNK, (m + 1) * CHUNK)
+            slot = 0 if m == 1 else max(m - 1, 0)
+            act, cols_of, rows_of = (act_e, cols_e, rows_e) if m == 1 else (act_l, cols_l, rows_l)
+            held = slice(slot * CHUNK, (slot + 1) * CHUNK)
+            cols, rows = cols_of[slot], rows_of[slot]
+            q, k = act[head, held], act[heads + head, held]
+            decay = cols[:, head:head + 1]
+            norm = cols[:, 2 * heads + head:2 * heads + head + 1]
+            gap = decay - rows[head:head + 1]
+            weight = jnp.exp(jnp.minimum(gap, 0.0)) * rows[heads + head:heads + head + 1]
+            attend = jnp.where(upto, weight * dot(q, k, (1, 1)) * norm, 0.0).astype(bf16)
+            inner = dot(attend, both_ref[head, m])
+            eff = (jnp.exp(decay) * norm) * q.astype(f32) - inner[:, :LANES]
+            ahead = dot(eff.astype(bf16), low_ref[head, m])
+            qp_ref[head, at] = ahead[:, :LANES].astype(bf16)
+            o_ref[head, at] = inner[:, LANES:] + ahead[:, LANES:]
+
+
+def gate_kernel(count, *refs):
+    w_ref = refs[count]
+    outs = refs[count + 1:]
+    tokens = jnp.concatenate([ref[...] for ref in refs[:count]], axis=0)
+    gate = silu(dot(tokens, w_ref[...]))
+    start = 0
+    for out in outs:
+        out[...] = gate[start:start + out.shape[0]]
+        start += out.shape[0]
+
+
 def pair_kernel(share, mine_ref, other_ref, out_ref):
     core = lax.axis_index("seq") & 1
     for j in range(out_ref.shape[0]):
@@ -351,7 +612,7 @@
 
 
 def final_kernel(
-    share, blocks, qp_ref, o_ref, pair_ref, mine_ref, other_ref,
+    share, blocks, ordered, qp_ref, o_ref, pair_ref, mine_ref, other_ref,
     own_gate_ref, gate_ref, late_gate_ref, gain_ref, out_ref,
 ):
     heads, seq_rows, dim = qp_ref.shape
@@ -374,7 +635,8 @@
             else:
                 gate = late_gate_ref[:, lanes]
             at = pl.ds(pl.multiple_of(lax.bitwise_xor(me, m) * rows, 8), rows)
-            y = o_ref[head, at] + dot(qp_ref[head, at], start)
+            held = at if ordered else slice(m * rows, (m + 1) * rows)
+            y = o_ref[head, held] + dot(qp_ref[head, held], start)
             scale = lax.rsqrt(jnp.mean(y * y, axis=-1, keepdims=True) + EPS)
             out_ref[at, lanes] = (y * scale * gain_ref[...] * gate).astype(bf16)
 
@@ -409,7 +671,6 @@
     rate, bias = decay_rate.reshape(1, heads), dt_bias.reshape(1, heads)
 
     early, late = gather_blocks(hidden, "tp")
-    rim = rim_rows(hidden, RIM)
     weights = [w_three, w_gate, small]
 
     def project(tokens, count, extra=0):
@@ -423,37 +684,111 @@
             [*tokens, *weights], flops=PROJECT_FLOPS, limit=20,
         )
 
-    own_p, own_gate, own_sc = project([hidden], rows)
-    mid_p, mid_gate, mid_sc = project([*early, rim], seq_rows - 2 * rows, RIM)
-    own, both, low, act, cols, rows_of = call(
-        functools.partial(delta_kernel, heads, blocks),
-        (
-            shape((heads, dim, 2 * dim), bf16),
-            shape((heads, chunks, CHUNK, 2 * dim), bf16),
-            shape((heads, chunks - 1, dim, 2 * dim), bf16),
-            shape((3 * heads, seq_rows, dim), bf16),
-            shape((chunks, CHUNK, LANES), f32),
-            shape((chunks, CHUNK, LANES), f32),
-        ),
-        [own_p, own_sc, mid_p, mid_sc, *late, w_three, small, taps, rate, bias],
-        flops=DELTA_FLOPS, limit=32,
-        scratch=[
-            pltpu.VMEM((3 * heads, seq_rows + RIM, dim), f32),
-            pltpu.VMEM((seq_rows, LANES), f32),
-            pltpu.VMEM((CHUNK.bit_length() - 1, CHUNK, 2 * CHUNK), bf16),
-            pltpu.VMEM((heads * chunks // 2, CHUNK, 2 * CHUNK), bf16),
-            pltpu.VMEM((heads * chunks // 2, CHUNK, 2 * CHUNK), f32),
-        ],
-    )
-    reach, base, late_gate = call(
-        functools.partial(reach_kernel, heads),
-        (
-            shape((heads, seq_rows, dim), bf16),
-            shape((heads, seq_rows, dim), f32),
-            shape((rows, columns), f32),
-        ),
-        [both, low, act, cols, rows_of, *late, w_gate], flops=REACH_FLOPS, limit=12,
-    )
+    by_block = rows == CHUNK and len(early) == blocks - 2 and blocks > 2
+    if by_block:
+        parts, across = rim_rows(hidden, RIM)
+        masks = call(
+            masks_kernel,
+            shape((CHUNK.bit_length() - 1, CHUNK, 2 * CHUNK), bf16), [],
+            flops=MASKS_FLOPS, limit=4,
+        )
+        act_e, cols_e, rows_e, raw, raw_sc, rims = call(
+            functools.partial(early_kernel, heads, blocks),
+            (
+                shape((3 * heads, rows, dim), bf16),
+                shape((1, CHUNK, LANES), f32),
+                shape((1, CHUNK, LANES), f32),
+                shape((3 * heads, seq_rows - 2 * rows, dim), f32),
+                shape((seq_rows - 2 * rows, LANES), f32),
+                shape((blocks - 1, 3 * heads, RIM, dim), f32),
+            ),
+            [
+                hidden, *early, across, parts[1],
+                w_three, small, taps, rate, bias,
+            ],
+            flops=PROJECT_FLOPS,
+            scratch=[
+                pltpu.VMEM((3 * heads, RIM + CHUNK, dim), f32),
+                pltpu.VMEM((blocks + 1, 3 * heads, RIM, dim), f32),
+            ],
+        )
+        own, both, low, act_l, cols_l, rows_l = call(
+            functools.partial(block_delta_kernel, heads, blocks),
+            (
+                shape((heads, dim, 2 * dim), bf16),
+                shape((heads, blocks, CHUNK, 2 * dim), bf16),
+                shape((heads, blocks, dim, 2 * dim), bf16),
+                shape((3 * heads, seq_rows - rows, dim), bf16),
+                shape((blocks - 1, CHUNK, LANES), f32),
+                shape((blocks - 1, CHUNK, LANES), f32),
+            ),
+            [
+                act_e, cols_e, rows_e, raw, raw_sc, rims, *late,
+                parts[0], *parts[2:], w_three, small, taps, rate, bias, masks,
+            ],
+            flops=DELTA_FLOPS, limit=28,
+            scratch=[
+                pltpu.VMEM((3 * heads, (blocks - 1) * (RIM + CHUNK), dim), f32),
+                pltpu.VMEM((seq_rows - rows, LANES), f32),
+                pltpu.VMEM((heads * blocks // 2, CHUNK, 2 * CHUNK), bf16),
+                pltpu.VMEM((heads * blocks // 2, CHUNK, 2 * CHUNK), f32),
+                pltpu.VMEM((blocks, heads, dim, 2 * dim), f32),
+                pltpu.VMEM((blocks, 8, LANES), f32),
+            ],
+        )
+        reach, base = call(
+            functools.partial(block_reach_kernel, heads, blocks),
+            (
+                shape((heads, seq_rows, dim), bf16),
+                shape((heads, seq_rows, dim), f32),
+            ),
+            [both, low, act_e, cols_e, rows_e, act_l, cols_l, rows_l],
+            flops=REACH_FLOPS, limit=14,
+        )
+        tokens = [hidden, *early, *late]
+        own_gate, mid_gate, late_gate = call(
+            functools.partial(gate_kernel, len(tokens)),
+            (
+                shape((rows, columns), f32),
+                shape((seq_rows - 2 * rows, columns), f32),
+                shape((rows, columns), f32),
+            ),
+            [*tokens, w_gate], flops=PROJECT_FLOPS, limit=14,
+        )
+    else:
+        own_p, own_gate, own_sc = project([hidden], rows)
+        parts, _ = rim_rows(hidden, RIM)
+        rim = sum(parts[1:], parts[0])
+        mid_p, mid_gate, mid_sc = project([*early, rim], seq_rows - 2 * rows, RIM)
+        own, both, low, act, cols, rows_of = call(
+            functools.partial(delta_kernel, heads, blocks),
+            (
+                shape((heads, dim, 2 * dim), bf16),
+                shape((heads, chunks, CHUNK, 2 * dim), bf16),
+                shape((heads, chunks - 1, dim, 2 * dim), bf16),
+                shape((3 * heads, seq_rows, dim), bf16),
+                shape((chunks, CHUNK, LANES), f32),
+                shape((chunks, CHUNK, LANES), f32),
+            ),
+            [own_p, own_sc, mid_p, mid_sc, *late, w_three, small, taps, rate, bias],
+            flops=DELTA_FLOPS, limit=32,
+            scratch=[
+                pltpu.VMEM((3 * heads, seq_rows + RIM, dim), f32),
+                pltpu.VMEM((seq_rows, LANES), f32),
+                pltpu.VMEM((CHUNK.bit_length() - 1, CHUNK, 2 * CHUNK), bf16),
+                pltpu.VMEM((heads * chunks // 2, CHUNK, 2 * CHUNK), bf16),
+                pltpu.VMEM((heads * chunks // 2, CHUNK, 2 * CHUNK), f32),
+            ],
+        )
+        reach, base, late_gate = call(
+            functools.partial(reach_kernel, heads),
+            (
+                shape((heads, seq_rows, dim), bf16),
+                shape((heads, seq_rows, dim), f32),
+                shape((rows, columns), f32),
+            ),
+            [both, low, act, cols, rows_of, *late, w_gate], flops=REACH_FLOPS, limit=12,
+        )
 
     share = heads % 2 == 0
     part = heads // 2 if share else heads
@@ -491,7 +826,7 @@
     )
     back = lax.ppermute(state, "seq", swap) if share else state
     return call(
-        functools.partial(final_kernel, share, blocks), shape((seq_rows, columns), bf16),
+        functools.partial(final_kernel, share, blocks, not by_block), shape((seq_rows, columns), bf16),
         [reach, base, other, state, back, own_gate, mid_gate, late_gate, norm_gain.reshape(1, dim)],
         flops=SMALL_FLOPS, limit=12,
     )

time: 64.7 us -> 67 us (1.036)
  waiting for transfers between devices: 14.4 us -> 24.8 us
  local copies, waits for them, and re-layouts: 7.13 us -> 1.08 us
  starting transfers between devices: 21.5 us -> 19.1 us
    ppermute x4, waiting for transfers between devices: 3.81 us -> 15.7 us  [swap(): return lax.ppermute(value, axis, [(i, i ^ step) for i in range(count)])]
    ppermute x4, starting transfers between devices: 11.9 us -> 3.29 us  [swap(): return lax.ppermute(value, axis, [(i, i ^ step) for i in range(count)])]
    ppermute x4 -> x5, starting transfers between devices: 3.27 us -> 9.5 us  [the longest x1 5.96 us: rim_rows(): across = lax.ppermute(tail, 'tp', route)]
    unnamed x22 -> x18, local copies, waits for them, and re-layouts: 6.24 us -> 0.04 us
    ppermute x3, waiting for transfers between devices: 9.38 us -> 7.98 us  [per_device(): parts.append(lax.ppermute(sent, 'seq', route))]
    pallas_call x8 -> x9, Pallas kernels: 21 us -> 21.5 us  [call(): pl.pallas_call(kernel, out_shape=out, in_specs=[whole()] * len(operands),...]
  transfers between devices with their start and end apart: 13 -> 14, of which waited for: 5 -> 5; matrix products, arithmetic and copies ran while one was open for 0% -> 0% of each run, Pallas kernels for 12% -> 13%
where the time goes in v5:
time: 67 us; the launch traced here: 66.8 us
  waiting for transfers between devices  24.8 us (37%)
  Pallas kernels  21.5 us (32%)
  starting transfers between devices  19.1 us (29%)
  local copies, waits for them, and re-layouts  1.08 us (2%)
    pallas_call x9, Pallas kernels, call(): pl.pallas_call(kernel, out_shape=out, in_specs=[whole()] * len(operands),...  21.5 us
    ppermute x4, waiting for transfers between devices, swap(): return lax.ppermute(value, axis, [(i, i ^ step) for i in range(count)])  15.7 us
    ppermute x3, waiting for transfers between devices, per_device(): parts.append(lax.ppermute(sent, 'seq', route))  7.98 us
    ppermute x1, starting transfers between devices, rim_rows(): across = lax.ppermute(tail, 'tp', route)  5.96 us
    ppermute x4, starting transfers between devices, rim_rows(): parts.append(lax.ppermute(tail, ('seq', 'tp'), route))  3.54 us
    ppermute x3, starting transfers between devices, per_device(): parts.append(lax.ppermute(sent, 'seq', route))  3.43 us
    ppermute x4, starting transfers between devices, swap(): return lax.ppermute(value, axis, [(i, i ^ step) for i in range(count)])  3.29 us
    ppermute x1, starting transfers between devices, per_device(): back = lax.ppermute(state, 'seq', swap) if share else state  1.57 us
  transfers between devices with their start and end apart: 14, of which 5 were waited for; matrix products, arithmetic and copies ran while one was open for 0% of the time, Pallas kernels for 13%

profile of v5, /device:TPU:17, one launch (start us, length us, event | category | flops | bytes accessed | tf_op | source)
XLA Modules:
  0.0 66.8 jit_solution(7980218491513272263)
XLA Ops:
  0.0 1.0 %slice.12 = bf16[16,2048]{1,0:T(8,128)(2,1)S(1)} slice(bf16[128,2048]{1,0:T(8,128)(2,1)} %refs_0_.3), slice={[112:128], [0:2048]} | slice | bytes 131072 | tf_op jit(solution)/shard_map/slice | solution.py:65
  1.1 0.8 %collective-permute-start.8 = (bf16[16,2048]{1,0:T(8,128)(2,1)S(1)}, bf16[16,2048]{1,0:T(8,128)(2,1)S(1)}, u32[]{:S(2)}, u32[]{:S(2)}) collective-permute-start(bf16[16,2048]{1,0:T(8,128)(2,1)S(1)} %slice.12), channel_id=1, source_target_pairs={{3,7},{7,11},{11,15},{15,19},{19,23},{23,27},{27,31}} | collective-permute-start | bytes 196616 | tf_op jit(solution)/shard_map/ppermute | solution.py:69
  1.9 0.8 %collective-permute-start.3 = (bf16[16,2048]{1,0:T(8,128)(2,1)S(1)}, bf16[16,2048]{1,0:T(8,128)(2,1)S(1)}, u32[]{:S(2)}, u32[]{:S(2)}) collective-permute-start(bf16[16,2048]{1,0:T(8,128)(2,1)S(1)} %slice.12), channel_id=1, source_target_pairs={{3,5},{7,9},{11,13},{15,17},{19,21},{23,25},{27,29}} | collective-permute-start | bytes 196616 | tf_op jit(solution)/shard_map/ppermute | solution.py:69
  2.7 6.0 %collective-permute-start.2 = (bf16[16,2048]{1,0:T(8,128)(2,1)S(1)}, bf16[16,2048]{1,0:T(8,128)(2,1)S(1)}, u32[]{:S(2)}, u32[]{:S(2)}) collective-permute-start(bf16[16,2048]{1,0:T(8,128)(2,1)S(1)} %slice.12), channel_id=1, source_target_pairs={{0,3},{1,2},{2,1},{3,0},{4,7},{5,6},{6,5},{7,4},{8,11},{9,10},{10,... | collective-permute-start | bytes 196616 | tf_op jit(solution)/shard_map/ppermute | solution.py:71
  8.6 0.4 collective-permute-start
  9.1 13.0 %collective-permute-done.1.refs_2_ = bf16[128,2048]{1,0:T(8,128)(2,1)S(1)} collective-permute-done((bf16[128,2048]{1,0:T(8,128)(2,1)}, bf16[128,2048]{1,0:T(8,128)(2,1)S(1)}, u32[]{:S(2)}, u32[]{:S(2)}) %collective-permute-start.1) | collective-permute-done | bytes 524320 | tf_op jit(solution)/shard_map/ppermute | solution.py:43
  22.1 0.7 collective-permute-start.7
  22.8 1.3 %collective-permute-start.6 = (bf16[16,2048]{1,0:T(8,128)(2,1)S(1)}, bf16[16,2048]{1,0:T(8,128)(2,1)S(1)}, u32[]{:S(2)}, u32[]{:S(2)}) collective-permute-start(bf16[16,2048]{1,0:T(8,128)(2,1)S(1)} %slice.12), channel_id=1, source_target_pairs={{3,4},{7,8},{11,12},{15,16},{19,20},{23,24},{27,28}} | collective-permute-start | bytes 196616 | tf_op jit(solution)/shard_map/ppermute | solution.py:69
  24.2 2.9 %collective-permute-start.5 = (bf16[64,2048]{1,0:T(8,128)(2,1)S(1)}, bf16[64,2048]{1,0:T(8,128)(2,1)S(1)}, u32[]{:S(2)}, u32[]{:S(2)}) collective-permute-start(bf16[64,2048]{1,0:T(8,128)(2,1)S(1)} %slice.17), channel_id=1, source_target_pairs={{0,2},{1,3},{2,0},{3,1},{4,6},{5,7},{6,4},{7,5},{8,10},{9,11},{10,... | collective-permute-start | bytes 786440 | tf_op jit(solution)/shard_map/ppermute | solution.py:43
  27.1 4.6 %shard_map.82 = (bf16[12,128,128]{2,1,0:T(8,128)(2,1)S(1)}, f32[1,128,128]{2,1,0:T(8,128)S(1)}, f32[1,128,128]{2,1,0:T(8,128)S(1)}, f32[12,256,128]{2,1,0:T(8,12...) custom-call(bf16[128,2048]{1,0:T(8,128)(2,1)S(1)} %copy-done, ...), custom_call_target="tpu_custom_call" | custom-call | flops 3000000000 | bytes 1048576 | tf_op jit(solution)/shard_map/pallas_call | solution.py:646
  31.8 2.7 %collective-permute-done.5.late1_ref.refs_4_ = bf16[64,2048]{1,0:T(8,128)(2,1)S(1)} collective-permute-done((bf16[64,2048]{1,0:T(8,128)(2,1)S(1)}, bf16[64,2048]{1,0:T(8,128)(2,1)S(1)}, u32[]{:S(2)}, u32[]{:S(2)}) %collective-permute-start.5) | collective-permute-done | bytes 262176 | tf_op jit(solution)/shard_map/ppermute | solution.py:43
  34.4 10.3 %shard_map.84 = (bf16[4,128,256]{2,1,0:T(8,128)(2,1)S(1)}, bf16[4,4,128,256]{3,2,1,0:T(8,128)(2,1)S(1)}, bf16[4,4,128,256]{3,2,1,0:T(8,128)(2,1)S(1)}, bf16[12,3...) custom-call(bf16[12,128,128]{2,1,0:T(8,128)(2,1)S(1)} %get-tuple-element.24.act_e, ...), custom_call_target="tpu_custom_call" | custom-call | flops 3000000000 | bytes 1048576 | tf_op jit(solution)/shard_map/pallas_call | solution.py:646
  44.7 1.3 %collective-permute-start.9 = (bf16[4,128,256]{2,1,0:T(8,128)(2,1)S(1)}, bf16[4,128,256]{2,1,0:T(8,128)(2,1)S(1)}, u32[]{:S(2)}, u32[]{:S(2)}) collective-permute-start(bf16[4,128,256]{2,1,0:T(8,128)(2,1)S(1)} %get-tuple-element.37.mine_ref), channel_id=1, source_target_pairs={{0,4},{4,0},{8,12},{12,8},{16,20},{20,16},{24,28},{28,24},{1,5},{5... | collective-permute-start | bytes 786440 | tf_op jit(solution)/shard_map/ppermute | solution.py:796
  46.0 1.2 %collective-permute-done.9.other_ref.pair_ref = bf16[4,128,256]{2,1,0:T(8,128)(2,1)S(1)} collective-permute-done((bf16[4,128,256]{2,1,0:T(8,128)(2,1)S(1)}, bf16[4,128,256]{2,1,0:T(8,128)(2,1)S(1)}, u32[]{:S(2)}, u32[]{:S(2)}) %collective-permute-start.9) | collective-permute-done | bytes 262176 | tf_op jit(solution)/shard_map/ppermute | solution.py:796
  47.4 1.3 %collective-permute-start.10 = (bf16[2,128,256]{2,1,0:T(8,128)(2,1)S(1)}, bf16[2,128,256]{2,1,0:T(8,128)(2,1)S(1)}, u32[]{:S(2)}, u32[]{:S(2)}) collective-permute-start(bf16[2,128,256]{2,1,0:T(8,128)(2,1)S(1)} %shard_map.86.block_ref), channel_id=1, source_target_pairs={{0,8},{4,12},{16,24},{20,28},{1,9},{5,13},{17,25},{21,29},{2,10},{... | collective-permute-start | bytes 393224 | tf_op jit(solution)/shard_map/ppermute | solution.py:813
  48.7 2.7 %collective-permute-done.10.sent_ref = bf16[2,128,256]{2,1,0:T(8,128)(2,1)S(1)} collective-permute-done((bf16[2,128,256]{2,1,0:T(8,128)(2,1)S(1)}, bf16[2,128,256]{2,1,0:T(8,128)(2,1)S(1)}, u32[]{:S(2)}, u32[]{:S(2)}) %collective-permute-start.10) | collective-permute-done | bytes 131104 | tf_op jit(solution)/shard_map/ppermute | solution.py:813
  51.4 0.2 shard_map.87
  51.6 0.7 collective-permute-start.12
  52.3 1.5 %collective-permute-start.11 = (bf16[2,128,128]{2,1,0:T(8,128)(2,1)S(1)}, bf16[2,128,128]{2,1,0:T(8,128)(2,1)S(1)}, u32[]{:S(2)}, u32[]{:S(2)}) collective-permute-start(bf16[2,128,128]{2,1,0:T(8,128)(2,1)S(1)} %slice.15), channel_id=1, source_target_pairs={{8,16},{12,20},{9,17},{13,21},{10,18},{14,22},{11,19},{15,23}} | collective-permute-start | bytes 196616 | tf_op jit(solution)/shard_map/ppermute | solution.py:813
  53.8 1.4 %shard_map.89 = (f32[128,512]{1,0:T(8,128)S(1)}, f32[256,512]{1,0:T(8,128)S(1)}, f32[128,512]{1,0:T(8,128)S(1)}) custom-call(bf16[128,2048]{1,0:T(8,128)(2,1)S(1)} %copy-done, bf16[128,2048]{1,0:T(8,128)(2,1)S(1)} %collective-permute-done.refs_1_, bf16[128,2048]{1,0:T(8,128)(2,1)S(1)} %collective-permute-done.1.refs_2_, ...), custom_call_target="tpu_custom_call" | custom-call | flops 3000000000 | bytes 1048576 | tf_op jit(solution)/shard_map/pallas_call | solution.py:646
  55.2 5.2 %collective-permute-done.11.refs_0_ = bf16[2,128,128]{2,1,0:T(8,128)(2,1)S(1)} collective-permute-done((bf16[2,128,128]{2,1,0:T(8,128)(2,1)S(1)}, bf16[2,128,128]{2,1,0:T(8,128)(2,1)S(1)}, u32[]{:S(2)}, u32[]{:S(2)}) %collective-permute-start.11) | collective-permute-done | bytes 65568 | tf_op jit(solution)/shard_map/ppermute | solution.py:813
  60.6 1.6 %collective-permute-start.13 = (bf16[2,128,128]{2,1,0:T(8,128)(2,1)S(1)}, bf16[2,128,128]{2,1,0:T(8,128)(2,1)S(1)}, u32[]{:S(2)}, u32[]{:S(2)}) collective-permute-start(bf16[2,128,128]{2,1,0:T(8,128)(2,1)S(1)} %shard_map.88.mine_ref), channel_id=1, source_target_pairs={{0,4},{4,0},{8,12},{12,8},{16,20},{20,16},{24,28},{28,24},{1,5},{5... | collective-permute-start | bytes 196616 | tf_op jit(solution)/shard_map/ppermute | solution.py:827
  62.2 2.8 %shard_map.85 = (bf16[4,512,128]{2,1,0:T(8,128)(2,1)S(1)}, f32[4,512,128]{2,1,0:T(8,128)S(1)}) custom-call(bf16[4,4,128,256]{3,2,1,0:T(8,128)(2,1)S(1)} %get-tuple-element.30.both_ref, bf16[4,4,128,256]{3,2,1,0:T(8,128)(2,1)S(1)} %get-tuple-element.31.low_ref, bf16[12,128,128]{2,1,0:T(8,128)(2,1)S(1)} %get-tuple-element.24.act_e, ...), custom_call_target="tpu_custom_call" | custom-call | flops 2000000000 | bytes 1048576 | tf_op jit(solution)/shard_map/pallas_call | solution.py:646
  65.0 1.8 %shard_map.90 = bf16[512,512]{1,0:T(8,128)(2,1)} custom-call(bf16[4,512,128]{2,1,0:T(8,128)(2,1)S(1)} %get-tuple-element.35.qp_ref, f32[4,512,128]{2,1,0:T(8,128)S(1)} %get-tuple-element.36.o_ref, bf16[4,128,256]{2,1,0:T(8,128)(2,1)S(1)} %collective-permute-done.9.other_ref.pair_ref, bf16[2,128,128]{2,1,0:T(8,128)(2,1)S(1)} %shard_map.88.mine_ref, ...), custom_call_target="tpu_custom_call" | custom-call | flops 50000000 | bytes 1048576 | tf_op jit(solution)/shard_map/pallas_call | solution.py:646
  (36 shorter events, 0.6 us)
Async XLA Ops:
  0.0 27.0 %slice-start = ((s8[6291456]{0:T(1024)(128)(4,1)}), s8[4194304]{0:T(1024)(128)(4,1)S(1)}, s32[]{:S(2)}) async-start(s8[6291456]{0:T(1024)(128)(4,1)} %bitcast.7), calls=%async_computation | async-start | bytes 8388608
  1.0 26.0 %copy-start = (bf16[128,2048]{1,0:T(8,128)(2,1)S(1)}, bf16[128,2048]{1,0:T(8,128)(2,1)}, u32[]{:S(2)}) copy-start(bf16[128,2048]{1,0:T(8,128)(2,1)} %refs_0_.3) | copy-start | bytes 1572868
  1.0 26.0 %slice-start.1 = ((s8[6291456]{0:T(1024)(128)(4,1)}), s8[2097152]{0:T(1024)(128)(4,1)S(1)}, s32[]{:S(2)}) async-start(s8[6291456]{0:T(1024)(128)(4,1)} %bitcast.7), calls=%async_computation.1 | async-start | bytes 4194304
  1.0 26.0 %copy-start.3 = (bf16[2048,2,4]{0,2,1:T(4,128)(2,1)S(1)}, bf16[2048,2,4]{0,2,1:T(4,128)(2,1)}, u32[]{:S(2)}) copy-start(bf16[2048,2,4]{0,2,1:T(4,128)(2,1)} %param.11) | copy-start | bytes 98308
  1.0 26.0 %copy-start.4 = (bf16[4,3,512]{2,0,1:T(4,128)(2,1)S(1)}, bf16[4,3,512]{2,0,1:T(4,128)(2,1)}, u32[]{:S(2)}) copy-start(bf16[4,3,512]{2,0,1:T(4,128)(2,1)} %param.12) | copy-start | bytes 36868
  1.0 26.0 %copy-start.5 = (f32[4]{0:T(128)S(1)}, f32[4]{0:T(128)}, u32[]{:S(2)}) copy-start(f32[4]{0:T(128)} %param.13) | copy-start | bytes 52
  1.0 26.0 %copy-start.6 = (f32[4]{0:T(128)S(1)}, f32[4]{0:T(128)}, u32[]{:S(2)}) copy-start(f32[4]{0:T(128)} %param.14) | copy-start | bytes 52
  1.1 30.7 %collective-permute-start.8 = (bf16[16,2048]{1,0:T(8,128)(2,1)S(1)}, bf16[16,2048]{1,0:T(8,128)(2,1)S(1)}, u32[]{:S(2)}, u32[]{:S(2)}) collective-permute-start(bf16[16,2048]{1,0:T(8,128)(2,1)S(1)} %slice.12), channel_id=1, source_target_pairs={{3,7},{7,11},{11,15},{15,19},{19,23},{23,27},{27,31}} | collective-permute-start | bytes 196616 | tf_op jit(solution)/shard_map/ppermute | solution.py:69
  1.9 22.2 %collective-permute-start.3 = (bf16[16,2048]{1,0:T(8,128)(2,1)S(1)}, bf16[16,2048]{1,0:T(8,128)(2,1)S(1)}, u32[]{:S(2)}, u32[]{:S(2)}) collective-permute-start(bf16[16,2048]{1,0:T(8,128)(2,1)S(1)} %slice.12), channel_id=1, source_target_pairs={{3,5},{7,9},{11,13},{15,17},{19,21},{23,25},{27,29}} | collective-permute-start | bytes 196616 | tf_op jit(solution)/shard_map/ppermute | solution.py:69
  2.7 21.5 %collective-permute-start.2 = (bf16[16,2048]{1,0:T(8,128)(2,1)S(1)}, bf16[16,2048]{1,0:T(8,128)(2,1)S(1)}, u32[]{:S(2)}, u32[]{:S(2)}) collective-permute-start(bf16[16,2048]{1,0:T(8,128)(2,1)S(1)} %slice.12), channel_id=1, source_target_pairs={{0,3},{1,2},{2,1},{3,0},{4,7},{5,6},{6,5},{7,4},{8,11},{9,10},{10,... | collective-permute-start | bytes 196616 | tf_op jit(solution)/shard_map/ppermute | solution.py:71
  8.6 13.4 %collective-permute-start.1 = (bf16[128,2048]{1,0:T(8,128)(2,1)}, bf16[128,2048]{1,0:T(8,128)(2,1)S(1)}, u32[]{:S(2)}, u32[]{:S(2)}) collective-permute-start(bf16[128,2048]{1,0:T(8,128)(2,1)} %refs_0_.3), channel_id=1, source_target_pairs={{0,2},{1,3},{2,0},{3,1},{4,6},{5,7},{6,4},{7,5},{8,10},{9,11},{10,... | collective-permute-start | bytes 1572872 | tf_op jit(solution)/shard_map/ppermute | solution.py:43
  8.6 14.1 %collective-permute-start = (bf16[128,2048]{1,0:T(8,128)(2,1)}, bf16[128,2048]{1,0:T(8,128)(2,1)S(1)}, u32[]{:S(2)}, u32[]{:S(2)}) collective-permute-start(bf16[128,2048]{1,0:T(8,128)(2,1)} %refs_0_.3), channel_id=1, source_target_pairs={{0,1},{1,0},{2,3},{3,2},{4,5},{5,4},{6,7},{7,6},{8,9},{9,8},{10,11... | collective-permute-start | bytes 1572872 | tf_op jit(solution)/shard_map/ppermute | solution.py:43
  22.1 9.7 %collective-permute-start.7 = (bf16[16,2048]{1,0:T(8,128)(2,1)S(1)}, bf16[16,2048]{1,0:T(8,128)(2,1)S(1)}, u32[]{:S(2)}, u32[]{:S(2)}) collective-permute-start(bf16[16,2048]{1,0:T(8,128)(2,1)S(1)} %slice.12), channel_id=1, source_target_pairs={{3,6},{7,10},{11,14},{15,18},{19,22},{23,26},{27,30}} | collective-permute-start | bytes 196616 | tf_op jit(solution)/shard_map/ppermute | solution.py:69
  22.8 9.0 %collective-permute-start.6 = (bf16[16,2048]{1,0:T(8,128)(2,1)S(1)}, bf16[16,2048]{1,0:T(8,128)(2,1)S(1)}, u32[]{:S(2)}, u32[]{:S(2)}) collective-permute-start(bf16[16,2048]{1,0:T(8,128)(2,1)S(1)} %slice.12), channel_id=1, source_target_pairs={{3,4},{7,8},{11,12},{15,16},{19,20},{23,24},{27,28}} | collective-permute-start | bytes 196616 | tf_op jit(solution)/shard_map/ppermute | solution.py:69
  24.1 7.7 %collective-permute-start.4 = (bf16[64,2048]{1,0:T(8,128)(2,1)S(1)}, bf16[64,2048]{1,0:T(8,128)(2,1)S(1)}, u32[]{:S(2)}, u32[]{:S(2)}) collective-permute-start(bf16[64,2048]{1,0:T(8,128)(2,1)S(1)} %slice.16), channel_id=1, source_target_pairs={{0,1},{1,0},{2,3},{3,2},{4,5},{5,4},{6,7},{7,6},{8,9},{9,8},{10,11... | collective-permute-start | bytes 786440 | tf_op jit(solution)/shard_map/ppermute | solution.py:43
  24.2 10.3 %collective-permute-start.5 = (bf16[64,2048]{1,0:T(8,128)(2,1)S(1)}, bf16[64,2048]{1,0:T(8,128)(2,1)S(1)}, u32[]{:S(2)}, u32[]{:S(2)}) collective-permute-start(bf16[64,2048]{1,0:T(8,128)(2,1)S(1)} %slice.17), channel_id=1, source_target_pairs={{0,2},{1,3},{2,0},{3,1},{4,6},{5,7},{6,4},{7,5},{8,10},{9,11},{10,... | collective-permute-start | bytes 786440 | tf_op jit(solution)/shard_map/ppermute | solution.py:43
  34.4 19.4 %copy-start.2 = (bf16[2048,512]{1,0:T(8,128)(2,1)S(1)}, bf16[2048,512]{1,0:T(8,128)(2,1)}, u32[]{:S(2)}) copy-start(bf16[2048,512]{1,0:T(8,128)(2,1)} %refs_5_.1) | copy-start | bytes 6291460
  44.7 2.5 %collective-permute-start.9 = (bf16[4,128,256]{2,1,0:T(8,128)(2,1)S(1)}, bf16[4,128,256]{2,1,0:T(8,128)(2,1)S(1)}, u32[]{:S(2)}, u32[]{:S(2)}) collective-permute-start(bf16[4,128,256]{2,1,0:T(8,128)(2,1)S(1)} %get-tuple-element.37.mine_ref), channel_id=1, source_target_pairs={{0,4},{4,0},{8,12},{12,8},{16,20},{20,16},{24,28},{28,24},{1,5},{5... | collective-permute-start | bytes 786440 | tf_op jit(solution)/shard_map/ppermute | solution.py:796
  47.4 4.0 %collective-permute-start.10 = (bf16[2,128,256]{2,1,0:T(8,128)(2,1)S(1)}, bf16[2,128,256]{2,1,0:T(8,128)(2,1)S(1)}, u32[]{:S(2)}, u32[]{:S(2)}) collective-permute-start(bf16[2,128,256]{2,1,0:T(8,128)(2,1)S(1)} %shard_map.86.block_ref), channel_id=1, source_target_pairs={{0,8},{4,12},{16,24},{20,28},{1,9},{5,13},{17,25},{21,29},{2,10},{... | collective-permute-start | bytes 393224 | tf_op jit(solution)/shard_map/ppermute | solution.py:813
  51.6 3.6 %collective-permute-start.12 = (bf16[2,128,128]{2,1,0:T(8,128)(2,1)S(1)}, bf16[2,128,128]{2,1,0:T(8,128)(2,1)S(1)}, u32[]{:S(2)}, u32[]{:S(2)}) collective-permute-start(bf16[2,128,128]{2,1,0:T(8,128)(2,1)S(1)} %slice.15), channel_id=1, source_target_pairs={{8,24},{12,28},{9,25},{13,29},{10,26},{14,30},{11,27},{15,31}} | collective-permute-start | bytes 196616 | tf_op jit(solution)/shard_map/ppermute | solution.py:813
  52.3 8.1 %collective-permute-start.11 = (bf16[2,128,128]{2,1,0:T(8,128)(2,1)S(1)}, bf16[2,128,128]{2,1,0:T(8,128)(2,1)S(1)}, u32[]{:S(2)}, u32[]{:S(2)}) collective-permute-start(bf16[2,128,128]{2,1,0:T(8,128)(2,1)S(1)} %slice.15), channel_id=1, source_target_pairs={{8,16},{12,20},{9,17},{13,21},{10,18},{14,22},{11,19},{15,23}} | collective-permute-start | bytes 196616 | tf_op jit(solution)/shard_map/ppermute | solution.py:813
  60.6 4.3 %collective-permute-start.13 = (bf16[2,128,128]{2,1,0:T(8,128)(2,1)S(1)}, bf16[2,128,128]{2,1,0:T(8,128)(2,1)S(1)}, u32[]{:S(2)}, u32[]{:S(2)}) collective-permute-start(bf16[2,128,128]{2,1,0:T(8,128)(2,1)S(1)} %shard_map.88.mine_ref), channel_id=1, source_target_pairs={{0,4},{4,0},{8,12},{12,8},{16,20},{20,16},{24,28},{28,24},{1,5},{5... | collective-permute-start | bytes 196616 | tf_op jit(solution)/shard_map/ppermute | solution.py:827
  62.2 2.8 %copy-start.1 = (f32[128]{0:T(128)S(1)}, f32[128]{0:T(128)}, u32[]{:S(2)}) copy-start(f32[128]{0:T(128)} %param.15) | copy-start | bytes 1540

commit v6 on v5

--- a/solution.py
+++ b/solution.py
@@ -11,7 +11,7 @@
 
 CHUNK = 128
 LANES = 128
-RIM = 16
+RIM = 8
 EPS = 1e-6
 PROJECT_FLOPS = 3000000000
 DELTA_FLOPS = 3000000000
@@ -341,7 +341,8 @@
     early = blocks - 1
     mid = early * CHUNK
     me = lax.axis_index("tp")
-    tokens = jnp.concatenate([ref[...] for ref in tokens_refs] + [part_ref[...]], axis=0)
+    edge = jnp.concatenate([tokens_refs[-1][...].astype(f32), part_ref[...].astype(f32)], axis=0)
+    tokens = jnp.concatenate([ref[...] for ref in tokens_refs[:-1]] + [edge.astype(bf16)], axis=0)
     raw = dot(tokens[:mid], scalar_weights(small_ref), (1, 1))
     later = [m for m in range(early) if m != 1]
     for slot, m in enumerate(later):
@@ -411,6 +412,7 @@
     before = part_refs[0][...].astype(f32)
     for ref in part_refs[1:]:
         before = before + ref[...].astype(f32)
+    before = jnp.concatenate([before, jnp.zeros_like(before)], axis=0)
     tokens = jnp.concatenate([late0_ref[...], late1_ref[...], before.astype(bf16)], axis=0)
     sc[:(slots - 1) * CHUNK] = raw_sc_ref[...]
     sc[(slots - 1) * CHUNK:] = dot(tokens[:CHUNK], scalar_weights(small_ref), (1, 1))
@@ -420,7 +422,7 @@
         for head in range(heads):
             tile = branch * heads + head
             lanes = slice(head * LANES, (head + 1) * LANES)
-            rim = made[CHUNK:, lanes]
+            rim = made[CHUNK:CHUNK + RIM, lanes]
             for slot in range(slots):
                 at = slot * span
                 first = me == (slot + 1 if slot else 0)

time: 67 us -> 65.9 us (0.984)
  the two profiles are of different devices: /device:TPU:17 before, /device:TPU:21 now
where the time goes in v6:
time: 65.9 us; the launch traced here: 65.7 us
  waiting for transfers between devices  24 us (36%)
  Pallas kernels  21.4 us (32%)
  starting transfers between devices  19.1 us (29%)
  local copies, waits for them, and re-layouts  1 us (2%)
    pallas_call x9, Pallas kernels, call(): pl.pallas_call(kernel, out_shape=out, in_specs=[whole()] * len(operands),...  21.4 us
    ppermute x4, waiting for transfers between devices, swap(): return lax.ppermute(value, axis, [(i, i ^ step) for i in range(count)])  14.3 us
    ppermute x3, waiting for transfers between devices, per_device(): parts.append(lax.ppermute(sent, 'seq', route))  8.52 us
    ppermute x4, starting transfers between devices, swap(): return lax.ppermute(value, axis, [(i, i ^ step) for i in range(count)])  6.39 us
    ppermute x4, starting transfers between devices, rim_rows(): parts.append(lax.ppermute(tail, ('seq', 'tp'), route))  3.52 us
    ppermute x3, starting transfers between devices, per_device(): parts.append(lax.ppermute(sent, 'seq', route))  3.43 us
    ppermute x1, starting transfers between devices, per_device(): other = lax.ppermute(own, 'seq', swap)  2.33 us
    ppermute x1, starting transfers between devices, rim_rows(): across = lax.ppermute(tail, 'tp', route)  1.85 us
  transfers between devices with their start and end apart: 14, of which 7 were waited for; matrix products, arithmetic and copies ran while one was open for 0% of the time, Pallas kernels for 13%

profile of v6, /device:TPU:21, one launch (start us, length us, event | category | flops | bytes accessed | tf_op | source)
XLA Modules:
  0.0 65.7 jit_solution(13700530002918333653)
XLA Ops:
  0.0 0.9 %slice.12 = bf16[8,2048]{1,0:T(8,128)(2,1)S(1)} slice(bf16[128,2048]{1,0:T(8,128)(2,1)} %refs_0_.3), slice={[120:128], [0:2048]} | slice | bytes 65536 | tf_op jit(solution)/shard_map/slice | solution.py:65
  1.0 0.8 %collective-permute-start.8 = (bf16[8,2048]{1,0:T(8,128)(2,1)S(1)}, bf16[8,2048]{1,0:T(8,128)(2,1)S(1)}, u32[]{:S(2)}, u32[]{:S(2)}) collective-permute-start(bf16[8,2048]{1,0:T(8,128)(2,1)S(1)} %slice.12), channel_id=1, source_target_pairs={{3,7},{7,11},{11,15},{15,19},{19,23},{23,27},{27,31}} | collective-permute-start | bytes 98312 | tf_op jit(solution)/shard_map/ppermute | solution.py:69
  1.8 0.8 %collective-permute-start.3 = (bf16[8,2048]{1,0:T(8,128)(2,1)S(1)}, bf16[8,2048]{1,0:T(8,128)(2,1)S(1)}, u32[]{:S(2)}, u32[]{:S(2)}) collective-permute-start(bf16[8,2048]{1,0:T(8,128)(2,1)S(1)} %slice.12), channel_id=1, source_target_pairs={{3,5},{7,9},{11,13},{15,17},{19,21},{23,25},{27,29}} | collective-permute-start | bytes 98312 | tf_op jit(solution)/shard_map/ppermute | solution.py:69
  2.6 1.8 %collective-permute-start.2 = (bf16[8,2048]{1,0:T(8,128)(2,1)S(1)}, bf16[8,2048]{1,0:T(8,128)(2,1)S(1)}, u32[]{:S(2)}, u32[]{:S(2)}) collective-permute-start(bf16[8,2048]{1,0:T(8,128)(2,1)S(1)} %slice.12), channel_id=1, source_target_pairs={{0,3},{1,2},{2,1},{3,0},{4,7},{5,6},{6,5},{7,4},{8,11},{9,10},{10,... | collective-permute-start | bytes 98312 | tf_op jit(solution)/shard_map/ppermute | solution.py:71
  4.4 4.3 %collective-permute-start.1 = (bf16[128,2048]{1,0:T(8,128)(2,1)}, bf16[128,2048]{1,0:T(8,128)(2,1)S(1)}, u32[]{:S(2)}, u32[]{:S(2)}) collective-permute-start(bf16[128,2048]{1,0:T(8,128)(2,1)} %refs_0_.3), channel_id=1, source_target_pairs={{0,2},{1,3},{2,0},{3,1},{4,6},{5,7},{6,4},{7,5},{8,10},{9,11},{10,... | collective-permute-start | bytes 1572872 | tf_op jit(solution)/shard_map/ppermute | solution.py:43
  8.9 11.9 %collective-permute-done.1.refs_2_ = bf16[128,2048]{1,0:T(8,128)(2,1)S(1)} collective-permute-done((bf16[128,2048]{1,0:T(8,128)(2,1)}, bf16[128,2048]{1,0:T(8,128)(2,1)S(1)}, u32[]{:S(2)}, u32[]{:S(2)}) %collective-permute-start.1) | collective-permute-done | bytes 524320 | tf_op jit(solution)/shard_map/ppermute | solution.py:43
  20.7 1.3 %collective-permute-start.7 = (bf16[8,2048]{1,0:T(8,128)(2,1)S(1)}, bf16[8,2048]{1,0:T(8,128)(2,1)S(1)}, u32[]{:S(2)}, u32[]{:S(2)}) collective-permute-start(bf16[8,2048]{1,0:T(8,128)(2,1)S(1)} %slice.12), channel_id=1, source_target_pairs={{3,6},{7,10},{11,14},{15,18},{19,22},{23,26},{27,30}} | collective-permute-start | bytes 98312 | tf_op jit(solution)/shard_map/ppermute | solution.py:69
  22.1 0.6 collective-permute-done.refs_1_
  22.6 0.7 collective-permute-start.6
  23.3 2.0 %collective-permute-start.4 = (bf16[64,2048]{1,0:T(8,128)(2,1)S(1)}, bf16[64,2048]{1,0:T(8,128)(2,1)S(1)}, u32[]{:S(2)}, u32[]{:S(2)}) collective-permute-start(bf16[64,2048]{1,0:T(8,128)(2,1)S(1)} %slice.16), channel_id=1, source_target_pairs={{0,1},{1,0},{2,3},{3,2},{4,5},{5,4},{6,7},{7,6},{8,9},{9,8},{10,11... | collective-permute-start | bytes 786440 | tf_op jit(solution)/shard_map/ppermute | solution.py:43
  25.4 4.5 %shard_map.82 = (bf16[12,128,128]{2,1,0:T(8,128)(2,1)S(1)}, f32[1,128,128]{2,1,0:T(8,128)S(1)}, f32[1,128,128]{2,1,0:T(8,128)S(1)}, f32[12,256,128]{2,1,0:T(8,12...) custom-call(bf16[128,2048]{1,0:T(8,128)(2,1)S(1)} %copy-done, ...), custom_call_target="tpu_custom_call" | custom-call | flops 3000000000 | bytes 1048576 | tf_op jit(solution)/shard_map/pallas_call | solution.py:648
  30.0 1.4 %collective-permute-done.4.late0_ref.refs_3_ = bf16[64,2048]{1,0:T(8,128)(2,1)S(1)} collective-permute-done((bf16[64,2048]{1,0:T(8,128)(2,1)S(1)}, bf16[64,2048]{1,0:T(8,128)(2,1)S(1)}, u32[]{:S(2)}, u32[]{:S(2)}) %collective-permute-start.4) | collective-permute-done | bytes 262176 | tf_op jit(solution)/shard_map/ppermute | solution.py:43
  31.8 10.3 %shard_map.84 = (bf16[4,128,256]{2,1,0:T(8,128)(2,1)S(1)}, bf16[4,4,128,256]{3,2,1,0:T(8,128)(2,1)S(1)}, bf16[4,4,128,256]{3,2,1,0:T(8,128)(2,1)S(1)}, bf16[12,3...) custom-call(bf16[12,128,128]{2,1,0:T(8,128)(2,1)S(1)} %get-tuple-element.24.act_e, ...), custom_call_target="tpu_custom_call" | custom-call | flops 3000000000 | bytes 1048576 | tf_op jit(solution)/shard_map/pallas_call | solution.py:648
  42.1 2.3 %collective-permute-start.9 = (bf16[4,128,256]{2,1,0:T(8,128)(2,1)S(1)}, bf16[4,128,256]{2,1,0:T(8,128)(2,1)S(1)}, u32[]{:S(2)}, u32[]{:S(2)}) collective-permute-start(bf16[4,128,256]{2,1,0:T(8,128)(2,1)S(1)} %get-tuple-element.37.mine_ref), channel_id=1, source_target_pairs={{0,4},{4,0},{8,12},{12,8},{16,20},{20,16},{24,28},{28,24},{1,5},{5... | collective-permute-start | bytes 786440 | tf_op jit(solution)/shard_map/ppermute | solution.py:798
  44.4 1.2 %collective-permute-done.9.other_ref.pair_ref = bf16[4,128,256]{2,1,0:T(8,128)(2,1)S(1)} collective-permute-done((bf16[4,128,256]{2,1,0:T(8,128)(2,1)S(1)}, bf16[4,128,256]{2,1,0:T(8,128)(2,1)S(1)}, u32[]{:S(2)}, u32[]{:S(2)}) %collective-permute-start.9) | collective-permute-done | bytes 262176 | tf_op jit(solution)/shard_map/ppermute | solution.py:798
  45.8 1.3 %collective-permute-start.10 = (bf16[2,128,256]{2,1,0:T(8,128)(2,1)S(1)}, bf16[2,128,256]{2,1,0:T(8,128)(2,1)S(1)}, u32[]{:S(2)}, u32[]{:S(2)}) collective-permute-start(bf16[2,128,256]{2,1,0:T(8,128)(2,1)S(1)} %shard_map.86.block_ref), channel_id=1, source_target_pairs={{0,8},{4,12},{16,24},{20,28},{1,9},{5,13},{17,25},{21,29},{2,10},{... | collective-permute-start | bytes 393224 | tf_op jit(solution)/shard_map/ppermute | solution.py:815
  47.1 2.7 %collective-permute-done.10.sent_ref = bf16[2,128,256]{2,1,0:T(8,128)(2,1)S(1)} collective-permute-done((bf16[2,128,256]{2,1,0:T(8,128)(2,1)S(1)}, bf16[2,128,256]{2,1,0:T(8,128)(2,1)S(1)}, u32[]{:S(2)}, u32[]{:S(2)}) %collective-permute-start.10) | collective-permute-done | bytes 131104 | tf_op jit(solution)/shard_map/ppermute | solution.py:815
  50.0 0.7 %collective-permute-start.12 = (bf16[2,128,128]{2,1,0:T(8,128)(2,1)S(1)}, bf16[2,128,128]{2,1,0:T(8,128)(2,1)S(1)}, u32[]{:S(2)}, u32[]{:S(2)}) collective-permute-start(bf16[2,128,128]{2,1,0:T(8,128)(2,1)S(1)} %slice.15), channel_id=1, source_target_pairs={{8,24},{12,28},{9,25},{13,29},{10,26},{14,30},{11,27},{15,31}} | collective-permute-start | bytes 196616 | tf_op jit(solution)/shard_map/ppermute | solution.py:815
  50.7 1.5 %collective-permute-start.11 = (bf16[2,128,128]{2,1,0:T(8,128)(2,1)S(1)}, bf16[2,128,128]{2,1,0:T(8,128)(2,1)S(1)}, u32[]{:S(2)}, u32[]{:S(2)}) collective-permute-start(bf16[2,128,128]{2,1,0:T(8,128)(2,1)S(1)} %slice.15), channel_id=1, source_target_pairs={{8,16},{12,20},{9,17},{13,21},{10,18},{14,22},{11,19},{15,23}} | collective-permute-start | bytes 196616 | tf_op jit(solution)/shard_map/ppermute | solution.py:815
  52.2 1.4 %shard_map.89 = (f32[128,512]{1,0:T(8,128)S(1)}, f32[256,512]{1,0:T(8,128)S(1)}, f32[128,512]{1,0:T(8,128)S(1)}) custom-call(bf16[128,2048]{1,0:T(8,128)(2,1)S(1)} %copy-done, bf16[128,2048]{1,0:T(8,128)(2,1)S(1)} %collective-permute-done.refs_1_, bf16[128,2048]{1,0:T(8,128)(2,1)S(1)} %collective-permute-done.1.refs_2_, ...), custom_call_target="tpu_custom_call" | custom-call | flops 3000000000 | bytes 1048576 | tf_op jit(solution)/shard_map/pallas_call | solution.py:648
  53.6 5.8 %collective-permute-done.11.refs_0_ = bf16[2,128,128]{2,1,0:T(8,128)(2,1)S(1)} collective-permute-done((bf16[2,128,128]{2,1,0:T(8,128)(2,1)S(1)}, bf16[2,128,128]{2,1,0:T(8,128)(2,1)S(1)}, u32[]{:S(2)}, u32[]{:S(2)}) %collective-permute-start.11) | collective-permute-done | bytes 65568 | tf_op jit(solution)/shard_map/ppermute | solution.py:815
  59.5 1.6 %collective-permute-start.13 = (bf16[2,128,128]{2,1,0:T(8,128)(2,1)S(1)}, bf16[2,128,128]{2,1,0:T(8,128)(2,1)S(1)}, u32[]{:S(2)}, u32[]{:S(2)}) collective-permute-start(bf16[2,128,128]{2,1,0:T(8,128)(2,1)S(1)} %shard_map.88.mine_ref), channel_id=1, source_target_pairs={{0,4},{4,0},{8,12},{12,8},{16,20},{20,16},{24,28},{28,24},{1,5},{5... | collective-permute-start | bytes 196616 | tf_op jit(solution)/shard_map/ppermute | solution.py:829
  61.1 2.8 %shard_map.85 = (bf16[4,512,128]{2,1,0:T(8,128)(2,1)S(1)}, f32[4,512,128]{2,1,0:T(8,128)S(1)}) custom-call(bf16[4,4,128,256]{3,2,1,0:T(8,128)(2,1)S(1)} %get-tuple-element.30.both_ref, bf16[4,4,128,256]{3,2,1,0:T(8,128)(2,1)S(1)} %get-tuple-element.31.low_ref, bf16[12,128,128]{2,1,0:T(8,128)(2,1)S(1)} %get-tuple-element.24.act_e, ...), custom_call_target="tpu_custom_call" | custom-call | flops 2000000000 | bytes 1048576 | tf_op jit(solution)/shard_map/pallas_call | solution.py:648
  63.9 1.8 %shard_map.90 = bf16[512,512]{1,0:T(8,128)(2,1)} custom-call(bf16[4,512,128]{2,1,0:T(8,128)(2,1)S(1)} %get-tuple-element.35.qp_ref, f32[4,512,128]{2,1,0:T(8,128)S(1)} %get-tuple-element.36.o_ref, bf16[4,128,256]{2,1,0:T(8,128)(2,1)S(1)} %collective-permute-done.9.other_ref.pair_ref, bf16[2,128,128]{2,1,0:T(8,128)(2,1)S(1)} %shard_map.88.mine_ref, ...), custom_call_target="tpu_custom_call" | custom-call | flops 50000000 | bytes 1048576 | tf_op jit(solution)/shard_map/pallas_call | solution.py:648
  (36 shorter events, 1.1 us)
Async XLA Ops:
  0.0 25.4 %slice-start = ((s8[6291456]{0:T(1024)(128)(4,1)}), s8[4194304]{0:T(1024)(128)(4,1)S(1)}, s32[]{:S(2)}) async-start(s8[6291456]{0:T(1024)(128)(4,1)} %bitcast.7), calls=%async_computation | async-start | bytes 8388608
  0.9 24.4 %copy-start = (bf16[128,2048]{1,0:T(8,128)(2,1)S(1)}, bf16[128,2048]{1,0:T(8,128)(2,1)}, u32[]{:S(2)}) copy-start(bf16[128,2048]{1,0:T(8,128)(2,1)} %refs_0_.3) | copy-start | bytes 1572868
  0.9 24.5 %slice-start.1 = ((s8[6291456]{0:T(1024)(128)(4,1)}), s8[2097152]{0:T(1024)(128)(4,1)S(1)}, s32[]{:S(2)}) async-start(s8[6291456]{0:T(1024)(128)(4,1)} %bitcast.7), calls=%async_computation.1 | async-start | bytes 4194304
  0.9 24.5 %copy-start.3 = (bf16[2048,2,4]{0,2,1:T(4,128)(2,1)S(1)}, bf16[2048,2,4]{0,2,1:T(4,128)(2,1)}, u32[]{:S(2)}) copy-start(bf16[2048,2,4]{0,2,1:T(4,128)(2,1)} %param.11) | copy-start | bytes 98308
  0.9 24.5 %copy-start.4 = (bf16[4,3,512]{2,0,1:T(4,128)(2,1)S(1)}, bf16[4,3,512]{2,0,1:T(4,128)(2,1)}, u32[]{:S(2)}) copy-start(bf16[4,3,512]{2,0,1:T(4,128)(2,1)} %param.12) | copy-start | bytes 36868
  0.9 24.5 %copy-start.5 = (f32[4]{0:T(128)S(1)}, f32[4]{0:T(128)}, u32[]{:S(2)}) copy-start(f32[4]{0:T(128)} %param.13) | copy-start | bytes 52
  0.9 24.5 %copy-start.6 = (f32[4]{0:T(128)S(1)}, f32[4]{0:T(128)}, u32[]{:S(2)}) copy-start(f32[4]{0:T(128)} %param.14) | copy-start | bytes 52
  1.0 29.0 %collective-permute-start.8 = (bf16[8,2048]{1,0:T(8,128)(2,1)S(1)}, bf16[8,2048]{1,0:T(8,128)(2,1)S(1)}, u32[]{:S(2)}, u32[]{:S(2)}) collective-permute-start(bf16[8,2048]{1,0:T(8,128)(2,1)S(1)} %slice.12), channel_id=1, source_target_pairs={{3,7},{7,11},{11,15},{15,19},{19,23},{23,27},{27,31}} | collective-permute-start | bytes 98312 | tf_op jit(solution)/shard_map/ppermute | solution.py:69
  1.8 21.5 %collective-permute-start.3 = (bf16[8,2048]{1,0:T(8,128)(2,1)S(1)}, bf16[8,2048]{1,0:T(8,128)(2,1)S(1)}, u32[]{:S(2)}, u32[]{:S(2)}) collective-permute-start(bf16[8,2048]{1,0:T(8,128)(2,1)S(1)} %slice.12), channel_id=1, source_target_pairs={{3,5},{7,9},{11,13},{15,17},{19,21},{23,25},{27,29}} | collective-permute-start | bytes 98312 | tf_op jit(solution)/shard_map/ppermute | solution.py:69
  2.6 22.8 %collective-permute-start.2 = (bf16[8,2048]{1,0:T(8,128)(2,1)S(1)}, bf16[8,2048]{1,0:T(8,128)(2,1)S(1)}, u32[]{:S(2)}, u32[]{:S(2)}) collective-permute-start(bf16[8,2048]{1,0:T(8,128)(2,1)S(1)} %slice.12), channel_id=1, source_target_pairs={{0,3},{1,2},{2,1},{3,0},{4,7},{5,6},{6,5},{7,4},{8,11},{9,10},{10,... | collective-permute-start | bytes 98312 | tf_op jit(solution)/shard_map/ppermute | solution.py:71
  4.4 16.3 %collective-permute-start.1 = (bf16[128,2048]{1,0:T(8,128)(2,1)}, bf16[128,2048]{1,0:T(8,128)(2,1)S(1)}, u32[]{:S(2)}, u32[]{:S(2)}) collective-permute-start(bf16[128,2048]{1,0:T(8,128)(2,1)} %refs_0_.3), channel_id=1, source_target_pairs={{0,2},{1,3},{2,0},{3,1},{4,6},{5,7},{6,4},{7,5},{8,10},{9,11},{10,... | collective-permute-start | bytes 1572872 | tf_op jit(solution)/shard_map/ppermute | solution.py:43
  8.8 13.9 %collective-permute-start = (bf16[128,2048]{1,0:T(8,128)(2,1)}, bf16[128,2048]{1,0:T(8,128)(2,1)S(1)}, u32[]{:S(2)}, u32[]{:S(2)}) collective-permute-start(bf16[128,2048]{1,0:T(8,128)(2,1)} %refs_0_.3), channel_id=1, source_target_pairs={{0,1},{1,0},{2,3},{3,2},{4,5},{5,4},{6,7},{7,6},{8,9},{9,8},{10,11... | collective-permute-start | bytes 1572872 | tf_op jit(solution)/shard_map/ppermute | solution.py:43
  20.7 9.2 %collective-permute-start.7 = (bf16[8,2048]{1,0:T(8,128)(2,1)S(1)}, bf16[8,2048]{1,0:T(8,128)(2,1)S(1)}, u32[]{:S(2)}, u32[]{:S(2)}) collective-permute-start(bf16[8,2048]{1,0:T(8,128)(2,1)S(1)} %slice.12), channel_id=1, source_target_pairs={{3,6},{7,10},{11,14},{15,18},{19,22},{23,26},{27,30}} | collective-permute-start | bytes 98312 | tf_op jit(solution)/shard_map/ppermute | solution.py:69
  22.6 7.3 %collective-permute-start.6 = (bf16[8,2048]{1,0:T(8,128)(2,1)S(1)}, bf16[8,2048]{1,0:T(8,128)(2,1)S(1)}, u32[]{:S(2)}, u32[]{:S(2)}) collective-permute-start(bf16[8,2048]{1,0:T(8,128)(2,1)S(1)} %slice.12), channel_id=1, source_target_pairs={{3,4},{7,8},{11,12},{15,16},{19,20},{23,24},{27,28}} | collective-permute-start | bytes 98312 | tf_op jit(solution)/shard_map/ppermute | solution.py:69
  23.3 8.1 %collective-permute-start.4 = (bf16[64,2048]{1,0:T(8,128)(2,1)S(1)}, bf16[64,2048]{1,0:T(8,128)(2,1)S(1)}, u32[]{:S(2)}, u32[]{:S(2)}) collective-permute-start(bf16[64,2048]{1,0:T(8,128)(2,1)S(1)} %slice.16), channel_id=1, source_target_pairs={{0,1},{1,0},{2,3},{3,2},{4,5},{5,4},{6,7},{7,6},{8,9},{9,8},{10,11... | collective-permute-start | bytes 786440 | tf_op jit(solution)/shard_map/ppermute | solution.py:43
  25.4 6.5 %collective-permute-start.5 = (bf16[64,2048]{1,0:T(8,128)(2,1)S(1)}, bf16[64,2048]{1,0:T(8,128)(2,1)S(1)}, u32[]{:S(2)}, u32[]{:S(2)}) collective-permute-start(bf16[64,2048]{1,0:T(8,128)(2,1)S(1)} %slice.17), channel_id=1, source_target_pairs={{0,2},{1,3},{2,0},{3,1},{4,6},{5,7},{6,4},{7,5},{8,10},{9,11},{10,... | collective-permute-start | bytes 786440 | tf_op jit(solution)/shard_map/ppermute | solution.py:43
  31.8 20.4 %copy-start.2 = (bf16[2048,512]{1,0:T(8,128)(2,1)S(1)}, bf16[2048,512]{1,0:T(8,128)(2,1)}, u32[]{:S(2)}) copy-start(bf16[2048,512]{1,0:T(8,128)(2,1)} %refs_5_.1) | copy-start | bytes 6291460
  42.1 3.5 %collective-permute-start.9 = (bf16[4,128,256]{2,1,0:T(8,128)(2,1)S(1)}, bf16[4,128,256]{2,1,0:T(8,128)(2,1)S(1)}, u32[]{:S(2)}, u32[]{:S(2)}) collective-permute-start(bf16[4,128,256]{2,1,0:T(8,128)(2,1)S(1)} %get-tuple-element.37.mine_ref), channel_id=1, source_target_pairs={{0,4},{4,0},{8,12},{12,8},{16,20},{20,16},{24,28},{28,24},{1,5},{5... | collective-permute-start | bytes 786440 | tf_op jit(solution)/shard_map/ppermute | solution.py:798
  45.8 4.0 %collective-permute-start.10 = (bf16[2,128,256]{2,1,0:T(8,128)(2,1)S(1)}, bf16[2,128,256]{2,1,0:T(8,128)(2,1)S(1)}, u32[]{:S(2)}, u32[]{:S(2)}) collective-permute-start(bf16[2,128,256]{2,1,0:T(8,128)(2,1)S(1)} %shard_map.86.block_ref), channel_id=1, source_target_pairs={{0,8},{4,12},{16,24},{20,28},{1,9},{5,13},{17,25},{21,29},{2,10},{... | collective-permute-start | bytes 393224 | tf_op jit(solution)/shard_map/ppermute | solution.py:815
  50.0 3.6 %collective-permute-start.12 = (bf16[2,128,128]{2,1,0:T(8,128)(2,1)S(1)}, bf16[2,128,128]{2,1,0:T(8,128)(2,1)S(1)}, u32[]{:S(2)}, u32[]{:S(2)}) collective-permute-start(bf16[2,128,128]{2,1,0:T(8,128)(2,1)S(1)} %slice.15), channel_id=1, source_target_pairs={{8,24},{12,28},{9,25},{13,29},{10,26},{14,30},{11,27},{15,31}} | collective-permute-start | bytes 196616 | tf_op jit(solution)/shard_map/ppermute | solution.py:815
  50.7 8.7 %collective-permute-start.11 = (bf16[2,128,128]{2,1,0:T(8,128)(2,1)S(1)}, bf16[2,128,128]{2,1,0:T(8,128)(2,1)S(1)}, u32[]{:S(2)}, u32[]{:S(2)}) collective-permute-start(bf16[2,128,128]{2,1,0:T(8,128)(2,1)S(1)} %slice.15), channel_id=1, source_target_pairs={{8,16},{12,20},{9,17},{13,21},{10,18},{14,22},{11,19},{15,23}} | collective-permute-start | bytes 196616 | tf_op jit(solution)/shard_map/ppermute | solution.py:815
  59.5 4.3 %collective-permute-start.13 = (bf16[2,128,128]{2,1,0:T(8,128)(2,1)S(1)}, bf16[2,128,128]{2,1,0:T(8,128)(2,1)S(1)}, u32[]{:S(2)}, u32[]{:S(2)}) collective-permute-start(bf16[2,128,128]{2,1,0:T(8,128)(2,1)S(1)} %shard_map.88.mine_ref), channel_id=1, source_target_pairs={{0,4},{4,0},{8,12},{12,8},{16,20},{20,16},{24,28},{28,24},{1,5},{5... | collective-permute-start | bytes 196616 | tf_op jit(solution)/shard_map/ppermute | solution.py:829
  61.1 2.8 %copy-start.1 = (f32[128]{0:T(128)S(1)}, f32[128]{0:T(128)}, u32[]{:S(2)}) copy-start(f32[128]{0:T(128)} %param.15) | copy-start | bytes 1540

commit v7 on v6

--- a/solution.py
+++ b/solution.py
@@ -334,32 +334,35 @@
 
 
 def early_kernel(heads, blocks, *refs):
-    count = blocks + 1
-    tokens_refs, part_ref = refs[:blocks], refs[blocks]
+    count = 2 * blocks - 2
+    tokens_refs = refs[:blocks]
+    part_refs = refs[blocks:count]
     w_ref, small_ref, taps_ref, rate_ref, bias_ref = refs[count:count + 5]
-    act, cols, rows_of, raw_ref, raw_sc_ref, rims_ref, xp, tails = refs[count + 5:]
+    act, cols, rows_of, own_ref, own_sc_ref, own_rim_ref, late_rim_ref, xp, sc, tails = refs[count + 5:]
     early = blocks - 1
+    span = RIM + CHUNK
     mid = early * CHUNK
     me = lax.axis_index("tp")
-    edge = jnp.concatenate([tokens_refs[-1][...].astype(f32), part_ref[...].astype(f32)], axis=0)
+    before = part_refs[0][...].astype(f32)
+    for ref in part_refs[1:]:
+        before = before + ref[...].astype(f32)
+    edge = jnp.concatenate([tokens_refs[-1][...].astype(f32), before], axis=0)
     tokens = jnp.concatenate([ref[...] for ref in tokens_refs[:-1]] + [edge.astype(bf16)], axis=0)
     raw = dot(tokens[:mid], scalar_weights(small_ref), (1, 1))
-    later = [m for m in range(early) if m != 1]
-    for slot, m in enumerate(later):
-        raw_sc_ref[slot * CHUNK:(slot + 1) * CHUNK] = raw[m * CHUNK:(m + 1) * CHUNK]
+    own_sc_ref[...] = raw[:CHUNK]
+    sc[...] = raw[CHUNK:]
 
     def fill(branch, carry):
         made = dot(tokens, w_ref[branch]).astype(bf16).astype(f32)
         for head in range(heads):
             tile = branch * heads + head
             lanes = slice(head * LANES, (head + 1) * LANES)
+            own_ref[tile] = made[:CHUNK, lanes]
             for m in range(early):
                 block = made[m * CHUNK:(m + 1) * CHUNK, lanes]
-                if m == 1:
-                    xp[tile, RIM:] = block
-                else:
-                    slot = later.index(m)
-                    raw_ref[tile, slot * CHUNK:(slot + 1) * CHUNK] = block
+                if m > 0:
+                    at = (m - 1) * span
+                    xp[tile, at + RIM:at + span] = block
                 tails[m, tile] = block[CHUNK - RIM:]
             tails[early, tile] = made[mid:mid + RIM, lanes]
             tails[blocks, tile] = made[mid + RIM:, lanes]
@@ -372,23 +375,25 @@
         index = lax.bitwise_xor(me, m)
         return jnp.where(index == 0, blocks, lax.bitwise_xor(me, jnp.maximum(index - 1, 0)))
 
-    for slot, m in enumerate(later + [early]):
-        rims_ref[slot] = tails[ahead_of(m)]
-    source = ahead_of(1)
-    for tile in range(3 * heads):
-        xp[tile, :RIM] = tails[source, tile]
+    own_rim_ref[...] = tails[ahead_of(0)]
+    late_rim_ref[...] = tails[ahead_of(early)]
 
     def prepare(slot, carry):
+        at = pl.ds(pl.multiple_of(slot * CHUNK, CHUNK), CHUNK)
+        base = pl.multiple_of(slot * span, 8)
+        source = ahead_of(slot + 1)
+        for tile in range(3 * heads):
+            xp[tile, pl.ds(base, RIM)] = tails[source, tile]
+
         def keep(tile, value):
-            act[tile] = value
-
-        base = pl.multiple_of(slot * CHUNK, CHUNK)
-        comb = convolve(heads, xp, base, taps_ref, raw[CHUNK:2 * CHUNK], rate, bias, keep)
-        cols[0] = comb
-        rows_of[0] = comb.T
+            act[tile, at] = value
+
+        comb = convolve(heads, xp, base, taps_ref, sc[at], rate, bias, keep)
+        cols[slot] = comb
+        rows_of[slot] = comb.T
         return carry
 
-    prepare(0, 0)
+    lax.fori_loop(0, early - 1, prepare, 0)
 
 
 def masks_kernel(out_ref):
@@ -400,22 +405,17 @@
 
 
 def block_delta_kernel(
-    heads, blocks, act_e, cols_e, rows_e, raw_ref, raw_sc_ref, rims_ref, late0_ref, late1_ref, *refs
+    heads, blocks, act_e, cols_e, rows_e, own_ref, own_sc_ref, own_rim_ref, late_rim_ref,
+    late0_ref, late1_ref, part0_ref, part1_ref, w_ref, small_ref, taps_ref, rate_ref, bias_ref,
+    masks, x_ref, both_ref, low_ref, act_l, cols_l, rows_l, xp, sc, mixes, solves, changes, lasts,
 ):
     me = lax.axis_index("tp")
-    part_refs = refs[:blocks - 1]
-    w_ref, small_ref, taps_ref, rate_ref, bias_ref, masks = refs[blocks - 1:blocks + 5]
-    x_ref, both_ref, low_ref, act_l, cols_l, rows_l = refs[blocks + 5:blocks + 11]
-    xp, sc, mixes, solves, changes, lasts = refs[blocks + 11:]
     span = RIM + CHUNK
-    slots = blocks - 1
-    before = part_refs[0][...].astype(f32)
-    for ref in part_refs[1:]:
-        before = before + ref[...].astype(f32)
+    before = part0_ref[...].astype(f32) + part1_ref[...].astype(f32)
     before = jnp.concatenate([before, jnp.zeros_like(before)], axis=0)
     tokens = jnp.concatenate([late0_ref[...], late1_ref[...], before.astype(bf16)], axis=0)
-    sc[:(slots - 1) * CHUNK] = raw_sc_ref[...]
-    sc[(slots - 1) * CHUNK:] = dot(tokens[:CHUNK], scalar_weights(small_ref), (1, 1))
+    sc[:CHUNK] = own_sc_ref[...]
+    sc[CHUNK:] = dot(tokens[:CHUNK], scalar_weights(small_ref), (1, 1))
 
     def fill(branch, carry):
         made = dot(tokens, w_ref[branch]).astype(bf16).astype(f32)
@@ -423,14 +423,10 @@
             tile = branch * heads + head
             lanes = slice(head * LANES, (head + 1) * LANES)
             rim = made[CHUNK:CHUNK + RIM, lanes]
-            for slot in range(slots):
-                at = slot * span
-                first = me == (slot + 1 if slot else 0)
-                xp[tile, at:at + RIM] = jnp.where(first, rim, rims_ref[slot, tile])
-                if slot == slots - 1:
-                    xp[tile, at + RIM:at + span] = made[:CHUNK, lanes]
-                else:
-                    xp[tile, at + RIM:at + span] = raw_ref[tile, slot * CHUNK:(slot + 1) * CHUNK]
+            xp[tile, :RIM] = jnp.where(me == 0, rim, own_rim_ref[tile])
+            xp[tile, RIM:span] = own_ref[tile]
+            xp[tile, span:span + RIM] = jnp.where(me == blocks - 1, rim, late_rim_ref[tile])
+            xp[tile, span + RIM:] = made[:CHUNK, lanes]
         return carry
 
     lax.fori_loop(0, 3, fill, 0)
@@ -448,27 +444,27 @@
         rows_l[slot] = comb.T
         return carry
 
-    lax.fori_loop(0, slots, prepare, 0)
+    lax.fori_loop(0, 2, prepare, 0)
 
     ri, ci = grid_index((CHUNK, CHUNK))
     levels = masks.shape[0]
 
     def part(branch, head, m):
-        held, slot = (act_e, 0) if m == 1 else (act_l, max(m - 1, 0))
+        held, slot = (act_e, m - 1) if 0 < m < blocks - 1 else (act_l, min(m, 1))
         return held[branch * heads + head, slot * CHUNK:(slot + 1) * CHUNK]
 
     def col(kind, head, m):
         lane = kind * heads + head
-        held, slot = (cols_e, 0) if m == 1 else (cols_l, max(m - 1, 0))
+        held, slot = (cols_e, m - 1) if 0 < m < blocks - 1 else (cols_l, min(m, 1))
         return held[slot, :, lane:lane + 1]
 
     def row(kind, head, m):
         lane = kind * heads + head
-        held, slot = (rows_e, 0) if m == 1 else (rows_l, max(m - 1, 0))
+        held, slot = (rows_e, m - 1) if 0 < m < blocks - 1 else (rows_l, min(m, 1))
         return held[slot, lane:lane + 1, :]
 
     for m in range(blocks):
-        held, slot = (cols_e, 0) if m == 1 else (cols_l, max(m - 1, 0))
+        held, slot = (cols_e, m - 1) if 0 < m < blocks - 1 else (cols_l, min(m, 1))
         lasts[m] = jnp.exp(held[slot, CHUNK - 8:])
 
     sets = [(head, m) for m in range(0, blocks, 2) for head in range(heads)]
@@ -536,8 +532,9 @@
     for head in range(heads):
         for m in range(blocks):
             at = slice(m * CHUNK, (m + 1) * CHUNK)
-            slot = 0 if m == 1 else max(m - 1, 0)
-            act, cols_of, rows_of = (act_e, cols_e, rows_e) if m == 1 else (act_l, cols_l, rows_l)
+            middle = 0 < m < blocks - 1
+            slot = m - 1 if middle else min(m, 1)
+            act, cols_of, rows_of = (act_e, cols_e, rows_e) if middle else (act_l, cols_l, rows_l)
             held = slice(slot * CHUNK, (slot + 1) * CHUNK)
             cols, rows = cols_of[slot], rows_of[slot]
             q, k = act[head, held], act[heads + head, held]
@@ -694,23 +691,25 @@
             shape((CHUNK.bit_length() - 1, CHUNK, 2 * CHUNK), bf16), [],
             flops=MASKS_FLOPS, limit=4,
         )
-        act_e, cols_e, rows_e, raw, raw_sc, rims = call(
+        act_e, cols_e, rows_e, own_f, own_sc, own_rim, late_rim = call(
             functools.partial(early_kernel, heads, blocks),
             (
-                shape((3 * heads, rows, dim), bf16),
-                shape((1, CHUNK, LANES), f32),
-                shape((1, CHUNK, LANES), f32),
-                shape((3 * heads, seq_rows - 2 * rows, dim), f32),
-                shape((seq_rows - 2 * rows, LANES), f32),
-                shape((blocks - 1, 3 * heads, RIM, dim), f32),
+                shape((3 * heads, seq_rows - 2 * rows, dim), bf16),
+                shape((blocks - 2, CHUNK, LANES), f32),
+                shape((blocks - 2, CHUNK, LANES), f32),
+                shape((3 * heads, rows, dim), f32),
+                shape((rows, LANES), f32),
+                shape((3 * heads, RIM, dim), f32),
+                shape((3 * heads, RIM, dim), f32),
             ),
             [
-                hidden, *early, across, parts[1],
+                hidden, *early, across, *parts[1:-1],
                 w_three, small, taps, rate, bias,
             ],
             flops=PROJECT_FLOPS,
             scratch=[
-                pltpu.VMEM((3 * heads, RIM + CHUNK, dim), f32),
+                pltpu.VMEM((3 * heads, (blocks - 2) * (RIM + CHUNK), dim), f32),
+                pltpu.VMEM((seq_rows - 2 * rows, LANES), f32),
                 pltpu.VMEM((blocks + 1, 3 * heads, RIM, dim), f32),
             ],
         )
@@ -720,18 +719,18 @@
                 shape((heads, dim, 2 * dim), bf16),
                 shape((heads, blocks, CHUNK, 2 * dim), bf16),
                 shape((heads, blocks, dim, 2 * dim), bf16),
-                shape((3 * heads, seq_rows - rows, dim), bf16),
-                shape((blocks - 1, CHUNK, LANES), f32),
-                shape((blocks - 1, CHUNK, LANES), f32),
+                shape((3 * heads, 2 * rows, dim), bf16),
+                shape((2, CHUNK, LANES), f32),
+                shape((2, CHUNK, LANES), f32),
             ),
             [
-                act_e, cols_e, rows_e, raw, raw_sc, rims, *late,
-                parts[0], *parts[2:], w_three, small, taps, rate, bias, masks,
+                act_e, cols_e, rows_e, own_f, own_sc, own_rim, late_rim, *late,
+                parts[0], parts[-1], w_three, small, taps, rate, bias, masks,
             ],
             flops=DELTA_FLOPS, limit=28,
             scratch=[
-                pltpu.VMEM((3 * heads, (blocks - 1) * (RIM + CHUNK), dim), f32),
-                pltpu.VMEM((seq_rows - rows, LANES), f32),
+                pltpu.VMEM((3 * heads, 2 * (RIM + CHUNK), dim), f32),
+                pltpu.VMEM((2 * rows, LANES), f32),
                 pltpu.VMEM((heads * blocks // 2, CHUNK, 2 * CHUNK), bf16),
                 pltpu.VMEM((heads * blocks // 2, CHUNK, 2 * CHUNK), f32),
                 pltpu.VMEM((blocks, heads, dim, 2 * dim), f32),

time: 65.9 us -> 65 us (0.986)
  starting transfers between devices: 19.1 us -> 18.4 us
  transfers between devices with their start and end apart: 14 -> 14, of which waited for: 7 -> 7; matrix products, arithmetic and copies ran while one was open for 0% -> 0% of each run, Pallas kernels for 13% -> 15%
where the time goes in v7:
time: 65 us; the launch traced here: 64.8 us
  waiting for transfers between devices  23.7 us (36%)
  Pallas kernels  21.3 us (33%)
  starting transfers between devices  18.4 us (28%)
  local copies, waits for them, and re-layouts  1 us (2%)
    pallas_call x9, Pallas kernels, call(): pl.pallas_call(kernel, out_shape=out, in_specs=[whole()] * len(operands),...  21.3 us
    ppermute x4, waiting for transfers between devices, swap(): return lax.ppermute(value, axis, [(i, i ^ step) for i in range(count)])  13.8 us
    ppermute x3, waiting for transfers between devices, per_device(): parts.append(lax.ppermute(sent, 'seq', route))  8.72 us
    ppermute x4, starting transfers between devices, swap(): return lax.ppermute(value, axis, [(i, i ^ step) for i in range(count)])  6.17 us
    ppermute x4, starting transfers between devices, rim_rows(): parts.append(lax.ppermute(tail, ('seq', 'tp'), route))  3.52 us
    ppermute x3, starting transfers between devices, per_device(): parts.append(lax.ppermute(sent, 'seq', route))  3.43 us
    ppermute x1, starting transfers between devices, per_device(): other = lax.ppermute(own, 'seq', swap)  2.53 us
    ppermute x1, starting transfers between devices, per_device(): back = lax.ppermute(state, 'seq', swap) if share else state  1.57 us
  transfers between devices with their start and end apart: 14, of which 7 were waited for; matrix products, arithmetic and copies ran while one was open for 0% of the time, Pallas kernels for 15%

profile of v7, /device:TPU:21, one launch (start us, length us, event | category | flops | bytes accessed | tf_op | source)
XLA Modules:
  0.0 64.8 jit_solution(8095930450554443378)
XLA Ops:
  0.0 0.9 %slice.12 = bf16[8,2048]{1,0:T(8,128)(2,1)S(1)} slice(bf16[128,2048]{1,0:T(8,128)(2,1)} %refs_0_.3), slice={[120:128], [0:2048]} | slice | bytes 65536 | tf_op jit(solution)/shard_map/slice | solution.py:65
  1.0 1.6 %collective-permute-start.4 = (bf16[8,2048]{1,0:T(8,128)(2,1)S(1)}, bf16[8,2048]{1,0:T(8,128)(2,1)S(1)}, u32[]{:S(2)}, u32[]{:S(2)}) collective-permute-start(bf16[8,2048]{1,0:T(8,128)(2,1)S(1)} %slice.12), channel_id=1, source_target_pairs={{3,6},{7,10},{11,14},{15,18},{19,22},{23,26},{27,30}} | collective-permute-start | bytes 98312 | tf_op jit(solution)/shard_map/ppermute | solution.py:69
  2.5 0.7 %collective-permute-start.3 = (bf16[8,2048]{1,0:T(8,128)(2,1)S(1)}, bf16[8,2048]{1,0:T(8,128)(2,1)S(1)}, u32[]{:S(2)}, u32[]{:S(2)}) collective-permute-start(bf16[8,2048]{1,0:T(8,128)(2,1)S(1)} %slice.12), channel_id=1, source_target_pairs={{3,5},{7,9},{11,13},{15,17},{19,21},{23,25},{27,29}} | collective-permute-start | bytes 98312 | tf_op jit(solution)/shard_map/ppermute | solution.py:69
  3.2 1.2 %collective-permute-start.2 = (bf16[8,2048]{1,0:T(8,128)(2,1)S(1)}, bf16[8,2048]{1,0:T(8,128)(2,1)S(1)}, u32[]{:S(2)}, u32[]{:S(2)}) collective-permute-start(bf16[8,2048]{1,0:T(8,128)(2,1)S(1)} %slice.12), channel_id=1, source_target_pairs={{0,3},{1,2},{2,1},{3,0},{4,7},{5,6},{6,5},{7,4},{8,11},{9,10},{10,... | collective-permute-start | bytes 98312 | tf_op jit(solution)/shard_map/ppermute | solution.py:71
  4.4 4.3 %collective-permute-start.1 = (bf16[128,2048]{1,0:T(8,128)(2,1)}, bf16[128,2048]{1,0:T(8,128)(2,1)S(1)}, u32[]{:S(2)}, u32[]{:S(2)}) collective-permute-start(bf16[128,2048]{1,0:T(8,128)(2,1)} %refs_0_.3), channel_id=1, source_target_pairs={{0,2},{1,3},{2,0},{3,1},{4,6},{5,7},{6,4},{7,5},{8,10},{9,11},{10,... | collective-permute-start | bytes 1572872 | tf_op jit(solution)/shard_map/ppermute | solution.py:43
  8.8 11.9 %collective-permute-done.1.refs_2_ = bf16[128,2048]{1,0:T(8,128)(2,1)S(1)} collective-permute-done((bf16[128,2048]{1,0:T(8,128)(2,1)}, bf16[128,2048]{1,0:T(8,128)(2,1)S(1)}, u32[]{:S(2)}, u32[]{:S(2)}) %collective-permute-start.1) | collective-permute-done | bytes 524320 | tf_op jit(solution)/shard_map/ppermute | solution.py:43
  20.7 0.7 %collective-permute-start.8 = (bf16[8,2048]{1,0:T(8,128)(2,1)S(1)}, bf16[8,2048]{1,0:T(8,128)(2,1)S(1)}, u32[]{:S(2)}, u32[]{:S(2)}) collective-permute-start(bf16[8,2048]{1,0:T(8,128)(2,1)S(1)} %slice.12), channel_id=1, source_target_pairs={{3,7},{7,11},{11,15},{15,19},{19,23},{23,27},{27,31}} | collective-permute-start | bytes 98312 | tf_op jit(solution)/shard_map/ppermute | solution.py:69
  21.4 1.2 %collective-permute-done.refs_1_ = bf16[128,2048]{1,0:T(8,128)(2,1)S(1)} collective-permute-done((bf16[128,2048]{1,0:T(8,128)(2,1)}, bf16[128,2048]{1,0:T(8,128)(2,1)S(1)}, u32[]{:S(2)}, u32[]{:S(2)}) %collective-permute-start) | collective-permute-done | bytes 524320 | tf_op jit(solution)/shard_map/ppermute | solution.py:43
  22.6 0.7 %collective-permute-start.7 = (bf16[8,2048]{1,0:T(8,128)(2,1)S(1)}, bf16[8,2048]{1,0:T(8,128)(2,1)S(1)}, u32[]{:S(2)}, u32[]{:S(2)}) collective-permute-start(bf16[8,2048]{1,0:T(8,128)(2,1)S(1)} %slice.12), channel_id=1, source_target_pairs={{3,4},{7,8},{11,12},{15,16},{19,20},{23,24},{27,28}} | collective-permute-start | bytes 98312 | tf_op jit(solution)/shard_map/ppermute | solution.py:69
  23.3 1.9 %collective-permute-start.5 = (bf16[64,2048]{1,0:T(8,128)(2,1)S(1)}, bf16[64,2048]{1,0:T(8,128)(2,1)S(1)}, u32[]{:S(2)}, u32[]{:S(2)}) collective-permute-start(bf16[64,2048]{1,0:T(8,128)(2,1)S(1)} %slice.16), channel_id=1, source_target_pairs={{0,1},{1,0},{2,3},{3,2},{4,5},{5,4},{6,7},{7,6},{8,9},{9,8},{10,11... | collective-permute-start | bytes 786440 | tf_op jit(solution)/shard_map/ppermute | solution.py:43
  25.2 5.4 %shard_map.82 = (bf16[12,256,128]{2,1,0:T(8,128)(2,1)S(1)}, f32[2,128,128]{2,1,0:T(8,128)S(1)}, f32[2,128,128]{2,1,0:T(8,128)S(1)}, f32[12,128,128]{2,1,0:T(8,12...) custom-call(bf16[128,2048]{1,0:T(8,128)(2,1)S(1)} %copy-done, ...), custom_call_target="tpu_custom_call" | custom-call | flops 3000000000 | bytes 1048576 | tf_op jit(solution)/shard_map/pallas_call | solution.py:645
  31.0 0.4 collective-permute-done.6.late1_ref.refs_4_
  31.4 9.4 %shard_map.84 = (bf16[4,128,256]{2,1,0:T(8,128)(2,1)S(1)}, bf16[4,4,128,256]{3,2,1,0:T(8,128)(2,1)S(1)}, bf16[4,4,128,256]{3,2,1,0:T(8,128)(2,1)S(1)}, bf16[12,2...) custom-call(bf16[12,256,128]{2,1,0:T(8,128)(2,1)S(1)} %get-tuple-element.25.act_e, ...), custom_call_target="tpu_custom_call" | custom-call | flops 3000000000 | bytes 1048576 | tf_op jit(solution)/shard_map/pallas_call | solution.py:645
  40.8 2.5 %collective-permute-start.9 = (bf16[4,128,256]{2,1,0:T(8,128)(2,1)S(1)}, bf16[4,128,256]{2,1,0:T(8,128)(2,1)S(1)}, u32[]{:S(2)}, u32[]{:S(2)}) collective-permute-start(bf16[4,128,256]{2,1,0:T(8,128)(2,1)S(1)} %get-tuple-element.39.mine_ref), channel_id=1, source_target_pairs={{0,4},{4,0},{8,12},{12,8},{16,20},{20,16},{24,28},{28,24},{1,5},{5... | collective-permute-start | bytes 786440 | tf_op jit(solution)/shard_map/ppermute | solution.py:797
  43.3 1.2 %collective-permute-done.9.other_ref.pair_ref = bf16[4,128,256]{2,1,0:T(8,128)(2,1)S(1)} collective-permute-done((bf16[4,128,256]{2,1,0:T(8,128)(2,1)S(1)}, bf16[4,128,256]{2,1,0:T(8,128)(2,1)S(1)}, u32[]{:S(2)}, u32[]{:S(2)}) %collective-permute-start.9) | collective-permute-done | bytes 262176 | tf_op jit(solution)/shard_map/ppermute | solution.py:797
  44.6 1.3 %collective-permute-start.10 = (bf16[2,128,256]{2,1,0:T(8,128)(2,1)S(1)}, bf16[2,128,256]{2,1,0:T(8,128)(2,1)S(1)}, u32[]{:S(2)}, u32[]{:S(2)}) collective-permute-start(bf16[2,128,256]{2,1,0:T(8,128)(2,1)S(1)} %shard_map.86.block_ref), channel_id=1, source_target_pairs={{0,8},{4,12},{16,24},{20,28},{1,9},{5,13},{17,25},{21,29},{2,10},{... | collective-permute-start | bytes 393224 | tf_op jit(solution)/shard_map/ppermute | solution.py:814
  45.9 2.7 %collective-permute-done.10.sent_ref = bf16[2,128,256]{2,1,0:T(8,128)(2,1)S(1)} collective-permute-done((bf16[2,128,256]{2,1,0:T(8,128)(2,1)S(1)}, bf16[2,128,256]{2,1,0:T(8,128)(2,1)S(1)}, u32[]{:S(2)}, u32[]{:S(2)}) %collective-permute-start.10) | collective-permute-done | bytes 131104 | tf_op jit(solution)/shard_map/ppermute | solution.py:814
  48.9 0.7 %collective-permute-start.12 = (bf16[2,128,128]{2,1,0:T(8,128)(2,1)S(1)}, bf16[2,128,128]{2,1,0:T(8,128)(2,1)S(1)}, u32[]{:S(2)}, u32[]{:S(2)}) collective-permute-start(bf16[2,128,128]{2,1,0:T(8,128)(2,1)S(1)} %slice.15), channel_id=1, source_target_pairs={{8,24},{12,28},{9,25},{13,29},{10,26},{14,30},{11,27},{15,31}} | collective-permute-start | bytes 196616 | tf_op jit(solution)/shard_map/ppermute | solution.py:814
  49.6 1.5 %collective-permute-start.11 = (bf16[2,128,128]{2,1,0:T(8,128)(2,1)S(1)}, bf16[2,128,128]{2,1,0:T(8,128)(2,1)S(1)}, u32[]{:S(2)}, u32[]{:S(2)}) collective-permute-start(bf16[2,128,128]{2,1,0:T(8,128)(2,1)S(1)} %slice.15), channel_id=1, source_target_pairs={{8,16},{12,20},{9,17},{13,21},{10,18},{14,22},{11,19},{15,23}} | collective-permute-start | bytes 196616 | tf_op jit(solution)/shard_map/ppermute | solution.py:814
  51.0 1.4 %shard_map.89 = (f32[128,512]{1,0:T(8,128)S(1)}, f32[256,512]{1,0:T(8,128)S(1)}, f32[128,512]{1,0:T(8,128)S(1)}) custom-call(bf16[128,2048]{1,0:T(8,128)(2,1)S(1)} %copy-done, bf16[128,2048]{1,0:T(8,128)(2,1)S(1)} %collective-permute-done.refs_1_, bf16[128,2048]{1,0:T(8,128)(2,1)S(1)} %collective-permute-done.1.refs_2_, ...), custom_call_target="tpu_custom_call" | custom-call | flops 3000000000 | bytes 1048576 | tf_op jit(solution)/shard_map/pallas_call | solution.py:645
  52.5 6.0 %collective-permute-done.11.refs_0_ = bf16[2,128,128]{2,1,0:T(8,128)(2,1)S(1)} collective-permute-done((bf16[2,128,128]{2,1,0:T(8,128)(2,1)S(1)}, bf16[2,128,128]{2,1,0:T(8,128)(2,1)S(1)}, u32[]{:S(2)}, u32[]{:S(2)}) %collective-permute-start.11) | collective-permute-done | bytes 65568 | tf_op jit(solution)/shard_map/ppermute | solution.py:814
  58.6 1.6 %collective-permute-start.13 = (bf16[2,128,128]{2,1,0:T(8,128)(2,1)S(1)}, bf16[2,128,128]{2,1,0:T(8,128)(2,1)S(1)}, u32[]{:S(2)}, u32[]{:S(2)}) collective-permute-start(bf16[2,128,128]{2,1,0:T(8,128)(2,1)S(1)} %shard_map.88.mine_ref), channel_id=1, source_target_pairs={{0,4},{4,0},{8,12},{12,8},{16,20},{20,16},{24,28},{28,24},{1,5},{5... | collective-permute-start | bytes 196616 | tf_op jit(solution)/shard_map/ppermute | solution.py:828
  60.2 2.8 %shard_map.85 = (bf16[4,512,128]{2,1,0:T(8,128)(2,1)S(1)}, f32[4,512,128]{2,1,0:T(8,128)S(1)}) custom-call(bf16[4,4,128,256]{3,2,1,0:T(8,128)(2,1)S(1)} %get-tuple-element.32.both_ref, bf16[4,4,128,256]{3,2,1,0:T(8,128)(2,1)S(1)} %get-tuple-element.33.low_ref, bf16[12,256,128]{2,1,0:T(8,128)(2,1)S(1)} %get-tuple-element.25.act_e, ...), custom_call_target="tpu_custom_call" | custom-call | flops 2000000000 | bytes 1048576 | tf_op jit(solution)/shard_map/pallas_call | solution.py:645
  63.0 1.8 %shard_map.90 = bf16[512,512]{1,0:T(8,128)(2,1)} custom-call(bf16[4,512,128]{2,1,0:T(8,128)(2,1)S(1)} %get-tuple-element.37.qp_ref, f32[4,512,128]{2,1,0:T(8,128)S(1)} %get-tuple-element.38.o_ref, bf16[4,128,256]{2,1,0:T(8,128)(2,1)S(1)} %collective-permute-done.9.other_ref.pair_ref, bf16[2,128,128]{2,1,0:T(8,128)(2,1)S(1)} %shard_map.88.mine_ref, ...), custom_call_target="tpu_custom_call" | custom-call | flops 50000000 | bytes 1048576 | tf_op jit(solution)/shard_map/pallas_call | solution.py:645
  (36 shorter events, 1.0 us)
Async XLA Ops:
  0.0 25.1 %slice-start = ((s8[6291456]{0:T(1024)(128)(4,1)}), s8[4194304]{0:T(1024)(128)(4,1)S(1)}, s32[]{:S(2)}) async-start(s8[6291456]{0:T(1024)(128)(4,1)} %bitcast.7), calls=%async_computation | async-start | bytes 8388608
  0.9 24.2 %copy-start = (bf16[128,2048]{1,0:T(8,128)(2,1)S(1)}, bf16[128,2048]{1,0:T(8,128)(2,1)}, u32[]{:S(2)}) copy-start(bf16[128,2048]{1,0:T(8,128)(2,1)} %refs_0_.3) | copy-start | bytes 1572868
  0.9 24.2 %slice-start.1 = ((s8[6291456]{0:T(1024)(128)(4,1)}), s8[2097152]{0:T(1024)(128)(4,1)S(1)}, s32[]{:S(2)}) async-start(s8[6291456]{0:T(1024)(128)(4,1)} %bitcast.7), calls=%async_computation.1 | async-start | bytes 4194304
  0.9 24.2 %copy-start.3 = (bf16[2048,2,4]{0,2,1:T(4,128)(2,1)S(1)}, bf16[2048,2,4]{0,2,1:T(4,128)(2,1)}, u32[]{:S(2)}) copy-start(bf16[2048,2,4]{0,2,1:T(4,128)(2,1)} %param.11) | copy-start | bytes 98308
  0.9 24.2 %copy-start.4 = (bf16[4,3,512]{2,0,1:T(4,128)(2,1)S(1)}, bf16[4,3,512]{2,0,1:T(4,128)(2,1)}, u32[]{:S(2)}) copy-start(bf16[4,3,512]{2,0,1:T(4,128)(2,1)} %param.12) | copy-start | bytes 36868
  0.9 24.2 %copy-start.5 = (f32[4]{0:T(128)S(1)}, f32[4]{0:T(128)}, u32[]{:S(2)}) copy-start(f32[4]{0:T(128)} %param.13) | copy-start | bytes 52
  0.9 24.2 %copy-start.6 = (f32[4]{0:T(128)S(1)}, f32[4]{0:T(128)}, u32[]{:S(2)}) copy-start(f32[4]{0:T(128)} %param.14) | copy-start | bytes 52
  1.0 22.3 %collective-permute-start.4 = (bf16[8,2048]{1,0:T(8,128)(2,1)S(1)}, bf16[8,2048]{1,0:T(8,128)(2,1)S(1)}, u32[]{:S(2)}, u32[]{:S(2)}) collective-permute-start(bf16[8,2048]{1,0:T(8,128)(2,1)S(1)} %slice.12), channel_id=1, source_target_pairs={{3,6},{7,10},{11,14},{15,18},{19,22},{23,26},{27,30}} | collective-permute-start | bytes 98312 | tf_op jit(solution)/shard_map/ppermute | solution.py:69
  2.5 22.6 %collective-permute-start.3 = (bf16[8,2048]{1,0:T(8,128)(2,1)S(1)}, bf16[8,2048]{1,0:T(8,128)(2,1)S(1)}, u32[]{:S(2)}, u32[]{:S(2)}) collective-permute-start(bf16[8,2048]{1,0:T(8,128)(2,1)S(1)} %slice.12), channel_id=1, source_target_pairs={{3,5},{7,9},{11,13},{15,17},{19,21},{23,25},{27,29}} | collective-permute-start | bytes 98312 | tf_op jit(solution)/shard_map/ppermute | solution.py:69
  3.2 21.9 %collective-permute-start.2 = (bf16[8,2048]{1,0:T(8,128)(2,1)S(1)}, bf16[8,2048]{1,0:T(8,128)(2,1)S(1)}, u32[]{:S(2)}, u32[]{:S(2)}) collective-permute-start(bf16[8,2048]{1,0:T(8,128)(2,1)S(1)} %slice.12), channel_id=1, source_target_pairs={{0,3},{1,2},{2,1},{3,0},{4,7},{5,6},{6,5},{7,4},{8,11},{9,10},{10,... | collective-permute-start | bytes 98312 | tf_op jit(solution)/shard_map/ppermute | solution.py:71
  4.4 16.3 %collective-permute-start.1 = (bf16[128,2048]{1,0:T(8,128)(2,1)}, bf16[128,2048]{1,0:T(8,128)(2,1)S(1)}, u32[]{:S(2)}, u32[]{:S(2)}) collective-permute-start(bf16[128,2048]{1,0:T(8,128)(2,1)} %refs_0_.3), channel_id=1, source_target_pairs={{0,2},{1,3},{2,0},{3,1},{4,6},{5,7},{6,4},{7,5},{8,10},{9,11},{10,... | collective-permute-start | bytes 1572872 | tf_op jit(solution)/shard_map/ppermute | solution.py:43
  8.7 13.8 %collective-permute-start = (bf16[128,2048]{1,0:T(8,128)(2,1)}, bf16[128,2048]{1,0:T(8,128)(2,1)S(1)}, u32[]{:S(2)}, u32[]{:S(2)}) collective-permute-start(bf16[128,2048]{1,0:T(8,128)(2,1)} %refs_0_.3), channel_id=1, source_target_pairs={{0,1},{1,0},{2,3},{3,2},{4,5},{5,4},{6,7},{7,6},{8,9},{9,8},{10,11... | collective-permute-start | bytes 1572872 | tf_op jit(solution)/shard_map/ppermute | solution.py:43
  20.7 9.9 %collective-permute-start.8 = (bf16[8,2048]{1,0:T(8,128)(2,1)S(1)}, bf16[8,2048]{1,0:T(8,128)(2,1)S(1)}, u32[]{:S(2)}, u32[]{:S(2)}) collective-permute-start(bf16[8,2048]{1,0:T(8,128)(2,1)S(1)} %slice.12), channel_id=1, source_target_pairs={{3,7},{7,11},{11,15},{15,19},{19,23},{23,27},{27,31}} | collective-permute-start | bytes 98312 | tf_op jit(solution)/shard_map/ppermute | solution.py:69
  22.6 8.1 %collective-permute-start.7 = (bf16[8,2048]{1,0:T(8,128)(2,1)S(1)}, bf16[8,2048]{1,0:T(8,128)(2,1)S(1)}, u32[]{:S(2)}, u32[]{:S(2)}) collective-permute-start(bf16[8,2048]{1,0:T(8,128)(2,1)S(1)} %slice.12), channel_id=1, source_target_pairs={{3,4},{7,8},{11,12},{15,16},{19,20},{23,24},{27,28}} | collective-permute-start | bytes 98312 | tf_op jit(solution)/shard_map/ppermute | solution.py:69
  23.3 7.7 %collective-permute-start.5 = (bf16[64,2048]{1,0:T(8,128)(2,1)S(1)}, bf16[64,2048]{1,0:T(8,128)(2,1)S(1)}, u32[]{:S(2)}, u32[]{:S(2)}) collective-permute-start(bf16[64,2048]{1,0:T(8,128)(2,1)S(1)} %slice.16), channel_id=1, source_target_pairs={{0,1},{1,0},{2,3},{3,2},{4,5},{5,4},{6,7},{7,6},{8,9},{9,8},{10,11... | collective-permute-start | bytes 786440 | tf_op jit(solution)/shard_map/ppermute | solution.py:43
  25.1 6.3 %collective-permute-start.6 = (bf16[64,2048]{1,0:T(8,128)(2,1)S(1)}, bf16[64,2048]{1,0:T(8,128)(2,1)S(1)}, u32[]{:S(2)}, u32[]{:S(2)}) collective-permute-start(bf16[64,2048]{1,0:T(8,128)(2,1)S(1)} %slice.17), channel_id=1, source_target_pairs={{0,2},{1,3},{2,0},{3,1},{4,6},{5,7},{6,4},{7,5},{8,10},{9,11},{10,... | collective-permute-start | bytes 786440 | tf_op jit(solution)/shard_map/ppermute | solution.py:43
  30.6 20.4 %copy-start.2 = (bf16[2048,512]{1,0:T(8,128)(2,1)S(1)}, bf16[2048,512]{1,0:T(8,128)(2,1)}, u32[]{:S(2)}) copy-start(bf16[2048,512]{1,0:T(8,128)(2,1)} %refs_5_.1) | copy-start | bytes 6291460
  40.8 3.7 %collective-permute-start.9 = (bf16[4,128,256]{2,1,0:T(8,128)(2,1)S(1)}, bf16[4,128,256]{2,1,0:T(8,128)(2,1)S(1)}, u32[]{:S(2)}, u32[]{:S(2)}) collective-permute-start(bf16[4,128,256]{2,1,0:T(8,128)(2,1)S(1)} %get-tuple-element.39.mine_ref), channel_id=1, source_target_pairs={{0,4},{4,0},{8,12},{12,8},{16,20},{20,16},{24,28},{28,24},{1,5},{5... | collective-permute-start | bytes 786440 | tf_op jit(solution)/shard_map/ppermute | solution.py:797
  44.6 4.0 %collective-permute-start.10 = (bf16[2,128,256]{2,1,0:T(8,128)(2,1)S(1)}, bf16[2,128,256]{2,1,0:T(8,128)(2,1)S(1)}, u32[]{:S(2)}, u32[]{:S(2)}) collective-permute-start(bf16[2,128,256]{2,1,0:T(8,128)(2,1)S(1)} %shard_map.86.block_ref), channel_id=1, source_target_pairs={{0,8},{4,12},{16,24},{20,28},{1,9},{5,13},{17,25},{21,29},{2,10},{... | collective-permute-start | bytes 393224 | tf_op jit(solution)/shard_map/ppermute | solution.py:814
  48.9 3.6 %collective-permute-start.12 = (bf16[2,128,128]{2,1,0:T(8,128)(2,1)S(1)}, bf16[2,128,128]{2,1,0:T(8,128)(2,1)S(1)}, u32[]{:S(2)}, u32[]{:S(2)}) collective-permute-start(bf16[2,128,128]{2,1,0:T(8,128)(2,1)S(1)} %slice.15), channel_id=1, source_target_pairs={{8,24},{12,28},{9,25},{13,29},{10,26},{14,30},{11,27},{15,31}} | collective-permute-start | bytes 196616 | tf_op jit(solution)/shard_map/ppermute | solution.py:814
  49.6 8.9 %collective-permute-start.11 = (bf16[2,128,128]{2,1,0:T(8,128)(2,1)S(1)}, bf16[2,128,128]{2,1,0:T(8,128)(2,1)S(1)}, u32[]{:S(2)}, u32[]{:S(2)}) collective-permute-start(bf16[2,128,128]{2,1,0:T(8,128)(2,1)S(1)} %slice.15), channel_id=1, source_target_pairs={{8,16},{12,20},{9,17},{13,21},{10,18},{14,22},{11,19},{15,23}} | collective-permute-start | bytes 196616 | tf_op jit(solution)/shard_map/ppermute | solution.py:814
  52.5 10.5 %copy-start.1 = (f32[128]{0:T(128)S(1)}, f32[128]{0:T(128)}, u32[]{:S(2)}) copy-start(f32[128]{0:T(128)} %param.15) | copy-start | bytes 1540
  58.6 4.3 %collective-permute-start.13 = (bf16[2,128,128]{2,1,0:T(8,128)(2,1)S(1)}, bf16[2,128,128]{2,1,0:T(8,128)(2,1)S(1)}, u32[]{:S(2)}, u32[]{:S(2)}) collective-permute-start(bf16[2,128,128]{2,1,0:T(8,128)(2,1)S(1)} %shard_map.88.mine_ref), channel_id=1, source_target_pairs={{0,4},{4,0},{8,12},{12,8},{16,20},{20,16},{24,28},{28,24},{1,5},{5... | collective-permute-start | bytes 196616 | tf_op jit(solution)/shard_map/ppermute | solution.py:828

commit v8 on v7

--- a/solution.py
+++ b/solution.py
@@ -334,11 +334,11 @@
 
 
 def early_kernel(heads, blocks, *refs):
-    count = 2 * blocks - 2
+    count = 2 * blocks
     tokens_refs = refs[:blocks]
     part_refs = refs[blocks:count]
     w_ref, small_ref, taps_ref, rate_ref, bias_ref = refs[count:count + 5]
-    act, cols, rows_of, own_ref, own_sc_ref, own_rim_ref, late_rim_ref, xp, sc, tails = refs[count + 5:]
+    act, cols, rows_of, rim_ref, xp, sc, tails = refs[count + 5:]
     early = blocks - 1
     span = RIM + CHUNK
     mid = early * CHUNK
@@ -348,21 +348,17 @@
         before = before + ref[...].astype(f32)
     edge = jnp.concatenate([tokens_refs[-1][...].astype(f32), before], axis=0)
     tokens = jnp.concatenate([ref[...] for ref in tokens_refs[:-1]] + [edge.astype(bf16)], axis=0)
-    raw = dot(tokens[:mid], scalar_weights(small_ref), (1, 1))
-    own_sc_ref[...] = raw[:CHUNK]
-    sc[...] = raw[CHUNK:]
+    sc[...] = dot(tokens[:mid], scalar_weights(small_ref), (1, 1))
 
     def fill(branch, carry):
         made = dot(tokens, w_ref[branch]).astype(bf16).astype(f32)
         for head in range(heads):
             tile = branch * heads + head
             lanes = slice(head * LANES, (head + 1) * LANES)
-            own_ref[tile] = made[:CHUNK, lanes]
             for m in range(early):
+                at = m * span
                 block = made[m * CHUNK:(m + 1) * CHUNK, lanes]
-                if m > 0:
-                    at = (m - 1) * span
-                    xp[tile, at + RIM:at + span] = block
+                xp[tile, at + RIM:at + span] = block
                 tails[m, tile] = block[CHUNK - RIM:]
             tails[early, tile] = made[mid:mid + RIM, lanes]
             tails[blocks, tile] = made[mid + RIM:, lanes]
@@ -375,13 +371,12 @@
         index = lax.bitwise_xor(me, m)
         return jnp.where(index == 0, blocks, lax.bitwise_xor(me, jnp.maximum(index - 1, 0)))
 
-    own_rim_ref[...] = tails[ahead_of(0)]
-    late_rim_ref[...] = tails[ahead_of(early)]
-
-    def prepare(slot, carry):
-        at = pl.ds(pl.multiple_of(slot * CHUNK, CHUNK), CHUNK)
-        base = pl.multiple_of(slot * span, 8)
-        source = ahead_of(slot + 1)
+    rim_ref[...] = tails[ahead_of(early)]
+
+    def prepare(m, carry):
+        at = pl.ds(pl.multiple_of(m * CHUNK, CHUNK), CHUNK)
+        base = pl.multiple_of(m * span, 8)
+        source = ahead_of(m)
         for tile in range(3 * heads):
             xp[tile, pl.ds(base, RIM)] = tails[source, tile]
 
@@ -389,11 +384,11 @@
             act[tile, at] = value
 
         comb = convolve(heads, xp, base, taps_ref, sc[at], rate, bias, keep)
-        cols[slot] = comb
-        rows_of[slot] = comb.T
+        cols[m] = comb
+        rows_of[m] = comb.T
         return carry
 
-    lax.fori_loop(0, early - 1, prepare, 0)
+    lax.fori_loop(0, early, prepare, 0)
 
 
 def masks_kernel(out_ref):
@@ -405,67 +400,58 @@
 
 
 def block_delta_kernel(
-    heads, blocks, act_e, cols_e, rows_e, own_ref, own_sc_ref, own_rim_ref, late_rim_ref,
-    late0_ref, late1_ref, part0_ref, part1_ref, w_ref, small_ref, taps_ref, rate_ref, bias_ref,
-    masks, x_ref, both_ref, low_ref, act_l, cols_l, rows_l, xp, sc, mixes, solves, changes, lasts,
+    heads, blocks, act_e, cols_e, rows_e, rim_ref, late0_ref, late1_ref, w_ref, small_ref,
+    taps_ref, rate_ref, bias_ref, masks, x_ref, both_ref, low_ref, act_l, cols_l, rows_l,
+    xp, mixes, solves, changes, lasts,
 ):
     me = lax.axis_index("tp")
-    span = RIM + CHUNK
-    before = part0_ref[...].astype(f32) + part1_ref[...].astype(f32)
-    before = jnp.concatenate([before, jnp.zeros_like(before)], axis=0)
-    tokens = jnp.concatenate([late0_ref[...], late1_ref[...], before.astype(bf16)], axis=0)
-    sc[:CHUNK] = own_sc_ref[...]
-    sc[CHUNK:] = dot(tokens[:CHUNK], scalar_weights(small_ref), (1, 1))
+    late = jnp.concatenate([late0_ref[...], late1_ref[...]], axis=0)
+    raw = dot(late, scalar_weights(small_ref), (1, 1))
 
     def fill(branch, carry):
-        made = dot(tokens, w_ref[branch]).astype(bf16).astype(f32)
+        made = dot(late, w_ref[branch]).astype(bf16).astype(f32)
         for head in range(heads):
             tile = branch * heads + head
             lanes = slice(head * LANES, (head + 1) * LANES)
-            rim = made[CHUNK:CHUNK + RIM, lanes]
-            xp[tile, :RIM] = jnp.where(me == 0, rim, own_rim_ref[tile])
-            xp[tile, RIM:span] = own_ref[tile]
-            xp[tile, span:span + RIM] = jnp.where(me == blocks - 1, rim, late_rim_ref[tile])
-            xp[tile, span + RIM:] = made[:CHUNK, lanes]
+            xp[tile, :RIM] = rim_ref[tile]
+            xp[tile, RIM:] = made[:, lanes]
         return carry
 
     lax.fori_loop(0, 3, fill, 0)
-    rate, bias = -lane_row(rate_ref), lane_row(bias_ref)
-
-    def prepare(slot, carry):
-        at = pl.ds(pl.multiple_of(slot * CHUNK, CHUNK), CHUNK)
-
-        def keep(tile, value):
-            act_l[tile, at] = value
-
-        base = pl.multiple_of(slot * span, 8)
-        comb = convolve(heads, xp, base, taps_ref, sc[at], rate, bias, keep)
-        cols_l[slot] = comb
-        rows_l[slot] = comb.T
-        return carry
-
-    lax.fori_loop(0, 2, prepare, 0)
+
+    def keep(tile, value):
+        act_l[tile] = value
+
+    comb = convolve(
+        heads, xp, 0, taps_ref, raw, -lane_row(rate_ref), lane_row(bias_ref), keep
+    )
+    cols_l[0] = comb
+    rows_l[0] = comb.T
 
     ri, ci = grid_index((CHUNK, CHUNK))
     levels = masks.shape[0]
 
     def part(branch, head, m):
-        held, slot = (act_e, m - 1) if 0 < m < blocks - 1 else (act_l, min(m, 1))
-        return held[branch * heads + head, slot * CHUNK:(slot + 1) * CHUNK]
+        tile = branch * heads + head
+        if m == blocks - 1:
+            return act_l[tile]
+        return act_e[tile, m * CHUNK:(m + 1) * CHUNK]
 
     def col(kind, head, m):
         lane = kind * heads + head
-        held, slot = (cols_e, m - 1) if 0 < m < blocks - 1 else (cols_l, min(m, 1))
-        return held[slot, :, lane:lane + 1]
+        if m == blocks - 1:
+            return cols_l[0, :, lane:lane + 1]
+        return cols_e[m, :, lane:lane + 1]
 
     def row(kind, head, m):
         lane = kind * heads + head
-        held, slot = (rows_e, m - 1) if 0 < m < blocks - 1 else (rows_l, min(m, 1))
-        return held[slot, lane:lane + 1, :]
+        if m == blocks - 1:
+            return rows_l[0, lane:lane + 1, :]
+        return rows_e[m, lane:lane + 1, :]
 
     for m in range(blocks):
-        held, slot = (cols_e, m - 1) if 0 < m < blocks - 1 else (cols_l, min(m, 1))
-        lasts[m] = jnp.exp(held[slot, CHUNK - 8:])
+        source = cols_l[0] if m == blocks - 1 else cols_e[m]
+        lasts[m] = jnp.exp(source[CHUNK - 8:])
 
     sets = [(head, m) for m in range(0, blocks, 2) for head in range(heads)]
     for s, (head, first) in enumerate(sets):
@@ -532,12 +518,11 @@
     for head in range(heads):
         for m in range(blocks):
             at = slice(m * CHUNK, (m + 1) * CHUNK)
-            middle = 0 < m < blocks - 1
-            slot = m - 1 if middle else min(m, 1)
-            act, cols_of, rows_of = (act_e, cols_e, rows_e) if middle else (act_l, cols_l, rows_l)
-            held = slice(slot * CHUNK, (slot + 1) * CHUNK)
-            cols, rows = cols_of[slot], rows_of[slot]
-            q, k = act[head, held], act[heads + head, held]
+            final = m == blocks - 1
+            cols = cols_l[0] if final else cols_e[m]
+            rows = rows_l[0] if final else rows_e[m]
+            q = act_l[head] if final else act_e[head, at]
+            k = act_l[heads + head] if final else act_e[heads + head, at]
             decay = cols[:, head:head + 1]
             norm = cols[:, 2 * heads + head:2 * heads + head + 1]
             gap = decay - rows[head:head + 1]
@@ -683,7 +668,7 @@
             [*tokens, *weights], flops=PROJECT_FLOPS, limit=20,
         )
 
-    by_block = rows == CHUNK and len(early) == blocks - 2 and blocks > 2
+    by_block = rows == CHUNK and len(early) == blocks - 2 and blocks % 2 == 0
     if by_block:
         parts, across = rim_rows(hidden, RIM)
         masks = call(
@@ -691,25 +676,22 @@
             shape((CHUNK.bit_length() - 1, CHUNK, 2 * CHUNK), bf16), [],
             flops=MASKS_FLOPS, limit=4,
         )
-        act_e, cols_e, rows_e, own_f, own_sc, own_rim, late_rim = call(
+        act_e, cols_e, rows_e, late_rim = call(
             functools.partial(early_kernel, heads, blocks),
             (
-                shape((3 * heads, seq_rows - 2 * rows, dim), bf16),
-                shape((blocks - 2, CHUNK, LANES), f32),
-                shape((blocks - 2, CHUNK, LANES), f32),
-                shape((3 * heads, rows, dim), f32),
-                shape((rows, LANES), f32),
-                shape((3 * heads, RIM, dim), f32),
+                shape((3 * heads, seq_rows - rows, dim), bf16),
+                shape((blocks - 1, CHUNK, LANES), f32),
+                shape((blocks - 1, CHUNK, LANES), f32),
                 shape((3 * heads, RIM, dim), f32),
             ),
             [
-                hidden, *early, across, *parts[1:-1],
+                hidden, *early, across, *parts,
                 w_three, small, taps, rate, bias,
             ],
             flops=PROJECT_FLOPS,
             scratch=[
-                pltpu.VMEM((3 * heads, (blocks - 2) * (RIM + CHUNK), dim), f32),
-                pltpu.VMEM((seq_rows - 2 * rows, LANES), f32),
+                pltpu.VMEM((3 * heads, (blocks - 1) * (RIM + CHUNK), dim), f32),
+                pltpu.VMEM((seq_rows - rows, LANES), f32),
                 pltpu.VMEM((blocks + 1, 3 * heads, RIM, dim), f32),
             ],
         )
@@ -719,18 +701,14 @@
                 shape((heads, dim, 2 * dim), bf16),
                 shape((heads, blocks, CHUNK, 2 * dim), bf16),
                 shape((heads, blocks, dim, 2 * dim), bf16),
-                shape((3 * heads, 2 * rows, dim), bf16),
-                shape((2, CHUNK, LANES), f32),
-                shape((2, CHUNK, LANES), f32),
+                shape((3 * heads, rows, dim), bf16),
+                shape((1, CHUNK, LANES), f32),
+                shape((1, CHUNK, LANES), f32),
             ),
-            [
-                act_e, cols_e, rows_e, own_f, own_sc, own_rim, late_rim, *late,
-                parts[0], parts[-1], w_three, small, taps, rate, bias, masks,
-            ],
+            [act_e, cols_e, rows_e, late_rim, *late, w_three, small, taps, rate, bias, masks],
             flops=DELTA_FLOPS, limit=28,
             scratch=[
-                pltpu.VMEM((3 * heads, 2 * (RIM + CHUNK), dim), f32),
-                pltpu.VMEM((2 * rows, LANES), f32),
+                pltpu.VMEM((3 * heads, RIM + CHUNK, dim), f32),
                 pltpu.VMEM((heads * blocks // 2, CHUNK, 2 * CHUNK), bf16),
                 pltpu.VMEM((heads * blocks // 2, CHUNK, 2 * CHUNK), f32),
                 pltpu.VMEM((blocks, heads, dim, 2 * dim), f32),

time: 65 us -> 59.3 us (0.912)
  the two profiles are of different devices: /device:TPU:21 before, /device:TPU:17 now
where the time goes in v8:
time: 59.3 us; the launch traced here: 59.1 us
  Pallas kernels  21.1 us (36%)
  starting transfers between devices  19.8 us (33%)
  waiting for transfers between devices  16.8 us (28%)
  local copies, waits for them, and re-layouts  1 us (2%)
    pallas_call x9, Pallas kernels, call(): pl.pallas_call(kernel, out_shape=out, in_specs=[whole()] * len(operands),...  21.1 us
    ppermute x3, waiting for transfers between devices, per_device(): parts.append(lax.ppermute(sent, 'seq', route))  7.41 us
    ppermute x4, waiting for transfers between devices, swap(): return lax.ppermute(value, axis, [(i, i ^ step) for i in range(count)])  7.34 us
    ppermute x1, starting transfers between devices, rim_rows(): across = lax.ppermute(tail, 'tp', route)  5.47 us
    ppermute x3, starting transfers between devices, per_device(): parts.append(lax.ppermute(sent, 'seq', route))  5.42 us
    ppermute x4, starting transfers between devices, rim_rows(): parts.append(lax.ppermute(tail, ('seq', 'tp'), route))  3.53 us
    ppermute x4, starting transfers between devices, swap(): return lax.ppermute(value, axis, [(i, i ^ step) for i in range(count)])  2.8 us
    ppermute x1, starting transfers between devices, per_device(): back = lax.ppermute(state, 'seq', swap) if share else state  2.13 us
  transfers between devices with their start and end apart: 14, of which 5 were waited for; matrix products, arithmetic and copies ran while one was open for 2% of the time, Pallas kernels for 18%

profile of v8, /device:TPU:17, one launch (start us, length us, event | category | flops | bytes accessed | tf_op | source)
XLA Modules:
  0.0 59.1 jit_solution(13334854747488999960)
XLA Ops:
  0.0 1.2 %collective-permute-start.1 = (bf16[128,2048]{1,0:T(8,128)(2,1)}, bf16[128,2048]{1,0:T(8,128)(2,1)S(1)}, u32[]{:S(2)}, u32[]{:S(2)}) collective-permute-start(bf16[128,2048]{1,0:T(8,128)(2,1)} %refs_0_.3), channel_id=1, source_target_pairs={{0,2},{1,3},{2,0},{3,1},{4,6},{5,7},{6,4},{7,5},{8,10},{9,11},{10,... | collective-permute-start | bytes 1572872 | tf_op jit(solution)/shard_map/ppermute | solution.py:43
  1.2 1.2 %collective-permute-start = (bf16[128,2048]{1,0:T(8,128)(2,1)}, bf16[128,2048]{1,0:T(8,128)(2,1)S(1)}, u32[]{:S(2)}, u32[]{:S(2)}) collective-permute-start(bf16[128,2048]{1,0:T(8,128)(2,1)} %refs_0_.3), channel_id=1, source_target_pairs={{0,1},{1,0},{2,3},{3,2},{4,5},{5,4},{6,7},{7,6},{8,9},{9,8},{10,11... | collective-permute-start | bytes 1572872 | tf_op jit(solution)/shard_map/ppermute | solution.py:43
  2.5 0.9 %slice.12 = bf16[8,2048]{1,0:T(8,128)(2,1)S(1)} slice(bf16[128,2048]{1,0:T(8,128)(2,1)} %refs_0_.3), slice={[120:128], [0:2048]} | slice | bytes 65536 | tf_op jit(solution)/shard_map/slice | solution.py:65
  3.4 0.8 %collective-permute-start.6 = (bf16[8,2048]{1,0:T(8,128)(2,1)S(1)}, bf16[8,2048]{1,0:T(8,128)(2,1)S(1)}, u32[]{:S(2)}, u32[]{:S(2)}) collective-permute-start(bf16[8,2048]{1,0:T(8,128)(2,1)S(1)} %slice.12), channel_id=1, source_target_pairs={{3,7},{7,11},{11,15},{15,19},{19,23},{23,27},{27,31}} | collective-permute-start | bytes 98312 | tf_op jit(solution)/shard_map/ppermute | solution.py:69
  4.2 0.8 %collective-permute-start.5 = (bf16[8,2048]{1,0:T(8,128)(2,1)S(1)}, bf16[8,2048]{1,0:T(8,128)(2,1)S(1)}, u32[]{:S(2)}, u32[]{:S(2)}) collective-permute-start(bf16[8,2048]{1,0:T(8,128)(2,1)S(1)} %slice.12), channel_id=1, source_target_pairs={{3,6},{7,10},{11,14},{15,18},{19,22},{23,26},{27,30}} | collective-permute-start | bytes 98312 | tf_op jit(solution)/shard_map/ppermute | solution.py:69
  5.0 0.7 %collective-permute-start.4 = (bf16[8,2048]{1,0:T(8,128)(2,1)S(1)}, bf16[8,2048]{1,0:T(8,128)(2,1)S(1)}, u32[]{:S(2)}, u32[]{:S(2)}) collective-permute-start(bf16[8,2048]{1,0:T(8,128)(2,1)S(1)} %slice.12), channel_id=1, source_target_pairs={{3,5},{7,9},{11,13},{15,17},{19,21},{23,25},{27,29}} | collective-permute-start | bytes 98312 | tf_op jit(solution)/shard_map/ppermute | solution.py:69
  5.7 7.3 %collective-permute-done.1.refs_2_ = bf16[128,2048]{1,0:T(8,128)(2,1)S(1)} collective-permute-done((bf16[128,2048]{1,0:T(8,128)(2,1)}, bf16[128,2048]{1,0:T(8,128)(2,1)S(1)}, u32[]{:S(2)}, u32[]{:S(2)}) %collective-permute-start.1) | collective-permute-done | bytes 524320 | tf_op jit(solution)/shard_map/ppermute | solution.py:43
  13.0 1.3 %collective-permute-start.3 = (bf16[8,2048]{1,0:T(8,128)(2,1)S(1)}, bf16[8,2048]{1,0:T(8,128)(2,1)S(1)}, u32[]{:S(2)}, u32[]{:S(2)}) collective-permute-start(bf16[8,2048]{1,0:T(8,128)(2,1)S(1)} %slice.12), channel_id=1, source_target_pairs={{3,4},{7,8},{11,12},{15,16},{19,20},{23,24},{27,28}} | collective-permute-start | bytes 98312 | tf_op jit(solution)/shard_map/ppermute | solution.py:69
  14.3 5.5 %collective-permute-start.2 = (bf16[8,2048]{1,0:T(8,128)(2,1)S(1)}, bf16[8,2048]{1,0:T(8,128)(2,1)S(1)}, u32[]{:S(2)}, u32[]{:S(2)}) collective-permute-start(bf16[8,2048]{1,0:T(8,128)(2,1)S(1)} %slice.12), channel_id=1, source_target_pairs={{0,3},{1,2},{2,1},{3,0},{4,7},{5,6},{6,5},{7,4},{8,11},{9,10},{10,... | collective-permute-start | bytes 98312 | tf_op jit(solution)/shard_map/ppermute | solution.py:71
  20.0 0.3 collective-permute-start.8
  20.3 0.9 %collective-permute-done.2.refs_3_ = bf16[8,2048]{1,0:T(8,128)(2,1)S(1)} collective-permute-done((bf16[8,2048]{1,0:T(8,128)(2,1)S(1)}, bf16[8,2048]{1,0:T(8,128)(2,1)S(1)}, u32[]{:S(2)}, u32[]{:S(2)}) %collective-permute-start.2) | collective-permute-done | bytes 32800 | tf_op jit(solution)/shard_map/ppermute | solution.py:71
  21.3 6.3 %shard_map.82 = (bf16[12,384,128]{2,1,0:T(8,128)(2,1)S(1)}, f32[3,128,128]{2,1,0:T(8,128)S(1)}, f32[3,128,128]{2,1,0:T(8,128)S(1)}, f32[12,8,128]{2,1,0:T(8,128)S(1)}) custom-call(bf16[128,2048]{1,0:T(8,128)(2,1)S(1)} %copy-done, bf16[128,2048]{1,0:T(8,128)(2,1)S(1)} %collective-permute-done.refs_1_, bf16[128,2048]{1,0:T(8,128)(2,1)S(1)} %collective-permute-done.1.refs_2_, ...), custom_call_target="tpu_custom_call" | custom-call | flops 3000000000 | bytes 1048576 | tf_op jit(solution)/shard_map/pallas_call | solution.py:630
  27.6 8.2 %shard_map.84 = (bf16[4,128,256]{2,1,0:T(8,128)(2,1)S(1)}, bf16[4,4,128,256]{3,2,1,0:T(8,128)(2,1)S(1)}, bf16[4,4,128,256]{3,2,1,0:T(8,128)(2,1)S(1)}, bf16[12,1...) custom-call(bf16[12,384,128]{2,1,0:T(8,128)(2,1)S(1)} %get-tuple-element.22.act_e, ...), custom_call_target="tpu_custom_call" | custom-call | flops 3000000000 | bytes 1048576 | tf_op jit(solution)/shard_map/pallas_call | solution.py:630
  35.9 0.4 collective-permute-start.9
  36.3 1.2 %collective-permute-done.9.other_ref.pair_ref = bf16[4,128,256]{2,1,0:T(8,128)(2,1)S(1)} collective-permute-done((bf16[4,128,256]{2,1,0:T(8,128)(2,1)S(1)}, bf16[4,128,256]{2,1,0:T(8,128)(2,1)S(1)}, u32[]{:S(2)}, u32[]{:S(2)}) %collective-permute-start.9) | collective-permute-done | bytes 262176 | tf_op jit(solution)/shard_map/ppermute | solution.py:775
  37.7 3.3 %collective-permute-start.10 = (bf16[2,128,256]{2,1,0:T(8,128)(2,1)S(1)}, bf16[2,128,256]{2,1,0:T(8,128)(2,1)S(1)}, u32[]{:S(2)}, u32[]{:S(2)}) collective-permute-start(bf16[2,128,256]{2,1,0:T(8,128)(2,1)S(1)} %shard_map.86.block_ref), channel_id=1, source_target_pairs={{0,8},{4,12},{16,24},{20,28},{1,9},{5,13},{17,25},{21,29},{2,10},{... | collective-permute-start | bytes 393224 | tf_op jit(solution)/shard_map/ppermute | solution.py:792
  41.0 2.5 %collective-permute-done.10.sent_ref = bf16[2,128,256]{2,1,0:T(8,128)(2,1)S(1)} collective-permute-done((bf16[2,128,256]{2,1,0:T(8,128)(2,1)S(1)}, bf16[2,128,256]{2,1,0:T(8,128)(2,1)S(1)}, u32[]{:S(2)}, u32[]{:S(2)}) %collective-permute-start.10) | collective-permute-done | bytes 131104 | tf_op jit(solution)/shard_map/ppermute | solution.py:792
  43.6 0.7 %collective-permute-start.12 = (bf16[2,128,128]{2,1,0:T(8,128)(2,1)S(1)}, bf16[2,128,128]{2,1,0:T(8,128)(2,1)S(1)}, u32[]{:S(2)}, u32[]{:S(2)}) collective-permute-start(bf16[2,128,128]{2,1,0:T(8,128)(2,1)S(1)} %slice.15), channel_id=1, source_target_pairs={{8,24},{12,28},{9,25},{13,29},{10,26},{14,30},{11,27},{15,31}} | collective-permute-start | bytes 196616 | tf_op jit(solution)/shard_map/ppermute | solution.py:792
  44.3 1.5 %collective-permute-start.11 = (bf16[2,128,128]{2,1,0:T(8,128)(2,1)S(1)}, bf16[2,128,128]{2,1,0:T(8,128)(2,1)S(1)}, u32[]{:S(2)}, u32[]{:S(2)}) collective-permute-start(bf16[2,128,128]{2,1,0:T(8,128)(2,1)S(1)} %slice.15), channel_id=1, source_target_pairs={{8,16},{12,20},{9,17},{13,21},{10,18},{14,22},{11,19},{15,23}} | collective-permute-start | bytes 196616 | tf_op jit(solution)/shard_map/ppermute | solution.py:792
  45.8 1.4 %shard_map.89 = (f32[128,512]{1,0:T(8,128)S(1)}, f32[256,512]{1,0:T(8,128)S(1)}, f32[128,512]{1,0:T(8,128)S(1)}) custom-call(bf16[128,2048]{1,0:T(8,128)(2,1)S(1)} %copy-done, bf16[128,2048]{1,0:T(8,128)(2,1)S(1)} %collective-permute-done.refs_1_, bf16[128,2048]{1,0:T(8,128)(2,1)S(1)} %collective-permute-done.1.refs_2_, ...), custom_call_target="tpu_custom_call" | custom-call | flops 3000000000 | bytes 1048576 | tf_op jit(solution)/shard_map/pallas_call | solution.py:630
  47.2 5.0 %collective-permute-done.11.refs_0_ = bf16[2,128,128]{2,1,0:T(8,128)(2,1)S(1)} collective-permute-done((bf16[2,128,128]{2,1,0:T(8,128)(2,1)S(1)}, bf16[2,128,128]{2,1,0:T(8,128)(2,1)S(1)}, u32[]{:S(2)}, u32[]{:S(2)}) %collective-permute-start.11) | collective-permute-done | bytes 65568 | tf_op jit(solution)/shard_map/ppermute | solution.py:792
  52.3 2.1 %collective-permute-start.13 = (bf16[2,128,128]{2,1,0:T(8,128)(2,1)S(1)}, bf16[2,128,128]{2,1,0:T(8,128)(2,1)S(1)}, u32[]{:S(2)}, u32[]{:S(2)}) collective-permute-start(bf16[2,128,128]{2,1,0:T(8,128)(2,1)S(1)} %shard_map.88.mine_ref), channel_id=1, source_target_pairs={{0,4},{4,0},{8,12},{12,8},{16,20},{20,16},{24,28},{28,24},{1,5},{5... | collective-permute-start | bytes 196616 | tf_op jit(solution)/shard_map/ppermute | solution.py:806
  54.5 2.8 %shard_map.85 = (bf16[4,512,128]{2,1,0:T(8,128)(2,1)S(1)}, f32[4,512,128]{2,1,0:T(8,128)S(1)}) custom-call(bf16[4,4,128,256]{3,2,1,0:T(8,128)(2,1)S(1)} %get-tuple-element.26.both_ref, bf16[4,4,128,256]{3,2,1,0:T(8,128)(2,1)S(1)} %get-tuple-element.27.low_ref, bf16[12,384,128]{2,1,0:T(8,128)(2,1)S(1)} %get-tuple-element.22.act_e, ...), custom_call_target="tpu_custom_call" | custom-call | flops 2000000000 | bytes 1048576 | tf_op jit(solution)/shard_map/pallas_call | solution.py:630
  57.3 1.8 %shard_map.90 = bf16[512,512]{1,0:T(8,128)(2,1)} custom-call(bf16[4,512,128]{2,1,0:T(8,128)(2,1)S(1)} %get-tuple-element.31.qp_ref, f32[4,512,128]{2,1,0:T(8,128)S(1)} %get-tuple-element.32.o_ref, bf16[4,128,256]{2,1,0:T(8,128)(2,1)S(1)} %collective-permute-done.9.other_ref.pair_ref, bf16[2,128,128]{2,1,0:T(8,128)(2,1)S(1)} %shard_map.88.mine_ref, ...), custom_call_target="tpu_custom_call" | custom-call | flops 50000000 | bytes 1048576 | tf_op jit(solution)/shard_map/pallas_call | solution.py:630
  (36 shorter events, 0.8 us)
Async XLA Ops:
  0.0 13.0 %collective-permute-start.1 = (bf16[128,2048]{1,0:T(8,128)(2,1)}, bf16[128,2048]{1,0:T(8,128)(2,1)S(1)}, u32[]{:S(2)}, u32[]{:S(2)}) collective-permute-start(bf16[128,2048]{1,0:T(8,128)(2,1)} %refs_0_.3), channel_id=1, source_target_pairs={{0,2},{1,3},{2,0},{3,1},{4,6},{5,7},{6,4},{7,5},{8,10},{9,11},{10,... | collective-permute-start | bytes 1572872 | tf_op jit(solution)/shard_map/ppermute | solution.py:43
  1.2 13.1 %collective-permute-start = (bf16[128,2048]{1,0:T(8,128)(2,1)}, bf16[128,2048]{1,0:T(8,128)(2,1)S(1)}, u32[]{:S(2)}, u32[]{:S(2)}) collective-permute-start(bf16[128,2048]{1,0:T(8,128)(2,1)} %refs_0_.3), channel_id=1, source_target_pairs={{0,1},{1,0},{2,3},{3,2},{4,5},{5,4},{6,7},{7,6},{8,9},{9,8},{10,11... | collective-permute-start | bytes 1572872 | tf_op jit(solution)/shard_map/ppermute | solution.py:43
  2.5 18.8 %slice-start = ((s8[6291456]{0:T(1024)(128)(4,1)}), s8[4194304]{0:T(1024)(128)(4,1)S(1)}, s32[]{:S(2)}) async-start(s8[6291456]{0:T(1024)(128)(4,1)} %bitcast.7), calls=%async_computation | async-start | bytes 8388608
  3.4 17.9 %copy-start = (bf16[128,2048]{1,0:T(8,128)(2,1)S(1)}, bf16[128,2048]{1,0:T(8,128)(2,1)}, u32[]{:S(2)}) copy-start(bf16[128,2048]{1,0:T(8,128)(2,1)} %refs_0_.3) | copy-start | bytes 1572868
  3.4 17.9 %slice-start.1 = ((s8[6291456]{0:T(1024)(128)(4,1)}), s8[2097152]{0:T(1024)(128)(4,1)S(1)}, s32[]{:S(2)}) async-start(s8[6291456]{0:T(1024)(128)(4,1)} %bitcast.7), calls=%async_computation.1 | async-start | bytes 4194304
  3.4 17.9 %copy-start.3 = (bf16[2048,2,4]{0,2,1:T(4,128)(2,1)S(1)}, bf16[2048,2,4]{0,2,1:T(4,128)(2,1)}, u32[]{:S(2)}) copy-start(bf16[2048,2,4]{0,2,1:T(4,128)(2,1)} %param.11) | copy-start | bytes 98308
  3.4 17.9 %copy-start.4 = (bf16[4,3,512]{2,0,1:T(4,128)(2,1)S(1)}, bf16[4,3,512]{2,0,1:T(4,128)(2,1)}, u32[]{:S(2)}) copy-start(bf16[4,3,512]{2,0,1:T(4,128)(2,1)} %param.12) | copy-start | bytes 36868
  3.4 17.9 %copy-start.5 = (f32[4]{0:T(128)S(1)}, f32[4]{0:T(128)}, u32[]{:S(2)}) copy-start(f32[4]{0:T(128)} %param.13) | copy-start | bytes 52
  3.4 17.9 %copy-start.6 = (f32[4]{0:T(128)S(1)}, f32[4]{0:T(128)}, u32[]{:S(2)}) copy-start(f32[4]{0:T(128)} %param.14) | copy-start | bytes 52
  3.4 16.5 %collective-permute-start.6 = (bf16[8,2048]{1,0:T(8,128)(2,1)S(1)}, bf16[8,2048]{1,0:T(8,128)(2,1)S(1)}, u32[]{:S(2)}, u32[]{:S(2)}) collective-permute-start(bf16[8,2048]{1,0:T(8,128)(2,1)S(1)} %slice.12), channel_id=1, source_target_pairs={{3,7},{7,11},{11,15},{15,19},{19,23},{23,27},{27,31}} | collective-permute-start | bytes 98312 | tf_op jit(solution)/shard_map/ppermute | solution.py:69
  4.2 15.8 %collective-permute-start.5 = (bf16[8,2048]{1,0:T(8,128)(2,1)S(1)}, bf16[8,2048]{1,0:T(8,128)(2,1)S(1)}, u32[]{:S(2)}, u32[]{:S(2)}) collective-permute-start(bf16[8,2048]{1,0:T(8,128)(2,1)S(1)} %slice.12), channel_id=1, source_target_pairs={{3,6},{7,10},{11,14},{15,18},{19,22},{23,26},{27,30}} | collective-permute-start | bytes 98312 | tf_op jit(solution)/shard_map/ppermute | solution.py:69
  5.0 15.3 %collective-permute-start.4 = (bf16[8,2048]{1,0:T(8,128)(2,1)S(1)}, bf16[8,2048]{1,0:T(8,128)(2,1)S(1)}, u32[]{:S(2)}, u32[]{:S(2)}) collective-permute-start(bf16[8,2048]{1,0:T(8,128)(2,1)S(1)} %slice.12), channel_id=1, source_target_pairs={{3,5},{7,9},{11,13},{15,17},{19,21},{23,25},{27,29}} | collective-permute-start | bytes 98312 | tf_op jit(solution)/shard_map/ppermute | solution.py:69
  13.0 7.3 %collective-permute-start.3 = (bf16[8,2048]{1,0:T(8,128)(2,1)S(1)}, bf16[8,2048]{1,0:T(8,128)(2,1)S(1)}, u32[]{:S(2)}, u32[]{:S(2)}) collective-permute-start(bf16[8,2048]{1,0:T(8,128)(2,1)S(1)} %slice.12), channel_id=1, source_target_pairs={{3,4},{7,8},{11,12},{15,16},{19,20},{23,24},{27,28}} | collective-permute-start | bytes 98312 | tf_op jit(solution)/shard_map/ppermute | solution.py:69
  14.3 6.9 %collective-permute-start.2 = (bf16[8,2048]{1,0:T(8,128)(2,1)S(1)}, bf16[8,2048]{1,0:T(8,128)(2,1)S(1)}, u32[]{:S(2)}, u32[]{:S(2)}) collective-permute-start(bf16[8,2048]{1,0:T(8,128)(2,1)S(1)} %slice.12), channel_id=1, source_target_pairs={{0,3},{1,2},{2,1},{3,0},{4,7},{5,6},{6,5},{7,4},{8,11},{9,10},{10,... | collective-permute-start | bytes 98312 | tf_op jit(solution)/shard_map/ppermute | solution.py:71
  20.0 7.7 %collective-permute-start.7 = (bf16[64,2048]{1,0:T(8,128)(2,1)S(1)}, bf16[64,2048]{1,0:T(8,128)(2,1)S(1)}, u32[]{:S(2)}, u32[]{:S(2)}) collective-permute-start(bf16[64,2048]{1,0:T(8,128)(2,1)S(1)} %slice.16), channel_id=1, source_target_pairs={{0,1},{1,0},{2,3},{3,2},{4,5},{5,4},{6,7},{7,6},{8,9},{9,8},{10,11... | collective-permute-start | bytes 786440 | tf_op jit(solution)/shard_map/ppermute | solution.py:43
  20.0 7.6 %collective-permute-start.8 = (bf16[64,2048]{1,0:T(8,128)(2,1)S(1)}, bf16[64,2048]{1,0:T(8,128)(2,1)S(1)}, u32[]{:S(2)}, u32[]{:S(2)}) collective-permute-start(bf16[64,2048]{1,0:T(8,128)(2,1)S(1)} %slice.17), channel_id=1, source_target_pairs={{0,2},{1,3},{2,0},{3,1},{4,6},{5,7},{6,4},{7,5},{8,10},{9,11},{10,... | collective-permute-start | bytes 786440 | tf_op jit(solution)/shard_map/ppermute | solution.py:43
  27.6 18.2 %copy-start.2 = (bf16[2048,512]{1,0:T(8,128)(2,1)S(1)}, bf16[2048,512]{1,0:T(8,128)(2,1)}, u32[]{:S(2)}) copy-start(bf16[2048,512]{1,0:T(8,128)(2,1)} %refs_5_.1) | copy-start | bytes 6291460
  35.9 1.6 %collective-permute-start.9 = (bf16[4,128,256]{2,1,0:T(8,128)(2,1)S(1)}, bf16[4,128,256]{2,1,0:T(8,128)(2,1)S(1)}, u32[]{:S(2)}, u32[]{:S(2)}) collective-permute-start(bf16[4,128,256]{2,1,0:T(8,128)(2,1)S(1)} %get-tuple-element.33.mine_ref), channel_id=1, source_target_pairs={{0,4},{4,0},{8,12},{12,8},{16,20},{20,16},{24,28},{28,24},{1,5},{5... | collective-permute-start | bytes 786440 | tf_op jit(solution)/shard_map/ppermute | solution.py:775
  37.7 5.7 %collective-permute-start.10 = (bf16[2,128,256]{2,1,0:T(8,128)(2,1)S(1)}, bf16[2,128,256]{2,1,0:T(8,128)(2,1)S(1)}, u32[]{:S(2)}, u32[]{:S(2)}) collective-permute-start(bf16[2,128,256]{2,1,0:T(8,128)(2,1)S(1)} %shard_map.86.block_ref), channel_id=1, source_target_pairs={{0,8},{4,12},{16,24},{20,28},{1,9},{5,13},{17,25},{21,29},{2,10},{... | collective-permute-start | bytes 393224 | tf_op jit(solution)/shard_map/ppermute | solution.py:792
  43.6 3.6 %collective-permute-start.12 = (bf16[2,128,128]{2,1,0:T(8,128)(2,1)S(1)}, bf16[2,128,128]{2,1,0:T(8,128)(2,1)S(1)}, u32[]{:S(2)}, u32[]{:S(2)}) collective-permute-start(bf16[2,128,128]{2,1,0:T(8,128)(2,1)S(1)} %slice.15), channel_id=1, source_target_pairs={{8,24},{12,28},{9,25},{13,29},{10,26},{14,30},{11,27},{15,31}} | collective-permute-start | bytes 196616 | tf_op jit(solution)/shard_map/ppermute | solution.py:792
  44.3 7.9 %collective-permute-start.11 = (bf16[2,128,128]{2,1,0:T(8,128)(2,1)S(1)}, bf16[2,128,128]{2,1,0:T(8,128)(2,1)S(1)}, u32[]{:S(2)}, u32[]{:S(2)}) collective-permute-start(bf16[2,128,128]{2,1,0:T(8,128)(2,1)S(1)} %slice.15), channel_id=1, source_target_pairs={{8,16},{12,20},{9,17},{13,21},{10,18},{14,22},{11,19},{15,23}} | collective-permute-start | bytes 196616 | tf_op jit(solution)/shard_map/ppermute | solution.py:792
  52.3 4.9 %collective-permute-start.13 = (bf16[2,128,128]{2,1,0:T(8,128)(2,1)S(1)}, bf16[2,128,128]{2,1,0:T(8,128)(2,1)S(1)}, u32[]{:S(2)}, u32[]{:S(2)}) collective-permute-start(bf16[2,128,128]{2,1,0:T(8,128)(2,1)S(1)} %shard_map.88.mine_ref), channel_id=1, source_target_pairs={{0,4},{4,0},{8,12},{12,8},{16,20},{20,16},{24,28},{28,24},{1,5},{5... | collective-permute-start | bytes 196616 | tf_op jit(solution)/shard_map/ppermute | solution.py:806
  54.5 2.8 %copy-start.1 = (f32[128]{0:T(128)S(1)}, f32[128]{0:T(128)}, u32[]{:S(2)}) copy-start(f32[128]{0:T(128)} %param.15) | copy-start | bytes 1540
